TPU v7x, 32 devices: a whole 2x2x4 slice. The times are simulated.
32 devices in a mesh: frame: 8 (over z, x), head: 4 (over y, core).
Axes of the slice: x: 2, y: 2, z: 4, core: 2. Of those that a mesh axis runs over, the one named last changes fastest.
Arguments:
- queries: bfloat16 [4096, 1024], P('frame', 'head'), may hold values from -6 to 6
- keys: bfloat16 [4096, 1024], P('frame', 'head'), may hold values from -6 to 6
- values: bfloat16 [4096, 1024], P('frame', 'head'), may hold values from -6 to 6
- band_width: int32 [8, 8], replicated, may hold values from 1 to 4, as said below
- band_offset: int32 [8, 8, 4], replicated, may hold values from 0 to 3
- out_weight: bfloat16 [1024, 1536], P('head'), may hold values from -0.1875 to 0.1875
Outputs:
- projected: bfloat16 [4096, 1536], P(('frame', 'head'))
Inputs may be any that keep to these rules, and one draw needn't show every extreme that they name: `band_width`: for distances 0 and 1 the widths lie in (2, 4], for 2 and 3 in (1, 2], for 4 to 7 in [1, 1]; each of these upper ends is reached by some frame.
All inputs are finite; a program needn't handle non-finite values.
Results may differ from a plain program's by a relative error of at most 0.015.
Values may be sent and summed in bfloat16 or wider, within the bound.
No kernel may reach another device: no remote copies, remote signals or barrier semaphores. Data moves between devices by JAX's collectives and lax.ppermute only.
A program may use at most 64 MiB of HBM per device.

v0:
```python
import functools
import math

import jax
import jax.numpy as jnp
from jax import lax
from jax.experimental import pallas as pl
from jax.experimental.pallas import tpu as pltpu
from jax.sharding import PartitionSpec as P


HEAD = 128
BLK = 128
RADIUS = 7
MAX_WIDTH = (4, 4, 2, 2, 1, 1, 1, 1)
MASKED = -1e30
EXPONENT = math.log2(math.e) / math.sqrt(HEAD)

VMEM = pl.BlockSpec(memory_space=pltpu.VMEM)
SMEM = pl.BlockSpec(memory_space=pltpu.SMEM)
HBM = pl.BlockSpec(memory_space=pltpu.HBM)


def in_vmem(value):
    return pltpu.with_memory_space_constraint(value, pltpu.VMEM)


def in_hbm(value):
    return pltpu.with_memory_space_constraint(value, pltpu.HBM)


def params():
    return pltpu.CompilerParams(vmem_limit_bytes=32 << 20)


def split_kernel(group, q_ref, k_ref, v_ref, width_ref, offset_ref, *refs):
    outs, sem = refs[:-1], refs[-1]
    width = outs[0].shape[1] // 2
    place = lax.rem(lax.axis_index("frame"), group)
    copies = []
    for part in range(group):
        column = (place if part == 0 else 1 - place) * width
        columns = pl.ds(pl.multiple_of(column, HEAD), width)
        pair, rows = outs[2 * part], outs[2 * part + 1]
        for source, target in (
            (k_ref, pair.at[:, :width]),
            (v_ref, pair.at[:, width:]),
            (q_ref, rows),
        ):
            copies.append(
                pltpu.make_async_copy(source.at[:, columns], target, sem.at[len(copies)])
            )
    for source, target in ((width_ref, outs[-2]), (offset_ref, outs[-1])):
        copies.append(pltpu.make_async_copy(source, target, sem.at[len(copies)]))
    for copy in copies:
        copy.start()
    for copy in copies:
        copy.wait()


def split(queries, keys, values, bands, group):
    tokens, columns = queries.shape
    width = columns // group
    pair = pltpu.VMEM((tokens, 2 * width), queries.dtype)
    rows = pltpu.VMEM((tokens, width), queries.dtype)
    return pl.pallas_call(
        functools.partial(split_kernel, group),
        out_shape=[pair, rows] * group + [pltpu.SMEM(b.shape, b.dtype) for b in bands],
        in_specs=[HBM] * 5,
        out_specs=[VMEM] * (2 * group) + [SMEM] * 2,
        scratch_shapes=[pltpu.SemaphoreType.DMA((3 * group + 2,))],
        compiler_params=params(),
        name="split",
    )(*[in_hbm(v) for v in (queries, keys, values, *bands)])


def frame_of(unit, place, group, member):
    return unit * group + (place if member == 0 else group - 1 - place)


def update(rows, query, key_slots, value_slots, oks, m_ref, acc_ref, head, first):
    scores = lax.dot_general(
        query, key_slots, (((1,), (1,)), ((), ())), preferred_element_type=jnp.float32
    )
    pieces = [scores[:, BLK * j : BLK * (j + 1)] for j in range(len(oks))]
    pieces = [s if ok is None else jnp.where(ok, s, MASKED) for s, ok in zip(pieces, oks)]
    tallest = functools.reduce(jnp.maximum, pieces)
    tallest = jnp.max(tallest, axis=1, keepdims=True)
    if first:
        peak = jnp.broadcast_to(tallest, (BLK, BLK))
    else:
        before = m_ref[head, rows, :]
        peak = jnp.maximum(before, tallest)
    weights = [jnp.exp2((s - peak) * EXPONENT).astype(jnp.bfloat16) for s in pieces]
    weights = jnp.concatenate(weights, axis=1)
    added = jnp.dot(weights, value_slots, preferred_element_type=jnp.float32)
    if not first:
        rescale = jnp.exp2((before - peak) * EXPONENT)
        rescale = jnp.concatenate([rescale, rescale], axis=1)
        added = acc_ref[head, rows, :] * rescale + added
    acc_ref[head, rows, :] = added
    m_ref[head, rows, :] = peak


def attend_kernel(cfg, width_ref, offset_ref, *refs):
    group, heads, shifts, units, begins, ends = cfg
    q_refs, refs = refs[:group], refs[group:]
    chunks = [refs[group * i : group * (i + 1)] for i in range(len(shifts))]
    refs = refs[group * len(shifts) :]
    if not begins:
        refs = refs[2:]
    if ends:
        out_ref, m_ref, acc_ref = refs
    else:
        m_ref, acc_ref = refs
    tokens = q_refs[0].shape[0]
    blocks = tokens // BLK
    width = heads * HEAD
    me = lax.axis_index("frame")
    unit, place = me // group, lax.rem(me, group)
    ones = jnp.ones((BLK, HEAD), jnp.bfloat16)

    def pair_slots(b, qf, kf, far, refs):
        distance = jnp.abs(qf - kf)
        present = distance <= RADIUS
        reach = jnp.minimum(distance, RADIUS)
        span = width_ref[qf, reach]
        start = offset_ref[qf, b, reach]
        most = min(MAX_WIDTH[min(far, RADIUS)], blocks)
        found = []
        for j in range(most):
            if most == blocks:
                inside = lax.rem(j - start + blocks, blocks) < span
                if far == 0:
                    inside = inside | ((distance == 0) & (b == j))
                found.append((refs, j, present & inside))
            else:
                inside = None if most == 1 and far * 1 <= RADIUS - 2 * (group - 1) else present & (j < span)
                found.append((refs, lax.rem(start + j, blocks), inside))
        return found

    def gather(found, head, column):
        parts = []
        for ref, block, _ in found:
            if isinstance(block, int):
                at = pl.ds(block * BLK, BLK)
            else:
                at = pl.ds(pl.multiple_of(block * BLK, BLK), BLK)
            parts.append(ref[at, column + head * HEAD : column + (head + 1) * HEAD])
        return parts

    def steps(shift, chunk, begin):
        far = max(0, abs(shift) * group - (group - 1))
        other = unit + shift
        most = min(MAX_WIDTH[min(far, RADIUS)], blocks)
        for member in range(group):
            qf = frame_of(unit, place, group, member)
            order = [member] + [i for i in range(group) if i != member]
            batches = [[i] for i in order] if most == blocks else [order]
            for index, batch in enumerate(batches):
                for head in range(heads):
                    for b in range(blocks):
                        found = []
                        for i in batch:
                            kf = frame_of(other, place, group, i)
                            found += pair_slots(b, qf, kf, far, chunk[i])
                        key_slots = jnp.concatenate(gather(found, head, 0), axis=0)
                        value_slots = jnp.concatenate(
                            [
                                jnp.concatenate([v, ones], axis=1)
                                for v in gather(found, head, width)
                            ],
                            axis=0,
                        )
                        rows = slice(member * tokens + b * BLK, member * tokens + (b + 1) * BLK)
                        query = q_refs[member][
                            b * BLK : (b + 1) * BLK, head * HEAD : (head + 1) * HEAD
                        ]
                        oks = [ok for _, _, ok in found]
                        update(
                            rows, query, key_slots, value_slots, oks,
                            m_ref, acc_ref, head, begin and index == 0,
                        )

    for shift, chunk in zip(shifts, chunks):
        if shift == 0:
            steps(shift, chunk, begins)
        else:
            other = unit + shift

            @pl.when((other >= 0) & (other < units))
            def _(shift=shift, chunk=chunk):
                steps(shift, chunk, False)

    if ends:
        for member in range(group):
            start = (place if member == 0 else group - 1 - place) * tokens
            for head in range(heads):
                for b in range(blocks):
                    rows = slice(member * tokens + b * BLK, member * tokens + (b + 1) * BLK)
                    both = acc_ref[head, rows, :]
                    at = pl.ds(pl.multiple_of(start + b * BLK, BLK), BLK)
                    out_ref[at, head * HEAD : (head + 1) * HEAD] = (
                        both[:, :HEAD] / both[:, HEAD:]
                    ).astype(out_ref.dtype)


def attend(cfg, bands, queries, chunks, state):
    group, heads, _, _, begins, ends = cfg
    tokens = queries[0].shape[0]
    rows = group * tokens
    m_shape = pltpu.VMEM((heads, rows, BLK), jnp.float32)
    acc_shape = pltpu.VMEM((heads, rows, 2 * HEAD), jnp.float32)
    flat = [in_vmem(c) for pair in chunks for c in pair]
    inputs = [*bands, *[in_vmem(q) for q in queries], *flat, *state]
    outs = [m_shape, acc_shape]
    aliases = {}
    if not begins:
        aliases = {len(inputs) - 2: 0, len(inputs) - 1: 1}
    if ends:
        outs = [jax.ShapeDtypeStruct((rows, heads * HEAD), queries[0].dtype), m_shape, acc_shape]
        aliases = {index: out + 1 for index, out in aliases.items()}
    work = 4 * len(flat) * tokens * rows * heads * HEAD
    return pl.pallas_call(
        functools.partial(attend_kernel, cfg),
        out_shape=outs,
        in_specs=[SMEM] * 2 + [VMEM] * (len(inputs) - 2),
        out_specs=[VMEM] * len(outs),
        input_output_aliases=aliases,
        compiler_params=params(),
        cost_estimate=pl.CostEstimate(flops=work, bytes_accessed=1 << 20, transcendentals=0),
    )(*inputs)


def project_kernel(group, ranks, rows_ref, *refs):
    weights, out_ref = refs[:-1], refs[-1]
    me = lax.axis_index("head")
    total = None
    for offset, weight in enumerate(weights):
        owner = me ^ offset
        left = jnp.concatenate([rows_ref[i * ranks + owner] for i in range(group)], axis=1)
        term = jnp.dot(left, weight[...], preferred_element_type=jnp.float32)
        total = term if total is None else total + term
    out_ref[...] = total.astype(out_ref.dtype)


def project(rows, weights, group):
    ranks = len(weights)
    tokens, columns = rows.shape[1], weights[0].shape[1]
    return pl.pallas_call(
        functools.partial(project_kernel, group, ranks),
        out_shape=jax.ShapeDtypeStruct((tokens, columns), rows.dtype),
        in_specs=[VMEM] * (1 + ranks),
        out_specs=VMEM,
        compiler_params=params(),
        cost_estimate=pl.CostEstimate(
            flops=2 * rows.size * columns, bytes_accessed=1 << 20, transcendentals=0
        ),
        name="project",
    )(in_vmem(rows), *[in_vmem(w) for w in weights])


def plan(shape, columns):
    frames, local_heads = shape["frame"], columns // HEAD
    group = 2 if local_heads % 2 == 0 and frames % 2 == 0 else 1
    units = frames // group
    return group, units, min(units - 1, (RADIUS + group - 1) // group)


def on_device(queries, keys, values, band_width, band_offset, out_weight):
    frames, ranks = lax.axis_size("frame"), lax.axis_size("head")
    tokens = queries.shape[0]
    group, units, furthest = plan({"frame": frames}, queries.shape[1])
    heads = queries.shape[1] // HEAD // group

    def along(value, steps):
        pairs = [(a * group + i, b * group + i) for a, b in steps for i in range(group)]
        return lax.ppermute(value, "frame", pairs)

    bands = (band_width, jnp.transpose(band_offset, (0, 2, 1)))
    *pieces, band_width, band_offset = split(queries, keys, values, bands, group)
    bands = (band_width, band_offset)
    chunks, query_rows = [pieces[0]], [pieces[1]]
    if group == 2:
        swap = [(f, f ^ 1) for f in range(frames)]
        chunks.append(lax.ppermute(pieces[2], "frame", swap))
        query_rows.append(lax.ppermute(pieces[3], "frame", swap))

    weights = {0: out_weight}
    bit = ranks // 2
    while bit:
        for offset in list(weights):
            pairs = [(h, h ^ bit) for h in range(ranks)]
            weights[offset ^ bit] = lax.ppermute(weights[offset], "head", pairs)
        bit //= 2
    weights = [weights[o] for o in range(ranks)]

    lower, upper = chunks, chunks
    arrived = []
    for k in range(1, furthest + 1):
        up = [(s, s + 1) for s in range(k - 1, units - 1)]
        down = [(s, s - 1) for s in range(1, units - k + 1)]
        lower = [along(c, up) for c in lower]
        upper = [along(c, down) for c in upper]
        arrived.append((lower, upper))

    cfg = (group, heads, (0,), units, True, False)
    state = attend(cfg, bands, query_rows, [chunks], [])
    for k, (lower, upper) in enumerate(arrived, 1):
        cfg = (group, heads, (-k, k), units, False, k == furthest)
        state = attend(cfg, bands, query_rows, [lower, upper], state)
    attended = state[0]

    members = [
        [(u * group + i) * ranks + h for i in range(group) for h in range(ranks)]
        for u in range(units)
    ]
    blocks = attended.reshape(group * ranks, tokens // ranks, heads * HEAD)
    rows = lax.all_to_all(
        blocks, ("frame", "head"), split_axis=0, concat_axis=0, tiled=True,
        axis_index_groups=members,
    )
    return project(rows, weights, group)


def solution(mesh):
    placed = (P("frame", "head"), P("frame", "head"), P("frame", "head"), P(), P(), P("head", None))
    return jax.shard_map(
        on_device, mesh=mesh, in_specs=placed, out_specs=P(("frame", "head"), None), check_vma=False
    )
```

profile of v0, /device:TPU:0, one launch (start us, length us, event | category | flops | bytes accessed | tf_op | source)
XLA Modules:
  0.0 58.3 jit_solution(13661619717368837766)
XLA Ops:
  0.0 0.0 copy-start
  0.0 3.0 %collective-permute-start.15 = (bf16[256,1536]{1,0:T(8,128)(2,1)}, bf16[256,1536]{1,0:T(8,128)(2,1)S(1)}, u32[]{:S(2)}, u32[]{:S(2)}) collective-permute-start(bf16[256,1536]{1,0:T(8,128)(2,1)} %refs_0_.1), channel_id=1, source_target_pairs={{0,2},{1,3},{2,0},{3,1},{4,6},{5,7},{6,4},{7,5},{8,10},{9,11},{10,... | collective-permute-start | bytes 2359304 | tf_op jit(solution)/shard_map/ppermute | solution.py:294
  3.0 1.3 %split.1 = (bf16[512,256]{1,0:T(8,128)(2,1)S(1)}, bf16[512,128]{1,0:T(8,128)(2,1)S(1)}, bf16[512,256]{1,0:T(8,128)(2,1)S(1)}, bf16[512,128]{1,0:T(8,128)(2,1)S(1...) custom-call(bf16[512,256]{1,0:T(8,128)(2,1)} %q_ref.1, bf16[512,256]{1,0:T(8,128)(2,1)} %k_ref.1, bf16[512,256]{1,0:T(8,128)(2,1)} %v_ref.1, ...), custom_call_target="tpu_custom_call" | custom-call | tf_op jit(solution)/shard_map/split/pallas_call | solution.py:66
  4.3 1.6 %collective-permute-start.4 = (bf16[512,256]{1,0:T(8,128)(2,1)S(1)}, bf16[512,256]{1,0:T(8,128)(2,1)S(1)}, u32[]{:S(2)}, u32[]{:S(2)}) collective-permute-start(bf16[512,256]{1,0:T(8,128)(2,1)S(1)} %get-tuple-element.23), channel_id=1, source_target_pairs={{0,4},{4,0},{8,12},{12,8},{16,20},{20,16},{24,28},{28,24},{1,5},{5... | collective-permute-start | bytes 786440 | tf_op jit(solution)/shard_map/ppermute | solution.py:286
  5.8 1.3 %collective-permute-start.8 = (bf16[512,256]{1,0:T(8,128)(2,1)S(1)}, bf16[512,256]{1,0:T(8,128)(2,1)S(1)}, u32[]{:S(2)}, u32[]{:S(2)}) collective-permute-start(bf16[512,256]{1,0:T(8,128)(2,1)S(1)} %get-tuple-element.22.refs_2_), channel_id=1, source_target_pairs={{8,0},{12,4},{16,8},{20,12},{24,16},{28,20},{9,1},{13,5},{17,9},{2... | collective-permute-start | bytes 786440 | tf_op jit(solution)/shard_map/ppermute | solution.py:278
  7.1 4.6 %collective-permute-start.1 = (bf16[512,256]{1,0:T(8,128)(2,1)S(1)}, bf16[512,256]{1,0:T(8,128)(2,1)S(1)}, u32[]{:S(2)}, u32[]{:S(2)}) collective-permute-start(bf16[512,256]{1,0:T(8,128)(2,1)S(1)} %get-tuple-element.22.refs_2_), channel_id=1, source_target_pairs={{0,8},{4,12},{8,16},{12,20},{16,24},{20,28},{1,9},{5,13},{9,17},{1... | collective-permute-start | bytes 786440 | tf_op jit(solution)/shard_map/ppermute | solution.py:278
  11.7 0.6 %collective-permute-start = (bf16[512,128]{1,0:T(8,128)(2,1)S(1)}, bf16[512,128]{1,0:T(8,128)(2,1)S(1)}, u32[]{:S(2)}, u32[]{:S(2)}) collective-permute-start(bf16[512,128]{1,0:T(8,128)(2,1)S(1)} %get-tuple-element.21), channel_id=1, source_target_pairs={{0,4},{4,0},{8,12},{12,8},{16,20},{20,16},{24,28},{28,24},{1,5},{5... | collective-permute-start | bytes 393224 | tf_op jit(solution)/shard_map/ppermute | solution.py:287
  12.3 0.0 collective-permute-done.4.refs_3_
  12.3 1.3 %collective-permute-start.11 = (bf16[512,256]{1,0:T(8,128)(2,1)S(1)}, bf16[512,256]{1,0:T(8,128)(2,1)S(1)}, u32[]{:S(2)}, u32[]{:S(2)}) collective-permute-start(bf16[512,256]{1,0:T(8,128)(2,1)S(1)} %collective-permute-done.4.refs_3_), channel_id=1, source_target_pairs={{8,0},{12,4},{16,8},{20,12},{24,16},{28,20},{9,1},{13,5},{17,9},{2... | collective-permute-start | bytes 786440 | tf_op jit(solution)/shard_map/ppermute | solution.py:278
  13.6 3.1 %collective-permute-done.refs_1_ = bf16[512,128]{1,0:T(8,128)(2,1)S(1)} collective-permute-done((bf16[512,128]{1,0:T(8,128)(2,1)S(1)}, bf16[512,128]{1,0:T(8,128)(2,1)S(1)}, u32[]{:S(2)}, u32[]{:S(2)}) %collective-permute-start) | collective-permute-done | bytes 131104 | tf_op jit(solution)/shard_map/ppermute | solution.py:287
  16.7 3.5 %collective-permute-start.5 = (bf16[512,256]{1,0:T(8,128)(2,1)S(1)}, bf16[512,256]{1,0:T(8,128)(2,1)S(1)}, u32[]{:S(2)}, u32[]{:S(2)}) collective-permute-start(bf16[512,256]{1,0:T(8,128)(2,1)S(1)} %collective-permute-done.4.refs_3_), channel_id=1, source_target_pairs={{0,8},{4,12},{8,16},{12,20},{16,24},{20,28},{1,9},{5,13},{9,17},{1... | collective-permute-start | bytes 786440 | tf_op jit(solution)/shard_map/ppermute | solution.py:278
  20.2 0.0 collective-permute-done.8.refs_4_
  20.2 1.3 %collective-permute-start.9 = (bf16[512,256]{1,0:T(8,128)(2,1)S(1)}, bf16[512,256]{1,0:T(8,128)(2,1)S(1)}, u32[]{:S(2)}, u32[]{:S(2)}) collective-permute-start(bf16[512,256]{1,0:T(8,128)(2,1)S(1)} %collective-permute-done.8.refs_4_), channel_id=1, source_target_pairs={{8,0},{12,4},{16,8},{20,12},{9,1},{13,5},{17,9},{21,13},{10,2},{14... | collective-permute-start | bytes 786440 | tf_op jit(solution)/shard_map/ppermute | solution.py:278
  21.5 0.0 collective-permute-done.1.refs_2_
  21.5 0.7 %collective-permute-start.2 = (bf16[512,256]{1,0:T(8,128)(2,1)S(1)}, bf16[512,256]{1,0:T(8,128)(2,1)S(1)}, u32[]{:S(2)}, u32[]{:S(2)}) collective-permute-start(bf16[512,256]{1,0:T(8,128)(2,1)S(1)} %collective-permute-done.1.refs_2_), channel_id=1, source_target_pairs={{8,16},{12,20},{16,24},{20,28},{9,17},{13,21},{17,25},{21,29},{10,... | collective-permute-start | bytes 786440 | tf_op jit(solution)/shard_map/ppermute | solution.py:278
  22.2 0.0 collective-permute-done.11.refs_5_
  22.2 1.3 %collective-permute-start.12 = (bf16[512,256]{1,0:T(8,128)(2,1)S(1)}, bf16[512,256]{1,0:T(8,128)(2,1)S(1)}, u32[]{:S(2)}, u32[]{:S(2)}) collective-permute-start(bf16[512,256]{1,0:T(8,128)(2,1)S(1)} %collective-permute-done.11.refs_5_), channel_id=1, source_target_pairs={{8,0},{12,4},{16,8},{20,12},{9,1},{13,5},{17,9},{21,13},{10,2},{14... | collective-permute-start | bytes 786440 | tf_op jit(solution)/shard_map/ppermute | solution.py:278
  23.5 0.5 collective-permute-done.5.refs_3_
  24.1 0.7 %collective-permute-start.6 = (bf16[512,256]{1,0:T(8,128)(2,1)S(1)}, bf16[512,256]{1,0:T(8,128)(2,1)S(1)}, u32[]{:S(2)}, u32[]{:S(2)}) collective-permute-start(bf16[512,256]{1,0:T(8,128)(2,1)S(1)} %collective-permute-done.5.refs_3_), channel_id=1, source_target_pairs={{8,16},{12,20},{16,24},{20,28},{9,17},{13,21},{17,25},{21,29},{10,... | collective-permute-start | bytes 786440 | tf_op jit(solution)/shard_map/ppermute | solution.py:278
  24.8 4.8 %collective-permute-done.9.refs_4_ = bf16[512,256]{1,0:T(8,128)(2,1)S(1)} collective-permute-done((bf16[512,256]{1,0:T(8,128)(2,1)S(1)}, bf16[512,256]{1,0:T(8,128)(2,1)S(1)}, u32[]{:S(2)}, u32[]{:S(2)}) %collective-permute-start.9) | collective-permute-done | bytes 262176 | tf_op jit(solution)/shard_map/ppermute | solution.py:278
  29.5 1.3 %collective-permute-start.10 = (bf16[512,256]{1,0:T(8,128)(2,1)S(1)}, bf16[512,256]{1,0:T(8,128)(2,1)S(1)}, u32[]{:S(2)}, u32[]{:S(2)}) collective-permute-start(bf16[512,256]{1,0:T(8,128)(2,1)S(1)} %collective-permute-done.9.refs_4_), channel_id=1, source_target_pairs={{8,0},{12,4},{9,1},{13,5},{10,2},{14,6},{11,3},{15,7}} | collective-permute-start | bytes 786440 | tf_op jit(solution)/shard_map/ppermute | solution.py:278
  30.8 0.0 collective-permute-done.2.refs_2_
  30.8 0.0 copy-done
  30.8 0.1 collective-permute-start.14
  30.9 0.0 collective-permute-done.15.refs_2_
  30.9 0.5 collective-permute-start.16
  31.4 4.6 %collective-permute-done.12.refs_5_ = bf16[512,256]{1,0:T(8,128)(2,1)S(1)} collective-permute-done((bf16[512,256]{1,0:T(8,128)(2,1)S(1)}, bf16[512,256]{1,0:T(8,128)(2,1)S(1)}, u32[]{:S(2)}, u32[]{:S(2)}) %collective-permute-start.12) | collective-permute-done | bytes 262176 | tf_op jit(solution)/shard_map/ppermute | solution.py:278
  36.0 0.7 %collective-permute-start.3 = (bf16[512,256]{1,0:T(8,128)(2,1)S(1)}, bf16[512,256]{1,0:T(8,128)(2,1)S(1)}, u32[]{:S(2)}, u32[]{:S(2)}) collective-permute-start(bf16[512,256]{1,0:T(8,128)(2,1)S(1)} %collective-permute-done.2.refs_2_), channel_id=1, source_target_pairs={{16,24},{20,28},{17,25},{21,29},{18,26},{22,30},{19,27},{23,31}} | collective-permute-start | bytes 786440 | tf_op jit(solution)/shard_map/ppermute | solution.py:278
  36.7 0.0 collective-permute-done.6.refs_3_
  36.7 1.3 %collective-permute-start.13 = (bf16[512,256]{1,0:T(8,128)(2,1)S(1)}, bf16[512,256]{1,0:T(8,128)(2,1)S(1)}, u32[]{:S(2)}, u32[]{:S(2)}) collective-permute-start(bf16[512,256]{1,0:T(8,128)(2,1)S(1)} %collective-permute-done.12.refs_5_), channel_id=1, source_target_pairs={{8,0},{12,4},{9,1},{13,5},{10,2},{14,6},{11,3},{15,7}} | collective-permute-start | bytes 786440 | tf_op jit(solution)/shard_map/ppermute | solution.py:278
  38.0 3.0 %collective-permute-done.10.refs_4_ = bf16[512,256]{1,0:T(8,128)(2,1)S(1)} collective-permute-done((bf16[512,256]{1,0:T(8,128)(2,1)S(1)}, bf16[512,256]{1,0:T(8,128)(2,1)S(1)}, u32[]{:S(2)}, u32[]{:S(2)}) %collective-permute-start.10) | collective-permute-done | bytes 262176 | tf_op jit(solution)/shard_map/ppermute | solution.py:278
  41.0 0.7 %collective-permute-start.7 = (bf16[512,256]{1,0:T(8,128)(2,1)S(1)}, bf16[512,256]{1,0:T(8,128)(2,1)S(1)}, u32[]{:S(2)}, u32[]{:S(2)}) collective-permute-start(bf16[512,256]{1,0:T(8,128)(2,1)S(1)} %collective-permute-done.6.refs_3_), channel_id=1, source_target_pairs={{16,24},{20,28},{17,25},{21,29},{18,26},{22,30},{19,27},{23,31}} | collective-permute-start | bytes 786440 | tf_op jit(solution)/shard_map/ppermute | solution.py:278
  41.7 1.5 %shard_map.64 = (f32[1,1024,128]{2,1,0:T(8,128)S(1)}, f32[1,1024,256]{2,1,0:T(8,128)S(1)}) custom-call(s32[8,8]{1,0:T(8,128)S(4)} %get-tuple-element.18.width_ref, s32[8,4,8]{2,1,0:T(4,128)S(4)} %get-tuple-element.19.offset_ref, bf16[512,128]{1,0:T(8,128)(2,1)S(1)} %get-tuple-element.20.refs_0_, bf16[512,128]{1,0:T(8,128)(2,1)S(1)} %collective-permute-done.refs_1_, ...), custom_call_target="tpu_custom_call" | custom-call | flops 536870912 | bytes 1048576 | tf_op jit(solution)/shard_map/pallas_call | solution.py:224
  43.3 1.7 %shard_map.65 = (f32[1,1024,128]{2,1,0:T(8,128)S(1)}, f32[1,1024,256]{2,1,0:T(8,128)S(1)}) custom-call(s32[8,8]{1,0:T(8,128)S(4)} %get-tuple-element.18.width_ref, s32[8,4,8]{2,1,0:T(4,128)S(4)} %get-tuple-element.19.offset_ref, bf16[512,128]{1,0:T(8,128)(2,1)S(1)} %get-tuple-element.20.refs_0_, ...), custom_call_target="tpu_custom_call", output_to_operand_aliasing={{0}: (8, {}), {1}: (9, {})} | custom-call | flops 1073741824 | bytes 1048576 | tf_op jit(solution)/shard_map/pallas_call | solution.py:224
  44.9 1.0 %shard_map.66 = (f32[1,1024,128]{2,1,0:T(8,128)S(1)}, f32[1,1024,256]{2,1,0:T(8,128)S(1)}) custom-call(s32[8,8]{1,0:T(8,128)S(4)} %get-tuple-element.18.width_ref, s32[8,4,8]{2,1,0:T(4,128)S(4)} %get-tuple-element.19.offset_ref, bf16[512,128]{1,0:T(8,128)(2,1)S(1)} %get-tuple-element.20.refs_0_, ...), custom_call_target="tpu_custom_call", output_to_operand_aliasing={{0}: (8, {}), {1}: (9, {})} | custom-call | flops 1073741824 | bytes 1048576 | tf_op jit(solution)/shard_map/pallas_call | solution.py:224
  46.0 0.0 collective-permute-done.3.refs_2_
  46.0 0.0 collective-permute-done.13.refs_5_
  46.0 0.0 collective-permute-done.7.refs_3_
  46.0 0.8 %shard_map.67 = (bf16[1024,128]{1,0:T(8,128)(2,1)S(1)}, f32[1,1024,128]{2,1,0:T(8,128)S(1)}, f32[1,1024,256]{2,1,0:T(8,128)S(1)}) custom-call(s32[8,8]{1,0:T(8,128)S(4)} %get-tuple-element.18.width_ref, s32[8,4,8]{2,1,0:T(4,128)S(4)} %get-tuple-element.19.offset_ref, ...), custom_call_target="tpu_custom_call", output_to_operand_aliasing={{1}: (8, {}), {2}: (9, {})} | custom-call | flops 1073741824 | bytes 1048576 | tf_op jit(solution)/shard_map/pallas_call | solution.py:224
  46.8 0.0 copy-start.1
  46.8 0.7 %copy-done.1 = bf16[1024,128]{1,0:T(8,128)(2,1)} copy-done((bf16[1024,128]{1,0:T(8,128)(2,1)}, bf16[1024,128]{1,0:T(8,128)(2,1)S(1)}, u32[]{:S(2)}) %copy-start.1) | copy-done | bytes 262168
  47.5 3.4 %all-to-all-start = ((bf16[8,128,128]{2,1,0:T(8,128)(2,1)}), bf16[8,128,128]{2,1,0:T(8,128)(2,1)S(1)}, u32[]{:S(2)}, u32[]{:S(2)}) async-start(bf16[8,128,128]{2,1,0:T(8,128)(2,1)} %bitcast.2), calls=%async_computation | async-start | bytes 524288 | tf_op jit(solution)/shard_map/all_to_all | solution.py:319
  50.9 0.0 collective-permute-done.14.refs_1_
  50.9 6.0 %all-to-all-done.rows_ref = bf16[8,128,128]{2,1,0:T(8,128)(2,1)S(1)} async-done(((bf16[8,128,128]{2,1,0:T(8,128)(2,1)}), bf16[8,128,128]{2,1,0:T(8,128)(2,1)S(1)}, u32[]{:S(2)}, u32[]{:S(2)}) %all-to-all-start) | async-done | bytes 262176 | tf_op jit(solution)/shard_map/all_to_all | solution.py:319
  56.9 0.0 collective-permute-done.16.refs_3_
  56.9 1.3 %project.1 = bf16[128,1536]{1,0:T(8,128)(2,1)} custom-call(bf16[8,128,128]{2,1,0:T(8,128)(2,1)S(1)} %all-to-all-done.rows_ref, bf16[256,1536]{1,0:T(8,128)(2,1)S(1)} %copy-done, bf16[256,1536]{1,0:T(8,128)(2,1)S(1)} %collective-permute-done.14.refs_1_, bf16[256,1536]{1,0:T(8,128)(2,1)S(1)} %collective-permute-done.15.refs_2_, ...), custom_call_target="tpu_custom_call" | custom-call | flops 402653184 | bytes 1048576 | tf_op jit(solution)/shard_map/project/pallas_call | solution.py:250
Async XLA Ops:
  0.0 30.8 %copy-start = (bf16[256,1536]{1,0:T(8,128)(2,1)S(1)}, bf16[256,1536]{1,0:T(8,128)(2,1)}, u32[]{:S(2)}) copy-start(bf16[256,1536]{1,0:T(8,128)(2,1)} %refs_0_.1) | copy-start | bytes 2359300
  0.0 30.9 %collective-permute-start.15 = (bf16[256,1536]{1,0:T(8,128)(2,1)}, bf16[256,1536]{1,0:T(8,128)(2,1)S(1)}, u32[]{:S(2)}, u32[]{:S(2)}) collective-permute-start(bf16[256,1536]{1,0:T(8,128)(2,1)} %refs_0_.1), channel_id=1, source_target_pairs={{0,2},{1,3},{2,0},{3,1},{4,6},{5,7},{6,4},{7,5},{8,10},{9,11},{10,... | collective-permute-start | bytes 2359304 | tf_op jit(solution)/shard_map/ppermute | solution.py:294
  4.3 8.0 %collective-permute-start.4 = (bf16[512,256]{1,0:T(8,128)(2,1)S(1)}, bf16[512,256]{1,0:T(8,128)(2,1)S(1)}, u32[]{:S(2)}, u32[]{:S(2)}) collective-permute-start(bf16[512,256]{1,0:T(8,128)(2,1)S(1)} %get-tuple-element.23), channel_id=1, source_target_pairs={{0,4},{4,0},{8,12},{12,8},{16,20},{20,16},{24,28},{28,24},{1,5},{5... | collective-permute-start | bytes 786440 | tf_op jit(solution)/shard_map/ppermute | solution.py:286
  5.8 14.4 %collective-permute-start.8 = (bf16[512,256]{1,0:T(8,128)(2,1)S(1)}, bf16[512,256]{1,0:T(8,128)(2,1)S(1)}, u32[]{:S(2)}, u32[]{:S(2)}) collective-permute-start(bf16[512,256]{1,0:T(8,128)(2,1)S(1)} %get-tuple-element.22.refs_2_), channel_id=1, source_target_pairs={{8,0},{12,4},{16,8},{20,12},{24,16},{28,20},{9,1},{13,5},{17,9},{2... | collective-permute-start | bytes 786440 | tf_op jit(solution)/shard_map/ppermute | solution.py:278
  7.1 14.4 %collective-permute-start.1 = (bf16[512,256]{1,0:T(8,128)(2,1)S(1)}, bf16[512,256]{1,0:T(8,128)(2,1)S(1)}, u32[]{:S(2)}, u32[]{:S(2)}) collective-permute-start(bf16[512,256]{1,0:T(8,128)(2,1)S(1)} %get-tuple-element.22.refs_2_), channel_id=1, source_target_pairs={{0,8},{4,12},{8,16},{12,20},{16,24},{20,28},{1,9},{5,13},{9,17},{1... | collective-permute-start | bytes 786440 | tf_op jit(solution)/shard_map/ppermute | solution.py:278
  11.7 5.0 %collective-permute-start = (bf16[512,128]{1,0:T(8,128)(2,1)S(1)}, bf16[512,128]{1,0:T(8,128)(2,1)S(1)}, u32[]{:S(2)}, u32[]{:S(2)}) collective-permute-start(bf16[512,128]{1,0:T(8,128)(2,1)S(1)} %get-tuple-element.21), channel_id=1, source_target_pairs={{0,4},{4,0},{8,12},{12,8},{16,20},{20,16},{24,28},{28,24},{1,5},{5... | collective-permute-start | bytes 393224 | tf_op jit(solution)/shard_map/ppermute | solution.py:287
  12.3 9.9 %collective-permute-start.11 = (bf16[512,256]{1,0:T(8,128)(2,1)S(1)}, bf16[512,256]{1,0:T(8,128)(2,1)S(1)}, u32[]{:S(2)}, u32[]{:S(2)}) collective-permute-start(bf16[512,256]{1,0:T(8,128)(2,1)S(1)} %collective-permute-done.4.refs_3_), channel_id=1, source_target_pairs={{8,0},{12,4},{16,8},{20,12},{24,16},{28,20},{9,1},{13,5},{17,9},{2... | collective-permute-start | bytes 786440 | tf_op jit(solution)/shard_map/ppermute | solution.py:278
  16.7 7.3 %collective-permute-start.5 = (bf16[512,256]{1,0:T(8,128)(2,1)S(1)}, bf16[512,256]{1,0:T(8,128)(2,1)S(1)}, u32[]{:S(2)}, u32[]{:S(2)}) collective-permute-start(bf16[512,256]{1,0:T(8,128)(2,1)S(1)} %collective-permute-done.4.refs_3_), channel_id=1, source_target_pairs={{0,8},{4,12},{8,16},{12,20},{16,24},{20,28},{1,9},{5,13},{9,17},{1... | collective-permute-start | bytes 786440 | tf_op jit(solution)/shard_map/ppermute | solution.py:278
  20.2 9.3 %collective-permute-start.9 = (bf16[512,256]{1,0:T(8,128)(2,1)S(1)}, bf16[512,256]{1,0:T(8,128)(2,1)S(1)}, u32[]{:S(2)}, u32[]{:S(2)}) collective-permute-start(bf16[512,256]{1,0:T(8,128)(2,1)S(1)} %collective-permute-done.8.refs_4_), channel_id=1, source_target_pairs={{8,0},{12,4},{16,8},{20,12},{9,1},{13,5},{17,9},{21,13},{10,2},{14... | collective-permute-start | bytes 786440 | tf_op jit(solution)/shard_map/ppermute | solution.py:278
  21.5 9.3 %collective-permute-start.2 = (bf16[512,256]{1,0:T(8,128)(2,1)S(1)}, bf16[512,256]{1,0:T(8,128)(2,1)S(1)}, u32[]{:S(2)}, u32[]{:S(2)}) collective-permute-start(bf16[512,256]{1,0:T(8,128)(2,1)S(1)} %collective-permute-done.1.refs_2_), channel_id=1, source_target_pairs={{8,16},{12,20},{16,24},{20,28},{9,17},{13,21},{17,25},{21,29},{10,... | collective-permute-start | bytes 786440 | tf_op jit(solution)/shard_map/ppermute | solution.py:278
  22.2 13.8 %collective-permute-start.12 = (bf16[512,256]{1,0:T(8,128)(2,1)S(1)}, bf16[512,256]{1,0:T(8,128)(2,1)S(1)}, u32[]{:S(2)}, u32[]{:S(2)}) collective-permute-start(bf16[512,256]{1,0:T(8,128)(2,1)S(1)} %collective-permute-done.11.refs_5_), channel_id=1, source_target_pairs={{8,0},{12,4},{16,8},{20,12},{9,1},{13,5},{17,9},{21,13},{10,2},{14... | collective-permute-start | bytes 786440 | tf_op jit(solution)/shard_map/ppermute | solution.py:278
  24.1 12.6 %collective-permute-start.6 = (bf16[512,256]{1,0:T(8,128)(2,1)S(1)}, bf16[512,256]{1,0:T(8,128)(2,1)S(1)}, u32[]{:S(2)}, u32[]{:S(2)}) collective-permute-start(bf16[512,256]{1,0:T(8,128)(2,1)S(1)} %collective-permute-done.5.refs_3_), channel_id=1, source_target_pairs={{8,16},{12,20},{16,24},{20,28},{9,17},{13,21},{17,25},{21,29},{10,... | collective-permute-start | bytes 786440 | tf_op jit(solution)/shard_map/ppermute | solution.py:278
  29.5 11.5 %collective-permute-start.10 = (bf16[512,256]{1,0:T(8,128)(2,1)S(1)}, bf16[512,256]{1,0:T(8,128)(2,1)S(1)}, u32[]{:S(2)}, u32[]{:S(2)}) collective-permute-start(bf16[512,256]{1,0:T(8,128)(2,1)S(1)} %collective-permute-done.9.refs_4_), channel_id=1, source_target_pairs={{8,0},{12,4},{9,1},{13,5},{10,2},{14,6},{11,3},{15,7}} | collective-permute-start | bytes 786440 | tf_op jit(solution)/shard_map/ppermute | solution.py:278
  30.8 20.1 %collective-permute-start.14 = (bf16[256,1536]{1,0:T(8,128)(2,1)S(1)}, bf16[256,1536]{1,0:T(8,128)(2,1)S(1)}, u32[]{:S(2)}, u32[]{:S(2)}) collective-permute-start(bf16[256,1536]{1,0:T(8,128)(2,1)S(1)} %copy-done), channel_id=1, source_target_pairs={{0,1},{1,0},{2,3},{3,2},{4,5},{5,4},{6,7},{7,6},{8,9},{9,8},{10,11... | collective-permute-start | bytes 2359304 | tf_op jit(solution)/shard_map/ppermute | solution.py:294
  30.9 26.0 %collective-permute-start.16 = (bf16[256,1536]{1,0:T(8,128)(2,1)S(1)}, bf16[256,1536]{1,0:T(8,128)(2,1)S(1)}, u32[]{:S(2)}, u32[]{:S(2)}) collective-permute-start(bf16[256,1536]{1,0:T(8,128)(2,1)S(1)} %collective-permute-done.15.refs_2_), channel_id=1, source_target_pairs={{0,1},{1,0},{2,3},{3,2},{4,5},{5,4},{6,7},{7,6},{8,9},{9,8},{10,11... | collective-permute-start | bytes 2359304 | tf_op jit(solution)/shard_map/ppermute | solution.py:294
  36.0 9.9 %collective-permute-start.3 = (bf16[512,256]{1,0:T(8,128)(2,1)S(1)}, bf16[512,256]{1,0:T(8,128)(2,1)S(1)}, u32[]{:S(2)}, u32[]{:S(2)}) collective-permute-start(bf16[512,256]{1,0:T(8,128)(2,1)S(1)} %collective-permute-done.2.refs_2_), channel_id=1, source_target_pairs={{16,24},{20,28},{17,25},{21,29},{18,26},{22,30},{19,27},{23,31}} | collective-permute-start | bytes 786440 | tf_op jit(solution)/shard_map/ppermute | solution.py:278
  36.7 9.3 %collective-permute-start.13 = (bf16[512,256]{1,0:T(8,128)(2,1)S(1)}, bf16[512,256]{1,0:T(8,128)(2,1)S(1)}, u32[]{:S(2)}, u32[]{:S(2)}) collective-permute-start(bf16[512,256]{1,0:T(8,128)(2,1)S(1)} %collective-permute-done.12.refs_5_), channel_id=1, source_target_pairs={{8,0},{12,4},{9,1},{13,5},{10,2},{14,6},{11,3},{15,7}} | collective-permute-start | bytes 786440 | tf_op jit(solution)/shard_map/ppermute | solution.py:278
  41.0 5.0 %collective-permute-start.7 = (bf16[512,256]{1,0:T(8,128)(2,1)S(1)}, bf16[512,256]{1,0:T(8,128)(2,1)S(1)}, u32[]{:S(2)}, u32[]{:S(2)}) collective-permute-start(bf16[512,256]{1,0:T(8,128)(2,1)S(1)} %collective-permute-done.6.refs_3_), channel_id=1, source_target_pairs={{16,24},{20,28},{17,25},{21,29},{18,26},{22,30},{19,27},{23,31}} | collective-permute-start | bytes 786440 | tf_op jit(solution)/shard_map/ppermute | solution.py:278
  46.8 0.7 %copy-start.1 = (bf16[1024,128]{1,0:T(8,128)(2,1)}, bf16[1024,128]{1,0:T(8,128)(2,1)S(1)}, u32[]{:S(2)}) copy-start(bf16[1024,128]{1,0:T(8,128)(2,1)S(1)} %get-tuple-element.30) | copy-start | bytes 786436
  47.5 9.5 %all-to-all-start = ((bf16[8,128,128]{2,1,0:T(8,128)(2,1)}), bf16[8,128,128]{2,1,0:T(8,128)(2,1)S(1)}, u32[]{:S(2)}, u32[]{:S(2)}) async-start(bf16[8,128,128]{2,1,0:T(8,128)(2,1)} %bitcast.2), calls=%async_computation | async-start | bytes 524288 | tf_op jit(solution)/shard_map/all_to_all | solution.py:319
where the time goes:
time: 58.7 us; the launch traced here: 58.3 us
  starting transfers between devices  27.6 us (47%)
  waiting for transfers between devices  22.2 us (38%)
  Pallas kernels  7.61 us (13%)
  local copies, waits for them, and re-layouts  0.7 us (1%)
    ppermute x12, starting transfers between devices, along(): return lax.ppermute(value, 'frame', pairs)  18.4 us
    ppermute x12, waiting for transfers between devices, along(): return lax.ppermute(value, 'frame', pairs)  13 us
    all_to_all x1, waiting for transfers between devices, on_device(): lax.all_to_all(blocks, ('frame', 'head'), split_axis=0, concat_axis=0, ti...  6.03 us
    pallas_call x4, Pallas kernels, attend(): pl.pallas_call(functools.partial(attend_kernel, cfg), out_shape=outs, in_...  5 us
    ppermute x3, starting transfers between devices, on_device(): weights[offset ^ bit] = lax.ppermute(weights[offset], 'head', pairs)  3.56 us
    all_to_all x1, starting transfers between devices, on_device(): lax.all_to_all(blocks, ('frame', 'head'), split_axis=0, concat_axis=0, ti...  3.41 us
    ppermute x1, waiting for transfers between devices, on_device(): query_rows.append(lax.ppermute(pieces[3], 'frame', swap))  3.14 us
    ppermute x1, starting transfers between devices, on_device(): chunks.append(lax.ppermute(pieces[2], 'frame', swap))  1.56 us
  transfers between devices with their start and end apart: 18, of which 6 were waited for; matrix products, arithmetic and copies ran while one was open for 0% of the time, Pallas kernels for 11%

commit v1 on v0

--- a/solution.py
+++ b/solution.py
@@ -149,9 +149,8 @@
             parts.append(ref[at, column + head * HEAD : column + (head + 1) * HEAD])
         return parts
 
-    def steps(shift, chunk, begin):
-        far = max(0, abs(shift) * group - (group - 1))
-        other = unit + shift
+    def steps(step, other, chunk, begin):
+        far = max(0, step * group - (group - 1))
         most = min(MAX_WIDTH[min(far, RADIUS)], blocks)
         for member in range(group):
             qf = frame_of(unit, place, group, member)
@@ -182,15 +181,16 @@
                             m_ref, acc_ref, head, begin and index == 0,
                         )
 
-    for shift, chunk in zip(shifts, chunks):
-        if shift == 0:
-            steps(shift, chunk, begins)
+    facing = 1 - 2 * lax.rem(unit, 2)
+    for (step, parity), chunk in zip(shifts, chunks):
+        if step == 0:
+            steps(0, unit, chunk, begins)
         else:
-            other = unit + shift
+            other = unit + step * (facing if parity == 0 else -facing)
 
             @pl.when((other >= 0) & (other < units))
-            def _(shift=shift, chunk=chunk):
-                steps(shift, chunk, False)
+            def _(step=step, other=other, chunk=chunk):
+                steps(step, other, chunk, False)
 
     if ends:
         for member in range(group):
@@ -267,6 +267,16 @@
     return group, units, min(units - 1, (RADIUS + group - 1) // group)
 
 
+def edges(units, k, parity):
+    sends = []
+    for low in range(parity, units - 1, 2):
+        if low + 1 - k >= 0:
+            sends.append((low, low + 1))
+        if low + k < units:
+            sends.append((low + 1, low))
+    return sends
+
+
 def on_device(queries, keys, values, band_width, band_offset, out_weight):
     frames, ranks = lax.axis_size("frame"), lax.axis_size("head")
     tokens = queries.shape[0]
@@ -295,20 +305,21 @@
         bit //= 2
     weights = [weights[o] for o in range(ranks)]
 
-    lower, upper = chunks, chunks
-    arrived = []
+    held, arrived = [chunks, chunks], []
     for k in range(1, furthest + 1):
-        up = [(s, s + 1) for s in range(k - 1, units - 1)]
-        down = [(s, s - 1) for s in range(1, units - k + 1)]
-        lower = [along(c, up) for c in lower]
-        upper = [along(c, down) for c in upper]
-        arrived.append((lower, upper))
-
-    cfg = (group, heads, (0,), units, True, False)
+        held = [
+            [along(c, edges(units, k, parity)) for c in source]
+            for parity, source in enumerate(reversed(held))
+            if edges(units, k, parity)
+        ]
+        arrived.append(held)
+
+    cfg = (group, heads, ((0, 0),), units, True, False)
     state = attend(cfg, bands, query_rows, [chunks], [])
-    for k, (lower, upper) in enumerate(arrived, 1):
-        cfg = (group, heads, (-k, k), units, False, k == furthest)
-        state = attend(cfg, bands, query_rows, [lower, upper], state)
+    for k, received in enumerate(arrived, 1):
+        shifts = tuple((k, parity) for parity in range(2) if edges(units, k, parity))
+        cfg = (group, heads, shifts, units, False, k == furthest)
+        state = attend(cfg, bands, query_rows, received, state)
     attended = state[0]
 
     members = [

time: 58.7 us -> 60.3 us (1.027)
  waiting for transfers between devices: 22.2 us -> 31.6 us
  starting transfers between devices: 27.6 us -> 19.9 us
    ppermute x12 -> x10, waiting for transfers between devices: 13 us -> 20.6 us  [along(): return lax.ppermute(value, 'frame', pairs)]
    ppermute x12 -> x10, starting transfers between devices: 18.4 us -> 11 us  [along(): return lax.ppermute(value, 'frame', pairs)]
    ppermute x1, waiting for transfers between devices: 0.01 us -> 4.89 us  [on_device(): chunks.append(lax.ppermute(pieces[2], 'frame', swap))]
    ppermute x1, waiting for transfers between devices: 3.14 us -> 0.01 us  [on_device(): query_rows.append(lax.ppermute(pieces[3], 'frame', swap))]
  transfers between devices with their start and end apart: 18 -> 16, of which waited for: 6 -> 8; matrix products, arithmetic and copies ran while one was open for 0% -> 0% of each run, Pallas kernels for 11% -> 10%
where the time goes in v1:
time: 60.3 us; the launch traced here: 60 us
  waiting for transfers between devices  31.6 us (52%)
  starting transfers between devices  19.9 us (33%)
  Pallas kernels  7.53 us (12%)
  local copies, waits for them, and re-layouts  0.7 us (1%)
    ppermute x10, waiting for transfers between devices, along(): return lax.ppermute(value, 'frame', pairs)  20.6 us
    ppermute x10, starting transfers between devices, along(): return lax.ppermute(value, 'frame', pairs)  11 us
    all_to_all x1, waiting for transfers between devices, on_device(): lax.all_to_all(blocks, ('frame', 'head'), split_axis=0, concat_axis=0, ti...  6.03 us
    pallas_call x4, Pallas kernels, attend(): pl.pallas_call(functools.partial(attend_kernel, cfg), out_shape=outs, in_...  4.91 us
    ppermute x1, waiting for transfers between devices, on_device(): chunks.append(lax.ppermute(pieces[2], 'frame', swap))  4.89 us
    ppermute x3, starting transfers between devices, on_device(): weights[offset ^ bit] = lax.ppermute(weights[offset], 'head', pairs)  3.42 us
    all_to_all x1, starting transfers between devices, on_device(): lax.all_to_all(blocks, ('frame', 'head'), split_axis=0, concat_axis=0, ti...  3.41 us
    ppermute x1, starting transfers between devices, on_device(): chunks.append(lax.ppermute(pieces[2], 'frame', swap))  1.56 us
  transfers between devices with their start and end apart: 16, of which 8 were waited for; matrix products, arithmetic and copies ran while one was open for 0% of the time, Pallas kernels for 10%

profile of v1, /device:TPU:0, one launch (start us, length us, event | category | flops | bytes accessed | tf_op | source)
XLA Modules:
  0.0 60.0 jit_solution(4373026469320490436)
XLA Ops:
  0.0 0.0 copy-start
  0.0 3.0 %collective-permute-start.13 = (bf16[256,1536]{1,0:T(8,128)(2,1)}, bf16[256,1536]{1,0:T(8,128)(2,1)S(1)}, u32[]{:S(2)}, u32[]{:S(2)}) collective-permute-start(bf16[256,1536]{1,0:T(8,128)(2,1)} %refs_0_.1), channel_id=1, source_target_pairs={{0,2},{1,3},{2,0},{3,1},{4,6},{5,7},{6,4},{7,5},{8,10},{9,11},{10,... | collective-permute-start | bytes 2359304 | tf_op jit(solution)/shard_map/ppermute | solution.py:304
  3.0 1.3 %split.1 = (bf16[512,256]{1,0:T(8,128)(2,1)S(1)}, bf16[512,128]{1,0:T(8,128)(2,1)S(1)}, bf16[512,256]{1,0:T(8,128)(2,1)S(1)}, bf16[512,128]{1,0:T(8,128)(2,1)S(1...) custom-call(bf16[512,256]{1,0:T(8,128)(2,1)} %q_ref.1, bf16[512,256]{1,0:T(8,128)(2,1)} %k_ref.1, bf16[512,256]{1,0:T(8,128)(2,1)} %v_ref.1, ...), custom_call_target="tpu_custom_call" | custom-call | tf_op jit(solution)/shard_map/split/pallas_call | solution.py:66
  4.3 1.6 %collective-permute-start.4 = (bf16[512,256]{1,0:T(8,128)(2,1)S(1)}, bf16[512,256]{1,0:T(8,128)(2,1)S(1)}, u32[]{:S(2)}, u32[]{:S(2)}) collective-permute-start(bf16[512,256]{1,0:T(8,128)(2,1)S(1)} %get-tuple-element.23), channel_id=1, source_target_pairs={{0,4},{4,0},{8,12},{12,8},{16,20},{20,16},{24,28},{28,24},{1,5},{5... | collective-permute-start | bytes 786440 | tf_op jit(solution)/shard_map/ppermute | solution.py:296
  5.8 0.5 collective-permute-start
  6.4 1.6 %collective-permute-start.1 = (bf16[512,256]{1,0:T(8,128)(2,1)S(1)}, bf16[512,256]{1,0:T(8,128)(2,1)S(1)}, u32[]{:S(2)}, u32[]{:S(2)}) collective-permute-start(bf16[512,256]{1,0:T(8,128)(2,1)S(1)} %get-tuple-element.22.refs_2_), channel_id=1, source_target_pairs={{0,8},{4,12},{8,0},{12,4},{16,24},{20,28},{24,16},{28,20},{1,9},{5... | collective-permute-start | bytes 786440 | tf_op jit(solution)/shard_map/ppermute | solution.py:288
  8.0 0.7 %collective-permute-start.8 = (bf16[512,256]{1,0:T(8,128)(2,1)S(1)}, bf16[512,256]{1,0:T(8,128)(2,1)S(1)}, u32[]{:S(2)}, u32[]{:S(2)}) collective-permute-start(bf16[512,256]{1,0:T(8,128)(2,1)S(1)} %get-tuple-element.22.refs_2_), channel_id=1, source_target_pairs={{8,16},{12,20},{16,8},{20,12},{9,17},{13,21},{17,9},{21,13},{10,18... | collective-permute-start | bytes 786440 | tf_op jit(solution)/shard_map/ppermute | solution.py:288
  8.6 4.9 %collective-permute-done.4.refs_3_ = bf16[512,256]{1,0:T(8,128)(2,1)S(1)} collective-permute-done((bf16[512,256]{1,0:T(8,128)(2,1)S(1)}, bf16[512,256]{1,0:T(8,128)(2,1)S(1)}, u32[]{:S(2)}, u32[]{:S(2)}) %collective-permute-start.4) | collective-permute-done | bytes 262176 | tf_op jit(solution)/shard_map/ppermute | solution.py:296
  13.5 1.6 %collective-permute-start.5 = (bf16[512,256]{1,0:T(8,128)(2,1)S(1)}, bf16[512,256]{1,0:T(8,128)(2,1)S(1)}, u32[]{:S(2)}, u32[]{:S(2)}) collective-permute-start(bf16[512,256]{1,0:T(8,128)(2,1)S(1)} %collective-permute-done.4.refs_3_), channel_id=1, source_target_pairs={{0,8},{4,12},{8,0},{12,4},{16,24},{20,28},{24,16},{28,20},{1,9},{5... | collective-permute-start | bytes 786440 | tf_op jit(solution)/shard_map/ppermute | solution.py:288
  15.1 0.0 collective-permute-done.refs_1_
  15.1 0.7 %collective-permute-start.10 = (bf16[512,256]{1,0:T(8,128)(2,1)S(1)}, bf16[512,256]{1,0:T(8,128)(2,1)S(1)}, u32[]{:S(2)}, u32[]{:S(2)}) collective-permute-start(bf16[512,256]{1,0:T(8,128)(2,1)S(1)} %collective-permute-done.4.refs_3_), channel_id=1, source_target_pairs={{8,16},{12,20},{16,8},{20,12},{9,17},{13,21},{17,9},{21,13},{10,18... | collective-permute-start | bytes 786440 | tf_op jit(solution)/shard_map/ppermute | solution.py:288
  15.8 0.0 collective-permute-done.1.refs_2_
  15.8 0.7 %collective-permute-start.2 = (bf16[512,256]{1,0:T(8,128)(2,1)S(1)}, bf16[512,256]{1,0:T(8,128)(2,1)S(1)}, u32[]{:S(2)}, u32[]{:S(2)}) collective-permute-start(bf16[512,256]{1,0:T(8,128)(2,1)S(1)} %collective-permute-done.1.refs_2_), channel_id=1, source_target_pairs={{8,16},{12,20},{16,8},{20,12},{9,17},{13,21},{17,9},{21,13},{10,18... | collective-permute-start | bytes 786440 | tf_op jit(solution)/shard_map/ppermute | solution.py:288
  16.5 0.0 collective-permute-done.8.refs_4_
  16.5 1.3 %collective-permute-start.9 = (bf16[512,256]{1,0:T(8,128)(2,1)S(1)}, bf16[512,256]{1,0:T(8,128)(2,1)S(1)}, u32[]{:S(2)}, u32[]{:S(2)}) collective-permute-start(bf16[512,256]{1,0:T(8,128)(2,1)S(1)} %collective-permute-done.8.refs_4_), channel_id=1, source_target_pairs={{8,0},{12,4},{16,24},{20,28},{9,1},{13,5},{17,25},{21,29},{10,2},{... | collective-permute-start | bytes 786440 | tf_op jit(solution)/shard_map/ppermute | solution.py:288
  17.8 2.1 %collective-permute-done.5.refs_3_ = bf16[512,256]{1,0:T(8,128)(2,1)S(1)} collective-permute-done((bf16[512,256]{1,0:T(8,128)(2,1)S(1)}, bf16[512,256]{1,0:T(8,128)(2,1)S(1)}, u32[]{:S(2)}, u32[]{:S(2)}) %collective-permute-start.5) | collective-permute-done | bytes 262176 | tf_op jit(solution)/shard_map/ppermute | solution.py:288
  19.9 0.7 %collective-permute-start.6 = (bf16[512,256]{1,0:T(8,128)(2,1)S(1)}, bf16[512,256]{1,0:T(8,128)(2,1)S(1)}, u32[]{:S(2)}, u32[]{:S(2)}) collective-permute-start(bf16[512,256]{1,0:T(8,128)(2,1)S(1)} %collective-permute-done.5.refs_3_), channel_id=1, source_target_pairs={{8,16},{12,20},{16,8},{20,12},{9,17},{13,21},{17,9},{21,13},{10,18... | collective-permute-start | bytes 786440 | tf_op jit(solution)/shard_map/ppermute | solution.py:288
  20.6 0.0 collective-permute-done.10.refs_5_
  20.6 0.0 copy-done
  20.6 0.1 collective-permute-start.12
  20.7 0.1 collective-permute-done.13.refs_2_
  20.8 0.4 collective-permute-start.14
  21.2 0.0 collective-permute-done.2.refs_4_
  21.2 1.3 %collective-permute-start.11 = (bf16[512,256]{1,0:T(8,128)(2,1)S(1)}, bf16[512,256]{1,0:T(8,128)(2,1)S(1)}, u32[]{:S(2)}, u32[]{:S(2)}) collective-permute-start(bf16[512,256]{1,0:T(8,128)(2,1)S(1)} %collective-permute-done.10.refs_5_), channel_id=1, source_target_pairs={{8,0},{12,4},{16,24},{20,28},{9,1},{13,5},{17,25},{21,29},{10,2},{... | collective-permute-start | bytes 786440 | tf_op jit(solution)/shard_map/ppermute | solution.py:288
  22.5 5.8 %collective-permute-done.9.refs_2_ = bf16[512,256]{1,0:T(8,128)(2,1)S(1)} collective-permute-done((bf16[512,256]{1,0:T(8,128)(2,1)S(1)}, bf16[512,256]{1,0:T(8,128)(2,1)S(1)}, u32[]{:S(2)}, u32[]{:S(2)}) %collective-permute-start.9) | collective-permute-done | bytes 262176 | tf_op jit(solution)/shard_map/ppermute | solution.py:288
  28.3 1.3 %collective-permute-start.3 = (bf16[512,256]{1,0:T(8,128)(2,1)S(1)}, bf16[512,256]{1,0:T(8,128)(2,1)S(1)}, u32[]{:S(2)}, u32[]{:S(2)}) collective-permute-start(bf16[512,256]{1,0:T(8,128)(2,1)S(1)} %collective-permute-done.2.refs_4_), channel_id=1, source_target_pairs={{8,0},{12,4},{16,24},{20,28},{9,1},{13,5},{17,25},{21,29},{10,2},{... | collective-permute-start | bytes 786440 | tf_op jit(solution)/shard_map/ppermute | solution.py:288
  29.6 0.0 collective-permute-done.6.refs_5_
  29.6 1.3 %collective-permute-start.7 = (bf16[512,256]{1,0:T(8,128)(2,1)S(1)}, bf16[512,256]{1,0:T(8,128)(2,1)S(1)}, u32[]{:S(2)}, u32[]{:S(2)}) collective-permute-start(bf16[512,256]{1,0:T(8,128)(2,1)S(1)} %collective-permute-done.6.refs_5_), channel_id=1, source_target_pairs={{8,0},{12,4},{16,24},{20,28},{9,1},{13,5},{17,25},{21,29},{10,2},{... | collective-permute-start | bytes 786440 | tf_op jit(solution)/shard_map/ppermute | solution.py:288
  30.9 1.5 %shard_map.64 = (f32[1,1024,128]{2,1,0:T(8,128)S(1)}, f32[1,1024,256]{2,1,0:T(8,128)S(1)}) custom-call(s32[8,8]{1,0:T(8,128)S(4)} %get-tuple-element.18.width_ref, s32[8,4,8]{2,1,0:T(4,128)S(4)} %get-tuple-element.19.offset_ref, bf16[512,128]{1,0:T(8,128)(2,1)S(1)} %get-tuple-element.20.refs_0_, bf16[512,128]{1,0:T(8,128)(2,1)S(1)} %collective-permute-done.refs_1_, ...), custom_call_target="tpu_custom_call" | custom-call | flops 536870912 | bytes 1048576 | tf_op jit(solution)/shard_map/pallas_call | solution.py:224
  32.4 1.7 %shard_map.65 = (f32[1,1024,128]{2,1,0:T(8,128)S(1)}, f32[1,1024,256]{2,1,0:T(8,128)S(1)}) custom-call(s32[8,8]{1,0:T(8,128)S(4)} %get-tuple-element.18.width_ref, s32[8,4,8]{2,1,0:T(4,128)S(4)} %get-tuple-element.19.offset_ref, bf16[512,128]{1,0:T(8,128)(2,1)S(1)} %get-tuple-element.20.refs_0_, ...), custom_call_target="tpu_custom_call", output_to_operand_aliasing={{0}: (8, {}), {1}: (9, {})} | custom-call | flops 1073741824 | bytes 1048576 | tf_op jit(solution)/shard_map/pallas_call | solution.py:224
  34.1 7.5 %collective-permute-done.11.refs_3_ = bf16[512,256]{1,0:T(8,128)(2,1)S(1)} collective-permute-done((bf16[512,256]{1,0:T(8,128)(2,1)S(1)}, bf16[512,256]{1,0:T(8,128)(2,1)S(1)}, u32[]{:S(2)}, u32[]{:S(2)}) %collective-permute-start.11) | collective-permute-done | bytes 262176 | tf_op jit(solution)/shard_map/ppermute | solution.py:288
  41.6 1.0 %shard_map.66 = (f32[1,1024,128]{2,1,0:T(8,128)S(1)}, f32[1,1024,256]{2,1,0:T(8,128)S(1)}) custom-call(s32[8,8]{1,0:T(8,128)S(4)} %get-tuple-element.18.width_ref, s32[8,4,8]{2,1,0:T(4,128)S(4)} %get-tuple-element.19.offset_ref, bf16[512,128]{1,0:T(8,128)(2,1)S(1)} %get-tuple-element.20.refs_0_, ...), custom_call_target="tpu_custom_call", output_to_operand_aliasing={{0}: (8, {}), {1}: (9, {})} | custom-call | flops 1073741824 | bytes 1048576 | tf_op jit(solution)/shard_map/pallas_call | solution.py:224
  42.6 2.3 %collective-permute-done.3.refs_2_ = bf16[512,256]{1,0:T(8,128)(2,1)S(1)} collective-permute-done((bf16[512,256]{1,0:T(8,128)(2,1)S(1)}, bf16[512,256]{1,0:T(8,128)(2,1)S(1)}, u32[]{:S(2)}, u32[]{:S(2)}) %collective-permute-start.3) | collective-permute-done | bytes 262176 | tf_op jit(solution)/shard_map/ppermute | solution.py:288
  44.9 2.8 %collective-permute-done.7.refs_3_ = bf16[512,256]{1,0:T(8,128)(2,1)S(1)} collective-permute-done((bf16[512,256]{1,0:T(8,128)(2,1)S(1)}, bf16[512,256]{1,0:T(8,128)(2,1)S(1)}, u32[]{:S(2)}, u32[]{:S(2)}) %collective-permute-start.7) | collective-permute-done | bytes 262176 | tf_op jit(solution)/shard_map/ppermute | solution.py:288
  47.7 0.7 %shard_map.67 = (bf16[1024,128]{1,0:T(8,128)(2,1)S(1)}, f32[1,1024,128]{2,1,0:T(8,128)S(1)}, f32[1,1024,256]{2,1,0:T(8,128)S(1)}) custom-call(s32[8,8]{1,0:T(8,128)S(4)} %get-tuple-element.18.width_ref, s32[8,4,8]{2,1,0:T(4,128)S(4)} %get-tuple-element.19.offset_ref, ...), custom_call_target="tpu_custom_call", output_to_operand_aliasing={{1}: (6, {}), {2}: (7, {})} | custom-call | flops 536870912 | bytes 1048576 | tf_op jit(solution)/shard_map/pallas_call | solution.py:224
  48.5 0.0 copy-start.1
  48.5 0.7 %copy-done.1 = bf16[1024,128]{1,0:T(8,128)(2,1)} copy-done((bf16[1024,128]{1,0:T(8,128)(2,1)}, bf16[1024,128]{1,0:T(8,128)(2,1)S(1)}, u32[]{:S(2)}) %copy-start.1) | copy-done | bytes 262168
  49.2 3.4 %all-to-all-start = ((bf16[8,128,128]{2,1,0:T(8,128)(2,1)}), bf16[8,128,128]{2,1,0:T(8,128)(2,1)S(1)}, u32[]{:S(2)}, u32[]{:S(2)}) async-start(bf16[8,128,128]{2,1,0:T(8,128)(2,1)} %bitcast.2), calls=%async_computation | async-start | bytes 524288 | tf_op jit(solution)/shard_map/all_to_all | solution.py:330
  52.6 0.0 collective-permute-done.12.refs_1_
  52.6 6.0 %all-to-all-done.rows_ref = bf16[8,128,128]{2,1,0:T(8,128)(2,1)S(1)} async-done(((bf16[8,128,128]{2,1,0:T(8,128)(2,1)}), bf16[8,128,128]{2,1,0:T(8,128)(2,1)S(1)}, u32[]{:S(2)}, u32[]{:S(2)}) %all-to-all-start) | async-done | bytes 262176 | tf_op jit(solution)/shard_map/all_to_all | solution.py:330
  58.6 0.0 collective-permute-done.14.refs_3_
  58.6 1.3 %project.1 = bf16[128,1536]{1,0:T(8,128)(2,1)} custom-call(bf16[8,128,128]{2,1,0:T(8,128)(2,1)S(1)} %all-to-all-done.rows_ref, bf16[256,1536]{1,0:T(8,128)(2,1)S(1)} %copy-done, bf16[256,1536]{1,0:T(8,128)(2,1)S(1)} %collective-permute-done.12.refs_1_, bf16[256,1536]{1,0:T(8,128)(2,1)S(1)} %collective-permute-done.13.refs_2_, ...), custom_call_target="tpu_custom_call" | custom-call | flops 402653184 | bytes 1048576 | tf_op jit(solution)/shard_map/project/pallas_call | solution.py:250
Async XLA Ops:
  0.0 20.6 %copy-start = (bf16[256,1536]{1,0:T(8,128)(2,1)S(1)}, bf16[256,1536]{1,0:T(8,128)(2,1)}, u32[]{:S(2)}) copy-start(bf16[256,1536]{1,0:T(8,128)(2,1)} %refs_0_.1) | copy-start | bytes 2359300
  0.0 20.8 %collective-permute-start.13 = (bf16[256,1536]{1,0:T(8,128)(2,1)}, bf16[256,1536]{1,0:T(8,128)(2,1)S(1)}, u32[]{:S(2)}, u32[]{:S(2)}) collective-permute-start(bf16[256,1536]{1,0:T(8,128)(2,1)} %refs_0_.1), channel_id=1, source_target_pairs={{0,2},{1,3},{2,0},{3,1},{4,6},{5,7},{6,4},{7,5},{8,10},{9,11},{10,... | collective-permute-start | bytes 2359304 | tf_op jit(solution)/shard_map/ppermute | solution.py:304
  4.3 9.2 %collective-permute-start.4 = (bf16[512,256]{1,0:T(8,128)(2,1)S(1)}, bf16[512,256]{1,0:T(8,128)(2,1)S(1)}, u32[]{:S(2)}, u32[]{:S(2)}) collective-permute-start(bf16[512,256]{1,0:T(8,128)(2,1)S(1)} %get-tuple-element.23), channel_id=1, source_target_pairs={{0,4},{4,0},{8,12},{12,8},{16,20},{20,16},{24,28},{28,24},{1,5},{5... | collective-permute-start | bytes 786440 | tf_op jit(solution)/shard_map/ppermute | solution.py:296
  5.8 9.3 %collective-permute-start = (bf16[512,128]{1,0:T(8,128)(2,1)S(1)}, bf16[512,128]{1,0:T(8,128)(2,1)S(1)}, u32[]{:S(2)}, u32[]{:S(2)}) collective-permute-start(bf16[512,128]{1,0:T(8,128)(2,1)S(1)} %get-tuple-element.21), channel_id=1, source_target_pairs={{0,4},{4,0},{8,12},{12,8},{16,20},{20,16},{24,28},{28,24},{1,5},{5... | collective-permute-start | bytes 393224 | tf_op jit(solution)/shard_map/ppermute | solution.py:297
  6.4 9.4 %collective-permute-start.1 = (bf16[512,256]{1,0:T(8,128)(2,1)S(1)}, bf16[512,256]{1,0:T(8,128)(2,1)S(1)}, u32[]{:S(2)}, u32[]{:S(2)}) collective-permute-start(bf16[512,256]{1,0:T(8,128)(2,1)S(1)} %get-tuple-element.22.refs_2_), channel_id=1, source_target_pairs={{0,8},{4,12},{8,0},{12,4},{16,24},{20,28},{24,16},{28,20},{1,9},{5... | collective-permute-start | bytes 786440 | tf_op jit(solution)/shard_map/ppermute | solution.py:288
  8.0 8.5 %collective-permute-start.8 = (bf16[512,256]{1,0:T(8,128)(2,1)S(1)}, bf16[512,256]{1,0:T(8,128)(2,1)S(1)}, u32[]{:S(2)}, u32[]{:S(2)}) collective-permute-start(bf16[512,256]{1,0:T(8,128)(2,1)S(1)} %get-tuple-element.22.refs_2_), channel_id=1, source_target_pairs={{8,16},{12,20},{16,8},{20,12},{9,17},{13,21},{17,9},{21,13},{10,18... | collective-permute-start | bytes 786440 | tf_op jit(solution)/shard_map/ppermute | solution.py:288
  13.5 6.4 %collective-permute-start.5 = (bf16[512,256]{1,0:T(8,128)(2,1)S(1)}, bf16[512,256]{1,0:T(8,128)(2,1)S(1)}, u32[]{:S(2)}, u32[]{:S(2)}) collective-permute-start(bf16[512,256]{1,0:T(8,128)(2,1)S(1)} %collective-permute-done.4.refs_3_), channel_id=1, source_target_pairs={{0,8},{4,12},{8,0},{12,4},{16,24},{20,28},{24,16},{28,20},{1,9},{5... | collective-permute-start | bytes 786440 | tf_op jit(solution)/shard_map/ppermute | solution.py:288
  15.1 5.5 %collective-permute-start.10 = (bf16[512,256]{1,0:T(8,128)(2,1)S(1)}, bf16[512,256]{1,0:T(8,128)(2,1)S(1)}, u32[]{:S(2)}, u32[]{:S(2)}) collective-permute-start(bf16[512,256]{1,0:T(8,128)(2,1)S(1)} %collective-permute-done.4.refs_3_), channel_id=1, source_target_pairs={{8,16},{12,20},{16,8},{20,12},{9,17},{13,21},{17,9},{21,13},{10,18... | collective-permute-start | bytes 786440 | tf_op jit(solution)/shard_map/ppermute | solution.py:288
  15.8 5.4 %collective-permute-start.2 = (bf16[512,256]{1,0:T(8,128)(2,1)S(1)}, bf16[512,256]{1,0:T(8,128)(2,1)S(1)}, u32[]{:S(2)}, u32[]{:S(2)}) collective-permute-start(bf16[512,256]{1,0:T(8,128)(2,1)S(1)} %collective-permute-done.1.refs_2_), channel_id=1, source_target_pairs={{8,16},{12,20},{16,8},{20,12},{9,17},{13,21},{17,9},{21,13},{10,18... | collective-permute-start | bytes 786440 | tf_op jit(solution)/shard_map/ppermute | solution.py:288
  16.5 11.8 %collective-permute-start.9 = (bf16[512,256]{1,0:T(8,128)(2,1)S(1)}, bf16[512,256]{1,0:T(8,128)(2,1)S(1)}, u32[]{:S(2)}, u32[]{:S(2)}) collective-permute-start(bf16[512,256]{1,0:T(8,128)(2,1)S(1)} %collective-permute-done.8.refs_4_), channel_id=1, source_target_pairs={{8,0},{12,4},{16,24},{20,28},{9,1},{13,5},{17,25},{21,29},{10,2},{... | collective-permute-start | bytes 786440 | tf_op jit(solution)/shard_map/ppermute | solution.py:288
  19.9 9.7 %collective-permute-start.6 = (bf16[512,256]{1,0:T(8,128)(2,1)S(1)}, bf16[512,256]{1,0:T(8,128)(2,1)S(1)}, u32[]{:S(2)}, u32[]{:S(2)}) collective-permute-start(bf16[512,256]{1,0:T(8,128)(2,1)S(1)} %collective-permute-done.5.refs_3_), channel_id=1, source_target_pairs={{8,16},{12,20},{16,8},{20,12},{9,17},{13,21},{17,9},{21,13},{10,18... | collective-permute-start | bytes 786440 | tf_op jit(solution)/shard_map/ppermute | solution.py:288
  20.6 32.0 %collective-permute-start.12 = (bf16[256,1536]{1,0:T(8,128)(2,1)S(1)}, bf16[256,1536]{1,0:T(8,128)(2,1)S(1)}, u32[]{:S(2)}, u32[]{:S(2)}) collective-permute-start(bf16[256,1536]{1,0:T(8,128)(2,1)S(1)} %copy-done), channel_id=1, source_target_pairs={{0,1},{1,0},{2,3},{3,2},{4,5},{5,4},{6,7},{7,6},{8,9},{9,8},{10,11... | collective-permute-start | bytes 2359304 | tf_op jit(solution)/shard_map/ppermute | solution.py:304
  20.8 37.8 %collective-permute-start.14 = (bf16[256,1536]{1,0:T(8,128)(2,1)S(1)}, bf16[256,1536]{1,0:T(8,128)(2,1)S(1)}, u32[]{:S(2)}, u32[]{:S(2)}) collective-permute-start(bf16[256,1536]{1,0:T(8,128)(2,1)S(1)} %collective-permute-done.13.refs_2_), channel_id=1, source_target_pairs={{0,1},{1,0},{2,3},{3,2},{4,5},{5,4},{6,7},{7,6},{8,9},{9,8},{10,11... | collective-permute-start | bytes 2359304 | tf_op jit(solution)/shard_map/ppermute | solution.py:304
  21.2 20.4 %collective-permute-start.11 = (bf16[512,256]{1,0:T(8,128)(2,1)S(1)}, bf16[512,256]{1,0:T(8,128)(2,1)S(1)}, u32[]{:S(2)}, u32[]{:S(2)}) collective-permute-start(bf16[512,256]{1,0:T(8,128)(2,1)S(1)} %collective-permute-done.10.refs_5_), channel_id=1, source_target_pairs={{8,0},{12,4},{16,24},{20,28},{9,1},{13,5},{17,25},{21,29},{10,2},{... | collective-permute-start | bytes 786440 | tf_op jit(solution)/shard_map/ppermute | solution.py:288
  28.3 16.7 %collective-permute-start.3 = (bf16[512,256]{1,0:T(8,128)(2,1)S(1)}, bf16[512,256]{1,0:T(8,128)(2,1)S(1)}, u32[]{:S(2)}, u32[]{:S(2)}) collective-permute-start(bf16[512,256]{1,0:T(8,128)(2,1)S(1)} %collective-permute-done.2.refs_4_), channel_id=1, source_target_pairs={{8,0},{12,4},{16,24},{20,28},{9,1},{13,5},{17,25},{21,29},{10,2},{... | collective-permute-start | bytes 786440 | tf_op jit(solution)/shard_map/ppermute | solution.py:288
  29.6 18.2 %collective-permute-start.7 = (bf16[512,256]{1,0:T(8,128)(2,1)S(1)}, bf16[512,256]{1,0:T(8,128)(2,1)S(1)}, u32[]{:S(2)}, u32[]{:S(2)}) collective-permute-start(bf16[512,256]{1,0:T(8,128)(2,1)S(1)} %collective-permute-done.6.refs_5_), channel_id=1, source_target_pairs={{8,0},{12,4},{16,24},{20,28},{9,1},{13,5},{17,25},{21,29},{10,2},{... | collective-permute-start | bytes 786440 | tf_op jit(solution)/shard_map/ppermute | solution.py:288
  48.5 0.7 %copy-start.1 = (bf16[1024,128]{1,0:T(8,128)(2,1)}, bf16[1024,128]{1,0:T(8,128)(2,1)S(1)}, u32[]{:S(2)}) copy-start(bf16[1024,128]{1,0:T(8,128)(2,1)S(1)} %get-tuple-element.30) | copy-start | bytes 786436
  49.2 9.5 %all-to-all-start = ((bf16[8,128,128]{2,1,0:T(8,128)(2,1)}), bf16[8,128,128]{2,1,0:T(8,128)(2,1)S(1)}, u32[]{:S(2)}, u32[]{:S(2)}) async-start(bf16[8,128,128]{2,1,0:T(8,128)(2,1)} %bitcast.2), calls=%async_computation | async-start | bytes 524288 | tf_op jit(solution)/shard_map/all_to_all | solution.py:330

commit v2 on v1

--- a/solution.py
+++ b/solution.py
@@ -102,18 +102,31 @@
     m_ref[head, rows, :] = peak
 
 
+def unit_at(spec, unit, units):
+    kind, step, parity = spec
+    if kind == "own":
+        return unit, None
+    if kind == "edge":
+        facing = 1 - 2 * lax.rem(unit, 2)
+        other = unit + step * (facing if parity == 0 else -facing)
+        return other, (other >= 0) & (other < units)
+    inwards = jnp.where(2 * unit < units, 1, -1)
+    return unit + step * inwards, (unit > 0) & (unit < units - 1)
+
+
 def attend_kernel(cfg, width_ref, offset_ref, *refs):
-    group, heads, shifts, units, begins, ends = cfg
-    q_refs, refs = refs[:group], refs[group:]
-    chunks = [refs[group * i : group * (i + 1)] for i in range(len(shifts))]
-    refs = refs[group * len(shifts) :]
+    group, heads, units, queries, keys, jobs, begins, ends = cfg
+    q_sets = [refs[group * i : group * (i + 1)] for i in range(len(queries))]
+    refs = refs[group * len(queries) :]
+    chunks = [refs[group * i : group * (i + 1)] for i in range(len(keys))]
+    refs = refs[group * len(keys) :]
     if not begins:
         refs = refs[2:]
     if ends:
         out_ref, m_ref, acc_ref = refs
     else:
         m_ref, acc_ref = refs
-    tokens = q_refs[0].shape[0]
+    tokens = q_sets[0][0].shape[0]
     blocks = tokens // BLK
     width = heads * HEAD
     me = lax.axis_index("frame")
@@ -149,11 +162,11 @@
             parts.append(ref[at, column + head * HEAD : column + (head + 1) * HEAD])
         return parts
 
-    def steps(step, other, chunk, begin):
+    def steps(step, base, mine, q_refs, other, chunk, begin):
         far = max(0, step * group - (group - 1))
         most = min(MAX_WIDTH[min(far, RADIUS)], blocks)
         for member in range(group):
-            qf = frame_of(unit, place, group, member)
+            qf = frame_of(mine, place, group, member)
             order = [member] + [i for i in range(group) if i != member]
             batches = [[i] for i in order] if most == blocks else [order]
             for index, batch in enumerate(batches):
@@ -171,7 +184,8 @@
                             ],
                             axis=0,
                         )
-                        rows = slice(member * tokens + b * BLK, member * tokens + (b + 1) * BLK)
+                        low = base + member * tokens + b * BLK
+                        rows = slice(low, low + BLK)
                         query = q_refs[member][
                             b * BLK : (b + 1) * BLK, head * HEAD : (head + 1) * HEAD
                         ]
@@ -181,34 +195,47 @@
                             m_ref, acc_ref, head, begin and index == 0,
                         )
 
-    facing = 1 - 2 * lax.rem(unit, 2)
-    for (step, parity), chunk in zip(shifts, chunks):
-        if step == 0:
-            steps(0, unit, chunk, begins)
+    for q, k, step, begin in jobs:
+        mine, there = unit_at(queries[q], unit, units)
+        other, counts = unit_at(keys[k], unit, units)
+        guard = counts if there is None else there
+        run = functools.partial(
+            steps, step, q * group * tokens, mine, q_sets[q], other, chunks[k], begin
+        )
+        if guard is None:
+            run()
         else:
-            other = unit + step * (facing if parity == 0 else -facing)
-
-            @pl.when((other >= 0) & (other < units))
-            def _(step=step, other=other, chunk=chunk):
-                steps(step, other, chunk, False)
+            pl.when(guard)(run)
+
+    def finish():
+        for q, spec in enumerate(queries):
+            base = q * group * tokens
+            slab = 0
+            if len(queries) > 1:
+                slab = lax.rem(unit_at(spec, unit, units)[0], 2) * group * tokens
+            for member in range(group):
+                start = slab + (place if member == 0 else group - 1 - place) * tokens
+                for head in range(heads):
+                    for b in range(blocks):
+                        low = base + member * tokens + b * BLK
+                        both = acc_ref[head, low : low + BLK, :]
+                        at = pl.ds(pl.multiple_of(start + b * BLK, BLK), BLK)
+                        out_ref[at, head * HEAD : (head + 1) * HEAD] = (
+                            both[:, :HEAD] / both[:, HEAD:]
+                        ).astype(out_ref.dtype)
 
     if ends:
-        for member in range(group):
-            start = (place if member == 0 else group - 1 - place) * tokens
-            for head in range(heads):
-                for b in range(blocks):
-                    rows = slice(member * tokens + b * BLK, member * tokens + (b + 1) * BLK)
-                    both = acc_ref[head, rows, :]
-                    at = pl.ds(pl.multiple_of(start + b * BLK, BLK), BLK)
-                    out_ref[at, head * HEAD : (head + 1) * HEAD] = (
-                        both[:, :HEAD] / both[:, HEAD:]
-                    ).astype(out_ref.dtype)
+        inner = unit_at(queries[0], unit, units)[1]
+        if inner is None:
+            finish()
+        else:
+            pl.when(inner)(finish)
 
 
 def attend(cfg, bands, queries, chunks, state):
-    group, heads, _, _, begins, ends = cfg
+    group, heads, _, query_units, _, jobs, begins, ends = cfg
     tokens = queries[0].shape[0]
-    rows = group * tokens
+    rows = len(query_units) * group * tokens
     m_shape = pltpu.VMEM((heads, rows, BLK), jnp.float32)
     acc_shape = pltpu.VMEM((heads, rows, 2 * HEAD), jnp.float32)
     flat = [in_vmem(c) for pair in chunks for c in pair]
@@ -220,7 +247,7 @@
     if ends:
         outs = [jax.ShapeDtypeStruct((rows, heads * HEAD), queries[0].dtype), m_shape, acc_shape]
         aliases = {index: out + 1 for index, out in aliases.items()}
-    work = 4 * len(flat) * tokens * rows * heads * HEAD
+    work = 4 * len(jobs) * (group * tokens) ** 2 * heads * HEAD
     return pl.pallas_call(
         functools.partial(attend_kernel, cfg),
         out_shape=outs,
@@ -229,26 +256,31 @@
         input_output_aliases=aliases,
         compiler_params=params(),
         cost_estimate=pl.CostEstimate(flops=work, bytes_accessed=1 << 20, transcendentals=0),
+        name="attend",
     )(*inputs)
 
 
-def project_kernel(group, ranks, rows_ref, *refs):
+def project_kernel(group, ranks, slabs, rows_ref, *refs):
     weights, out_ref = refs[:-1], refs[-1]
     me = lax.axis_index("head")
+    base = 0
+    if slabs > 1:
+        pair = lax.axis_index("frame") // (slabs * group)
+        base = (1 - pair) * group * ranks
     total = None
     for offset, weight in enumerate(weights):
         owner = me ^ offset
-        left = jnp.concatenate([rows_ref[i * ranks + owner] for i in range(group)], axis=1)
+        left = jnp.concatenate([rows_ref[base + i * ranks + owner] for i in range(group)], axis=1)
         term = jnp.dot(left, weight[...], preferred_element_type=jnp.float32)
         total = term if total is None else total + term
     out_ref[...] = total.astype(out_ref.dtype)
 
 
-def project(rows, weights, group):
+def project(rows, weights, group, slabs):
     ranks = len(weights)
     tokens, columns = rows.shape[1], weights[0].shape[1]
     return pl.pallas_call(
-        functools.partial(project_kernel, group, ranks),
+        functools.partial(project_kernel, group, ranks, slabs),
         out_shape=jax.ShapeDtypeStruct((tokens, columns), rows.dtype),
         in_specs=[VMEM] * (1 + ranks),
         out_specs=VMEM,
@@ -267,6 +299,10 @@
     return group, units, min(units - 1, (RADIUS + group - 1) // group)
 
 
+def folds(units, furthest):
+    return units == 4 and furthest == units - 1
+
+
 def edges(units, k, parity):
     sends = []
     for low in range(parity, units - 1, 2):
@@ -305,33 +341,62 @@
         bit //= 2
     weights = [weights[o] for o in range(ranks)]
 
-    held, arrived = [chunks, chunks], []
-    for k in range(1, furthest + 1):
-        held = [
-            [along(c, edges(units, k, parity)) for c in source]
-            for parity, source in enumerate(reversed(held))
-            if edges(units, k, parity)
+    own = ("own", 0, 0)
+    fold = folds(units, furthest)
+    if fold:
+        outer = [(0, 1), (3, 2)]
+        inner = [(1, 2), (2, 1)]
+        near = [along(c, inner) for c in chunks]
+        behind = [along(c, outer) for c in chunks]
+        theirs = [along(q, outer) for q in query_rows]
+        distant = [along(c, inner) for c in behind]
+        queries = tuple(("fold", n, 0) for n in (0, -1))
+        rows = query_rows + theirs
+        calls = [
+            ([(0, chunks)], [(0, 0, 0, True)]),
+            ([(1, near)], [(0, 0, 1, False)]),
+            (
+                [(-1, behind), (0, chunks), (1, near)],
+                [(1, 0, 0, True), (1, 1, 1, False), (0, 0, 1, False), (1, 2, 2, False)],
+            ),
+            ([(2, distant)], [(1, 0, 3, False), (0, 0, 2, False)]),
         ]
-        arrived.append(held)
-
-    cfg = (group, heads, ((0, 0),), units, True, False)
-    state = attend(cfg, bands, query_rows, [chunks], [])
-    for k, received in enumerate(arrived, 1):
-        shifts = tuple((k, parity) for parity in range(2) if edges(units, k, parity))
-        cfg = (group, heads, shifts, units, False, k == furthest)
-        state = attend(cfg, bands, query_rows, received, state)
+        state = []
+        for index, (held, jobs) in enumerate(calls):
+            keys = tuple(("fold", n, 0) for n, _ in held)
+            used = {q for q, _, _, _ in jobs}
+            given = rows if 1 in used else query_rows + query_rows
+            cfg = (group, heads, units, queries, keys, tuple(jobs), index == 0, index == len(calls) - 1)
+            state = attend(cfg, bands, given, [c for _, c in held], state)
+    else:
+        held, arrived = [chunks, chunks], []
+        for k in range(1, furthest + 1):
+            held = [
+                [along(c, edges(units, k, parity)) for c in source]
+                for parity, source in enumerate(reversed(held))
+                if edges(units, k, parity)
+            ]
+            arrived.append(held)
+        cfg = (group, heads, units, (own,), (own,), ((0, 0, 0, True),), True, False)
+        state = attend(cfg, bands, query_rows, [chunks], [])
+        for k, received in enumerate(arrived, 1):
+            keys = tuple(("edge", k, parity) for parity in range(2) if edges(units, k, parity))
+            jobs = tuple((0, i, k, False) for i in range(len(keys)))
+            cfg = (group, heads, units, (own,), keys, jobs, False, k == furthest)
+            state = attend(cfg, bands, query_rows, received, state)
     attended = state[0]
 
+    slabs = 2 if fold else 1
     members = [
-        [(u * group + i) * ranks + h for i in range(group) for h in range(ranks)]
-        for u in range(units)
+        [(f * ranks + h) for f in range(u * group, (u + slabs) * group) for h in range(ranks)]
+        for u in range(0, units, slabs)
     ]
-    blocks = attended.reshape(group * ranks, tokens // ranks, heads * HEAD)
+    blocks = attended.reshape(slabs * group * ranks, tokens // ranks, heads * HEAD)
     rows = lax.all_to_all(
         blocks, ("frame", "head"), split_axis=0, concat_axis=0, tiled=True,
         axis_index_groups=members,
     )
-    return project(rows, weights, group)
+    return project(rows, weights, group, slabs)
 
 
 def solution(mesh):

time: 60.3 us -> 57.3 us (0.950)
  waiting for transfers between devices: 31.6 us -> 12.3 us
  starting transfers between devices: 19.9 us -> 38.9 us
  Pallas kernels: 7.53 us -> 3.49 us
  local copies, waits for them, and re-layouts: 0.7 us -> 2.03 us
    ppermute x10 -> x8, waiting for transfers between devices: 20.6 us -> 3.25 us  [along(): return lax.ppermute(value, 'frame', pairs)]
    all_to_all x1, starting transfers between devices: 3.41 us -> 15.2 us  [on_device(): lax.all_to_all(blocks, ('frame', 'head'), split_axis=0, concat_axis=0, ti...]
    ppermute x10 -> x8, starting transfers between devices: 11 us -> 18.5 us  [along(): return lax.ppermute(value, 'frame', pairs)]
    ppermute x1, waiting for transfers between devices: 4.89 us -> 0.01 us  [on_device(): chunks.append(lax.ppermute(pieces[2], 'frame', swap))]
    pallas_call x4, Pallas kernels: 4.91 us -> 0.89 us  [attend(): pl.pallas_call(functools.partial(attend_kernel, cfg), out_shape=outs, in_...]
    ppermute x3, waiting for transfers between devices: 0.15 us -> 2.98 us  [on_device(): weights[offset ^ bit] = lax.ppermute(weights[offset], 'head', pairs)]
    ppermute x1, starting transfers between devices: 1.56 us -> 3.03 us  [on_device(): chunks.append(lax.ppermute(pieces[2], 'frame', swap))]
    unnamed x4 -> x6, local copies, waits for them, and re-layouts: 0.7 us -> 2.03 us
  transfers between devices with their start and end apart: 16 -> 14, of which waited for: 8 -> 6; matrix products, arithmetic and copies ran while one was open for 0% -> 0% of each run, Pallas kernels for 10% -> 2%
where the time goes in v2:
time: 57.3 us; the launch traced here: 56.9 us
  starting transfers between devices  38.9 us (68%)
  waiting for transfers between devices  12.3 us (21%)
  Pallas kernels  3.49 us (6%)
  local copies, waits for them, and re-layouts  2.03 us (4%)
    ppermute x8, starting transfers between devices, along(): return lax.ppermute(value, 'frame', pairs)  18.5 us
    all_to_all x1, starting transfers between devices, on_device(): lax.all_to_all(blocks, ('frame', 'head'), split_axis=0, concat_axis=0, ti...  15.2 us
    all_to_all x1, waiting for transfers between devices, on_device(): lax.all_to_all(blocks, ('frame', 'head'), split_axis=0, concat_axis=0, ti...  6.06 us
    ppermute x8, waiting for transfers between devices, along(): return lax.ppermute(value, 'frame', pairs)  3.25 us
    ppermute x1, starting transfers between devices, on_device(): chunks.append(lax.ppermute(pieces[2], 'frame', swap))  3.03 us
    ppermute x3, waiting for transfers between devices, on_device(): weights[offset ^ bit] = lax.ppermute(weights[offset], 'head', pairs)  2.98 us
    ppermute x3, starting transfers between devices, on_device(): weights[offset ^ bit] = lax.ppermute(weights[offset], 'head', pairs)  2.16 us
    unnamed x6, local copies, waits for them, and re-layouts  2.03 us
  transfers between devices with their start and end apart: 14, of which 6 were waited for; matrix products, arithmetic and copies ran while one was open for 0% of the time, Pallas kernels for 2%

profile of v2, /device:TPU:0, one launch (start us, length us, event | category | flops | bytes accessed | tf_op | source)
XLA Modules:
  0.0 56.9 jit_solution(5478102450210554354)
XLA Ops:
  0.0 1.3 %split.1 = (bf16[512,256]{1,0:T(8,128)(2,1)S(1)}, bf16[512,128]{1,0:T(8,128)(2,1)S(1)}, bf16[512,256]{1,0:T(8,128)(2,1)S(1)}, bf16[512,128]{1,0:T(8,128)(2,1)S(1...) custom-call(bf16[512,256]{1,0:T(8,128)(2,1)} %q_ref.1, bf16[512,256]{1,0:T(8,128)(2,1)} %k_ref.1, bf16[512,256]{1,0:T(8,128)(2,1)} %v_ref.1, ...), custom_call_target="tpu_custom_call" | custom-call | tf_op jit(solution)/shard_map/split/pallas_call | solution.py:66
  1.3 3.0 %collective-permute-start.5 = (bf16[512,256]{1,0:T(8,128)(2,1)S(1)}, bf16[512,256]{1,0:T(8,128)(2,1)S(1)}, u32[]{:S(2)}, u32[]{:S(2)}) collective-permute-start(bf16[512,256]{1,0:T(8,128)(2,1)S(1)} %get-tuple-element.23), channel_id=1, source_target_pairs={{0,4},{4,0},{8,12},{12,8},{16,20},{20,16},{24,28},{28,24},{1,5},{5... | collective-permute-start | bytes 786440 | tf_op jit(solution)/shard_map/ppermute | solution.py:332
  4.3 0.1 collective-permute-start
  4.4 0.7 %collective-permute-start.8 = (bf16[512,256]{1,0:T(8,128)(2,1)S(1)}, bf16[512,256]{1,0:T(8,128)(2,1)S(1)}, u32[]{:S(2)}, u32[]{:S(2)}) collective-permute-start(bf16[512,256]{1,0:T(8,128)(2,1)S(1)} %get-tuple-element.22.refs_4_.refs_6_), channel_id=1, source_target_pairs={{8,16},{12,20},{16,8},{20,12},{9,17},{13,21},{17,9},{21,13},{10,18... | collective-permute-start | bytes 786440 | tf_op jit(solution)/shard_map/ppermute | solution.py:324
  5.1 6.8 %collective-permute-start.3 = (bf16[512,256]{1,0:T(8,128)(2,1)S(1)}, bf16[512,256]{1,0:T(8,128)(2,1)S(1)}, u32[]{:S(2)}, u32[]{:S(2)}) collective-permute-start(bf16[512,256]{1,0:T(8,128)(2,1)S(1)} %get-tuple-element.22.refs_4_.refs_6_), channel_id=1, source_target_pairs={{0,8},{4,12},{24,16},{28,20},{1,9},{5,13},{25,17},{29,21},{2,10},{... | collective-permute-start | bytes 786440 | tf_op jit(solution)/shard_map/ppermute | solution.py:324
  11.8 0.0 collective-permute-done.5.refs_5_.refs_7_
  11.9 0.7 %collective-permute-start.9 = (bf16[512,256]{1,0:T(8,128)(2,1)S(1)}, bf16[512,256]{1,0:T(8,128)(2,1)S(1)}, u32[]{:S(2)}, u32[]{:S(2)}) collective-permute-start(bf16[512,256]{1,0:T(8,128)(2,1)S(1)} %collective-permute-done.5.refs_5_.refs_7_), channel_id=1, source_target_pairs={{8,16},{12,20},{16,8},{20,12},{9,17},{13,21},{17,9},{21,13},{10,18... | collective-permute-start | bytes 786440 | tf_op jit(solution)/shard_map/ppermute | solution.py:324
  12.5 6.4 %collective-permute-start.6 = (bf16[512,256]{1,0:T(8,128)(2,1)S(1)}, bf16[512,256]{1,0:T(8,128)(2,1)S(1)}, u32[]{:S(2)}, u32[]{:S(2)}) collective-permute-start(bf16[512,256]{1,0:T(8,128)(2,1)S(1)} %collective-permute-done.5.refs_5_.refs_7_), channel_id=1, source_target_pairs={{0,8},{4,12},{24,16},{28,20},{1,9},{5,13},{25,17},{29,21},{2,10},{... | collective-permute-start | bytes 786440 | tf_op jit(solution)/shard_map/ppermute | solution.py:324
  19.0 0.0 collective-permute-done.refs_1_.refs_3_
  19.0 1.6 %collective-permute-start.11 = (bf16[256,1536]{1,0:T(8,128)(2,1)}, bf16[256,1536]{1,0:T(8,128)(2,1)S(1)}, u32[]{:S(2)}, u32[]{:S(2)}) collective-permute-start(bf16[256,1536]{1,0:T(8,128)(2,1)} %refs_0_.1), channel_id=1, source_target_pairs={{0,2},{1,3},{2,0},{3,1},{4,6},{5,7},{6,4},{7,5},{8,10},{9,11},{10,... | collective-permute-start | bytes 2359304 | tf_op jit(solution)/shard_map/ppermute | solution.py:340
  20.6 0.0 collective-permute-done.8.refs_4_.refs_8_
  20.6 1.3 %collective-permute-start.1 = (bf16[512,128]{1,0:T(8,128)(2,1)S(1)}, bf16[512,128]{1,0:T(8,128)(2,1)S(1)}, u32[]{:S(2)}, u32[]{:S(2)}) collective-permute-start(bf16[512,128]{1,0:T(8,128)(2,1)S(1)} %get-tuple-element.20.refs_0_.refs_2_), channel_id=1, source_target_pairs={{0,8},{4,12},{24,16},{28,20},{1,9},{5,13},{25,17},{29,21},{2,10},{... | collective-permute-start | bytes 393224 | tf_op jit(solution)/shard_map/ppermute | solution.py:324
  21.9 0.0 collective-permute-done.3.refs_4_
  21.9 1.3 %collective-permute-start.2 = (bf16[512,128]{1,0:T(8,128)(2,1)S(1)}, bf16[512,128]{1,0:T(8,128)(2,1)S(1)}, u32[]{:S(2)}, u32[]{:S(2)}) collective-permute-start(bf16[512,128]{1,0:T(8,128)(2,1)S(1)} %collective-permute-done.refs_1_.refs_3_), channel_id=1, source_target_pairs={{0,8},{4,12},{24,16},{28,20},{1,9},{5,13},{25,17},{29,21},{2,10},{... | collective-permute-start | bytes 393224 | tf_op jit(solution)/shard_map/ppermute | solution.py:324
  23.2 0.0 collective-permute-done.9.refs_5_.refs_9_
  23.2 0.7 %collective-permute-start.4 = (bf16[512,256]{1,0:T(8,128)(2,1)S(1)}, bf16[512,256]{1,0:T(8,128)(2,1)S(1)}, u32[]{:S(2)}, u32[]{:S(2)}) collective-permute-start(bf16[512,256]{1,0:T(8,128)(2,1)S(1)} %collective-permute-done.3.refs_4_), channel_id=1, source_target_pairs={{8,16},{12,20},{16,8},{20,12},{9,17},{13,21},{17,9},{21,13},{10,18... | collective-permute-start | bytes 786440 | tf_op jit(solution)/shard_map/ppermute | solution.py:324
  23.9 1.2 %collective-permute-done.6.refs_5_ = bf16[512,256]{1,0:T(8,128)(2,1)S(1)} collective-permute-done((bf16[512,256]{1,0:T(8,128)(2,1)S(1)}, bf16[512,256]{1,0:T(8,128)(2,1)S(1)}, u32[]{:S(2)}, u32[]{:S(2)}) %collective-permute-start.6) | collective-permute-done | bytes 262176 | tf_op jit(solution)/shard_map/ppermute | solution.py:324
  25.1 0.7 %collective-permute-start.7 = (bf16[512,256]{1,0:T(8,128)(2,1)S(1)}, bf16[512,256]{1,0:T(8,128)(2,1)S(1)}, u32[]{:S(2)}, u32[]{:S(2)}) collective-permute-start(bf16[512,256]{1,0:T(8,128)(2,1)S(1)} %collective-permute-done.6.refs_5_), channel_id=1, source_target_pairs={{8,16},{12,20},{16,8},{20,12},{9,17},{13,21},{17,9},{21,13},{10,18... | collective-permute-start | bytes 786440 | tf_op jit(solution)/shard_map/ppermute | solution.py:324
  25.8 0.7 %collective-permute-done.1.refs_2_ = bf16[512,128]{1,0:T(8,128)(2,1)S(1)} collective-permute-done((bf16[512,128]{1,0:T(8,128)(2,1)S(1)}, bf16[512,128]{1,0:T(8,128)(2,1)S(1)}, u32[]{:S(2)}, u32[]{:S(2)}) %collective-permute-start.1) | collective-permute-done | bytes 131104 | tf_op jit(solution)/shard_map/ppermute | solution.py:324
  26.5 1.4 %collective-permute-done.2.refs_3_ = bf16[512,128]{1,0:T(8,128)(2,1)S(1)} collective-permute-done((bf16[512,128]{1,0:T(8,128)(2,1)S(1)}, bf16[512,128]{1,0:T(8,128)(2,1)S(1)}, u32[]{:S(2)}, u32[]{:S(2)}) %collective-permute-start.2) | collective-permute-done | bytes 131104 | tf_op jit(solution)/shard_map/ppermute | solution.py:324
  27.9 0.0 collective-permute-done.4.refs_4_
  27.9 0.0 collective-permute-done.7.refs_5_
  27.9 0.0 copy-start
  27.9 0.8 %attend.7 = (bf16[2048,128]{1,0:T(8,128)(2,1)}, f32[1,2048,128]{2,1,0:T(8,128)S(1)}, f32[1,2048,256]{2,1,0:T(8,128)S(1)}) custom-call(s32[8,8]{1,0:T(8,128)S(4)} %get-tuple-element.18.width_ref, s32[8,4,8]{2,1,0:T(4,128)S(4)} %get-tuple-element.19.offset_ref, ...), custom_call_target="tpu_custom_call", output_to_operand_aliasing={{1}: (8, {}), {2}: (9, {})} | custom-call | flops 1073741824 | bytes 1048576 | tf_op jit(solution)/shard_map/attend/pallas_call | solution.py:251
  28.7 15.2 %all-to-all-start = ((bf16[16,128,128]{2,1,0:T(8,128)(2,1)}), bf16[16,128,128]{2,1,0:T(8,128)(2,1)S(1)}, u32[]{:S(2)}, u32[]{:S(2)}) async-start(bf16[16,128,128]{2,1,0:T(8,128)(2,1)} %bitcast.1), calls=%async_computation | async-start | bytes 1048576 | tf_op jit(solution)/shard_map/all_to_all | solution.py:395
  43.9 0.0 copy-done
  43.9 0.5 collective-permute-start.10
  44.4 0.0 collective-permute-done.11.refs_2_
  44.4 0.1 collective-permute-start.12
  44.5 1.9 %collective-permute-done.10.refs_1_ = bf16[256,1536]{1,0:T(8,128)(2,1)S(1)} collective-permute-done((bf16[256,1536]{1,0:T(8,128)(2,1)S(1)}, bf16[256,1536]{1,0:T(8,128)(2,1)S(1)}, u32[]{:S(2)}, u32[]{:S(2)}) %collective-permute-start.10) | collective-permute-done | bytes 786464 | tf_op jit(solution)/shard_map/ppermute | solution.py:340
  46.4 1.1 %collective-permute-done.12.refs_3_ = bf16[256,1536]{1,0:T(8,128)(2,1)S(1)} collective-permute-done((bf16[256,1536]{1,0:T(8,128)(2,1)S(1)}, bf16[256,1536]{1,0:T(8,128)(2,1)S(1)}, u32[]{:S(2)}, u32[]{:S(2)}) %collective-permute-start.12) | collective-permute-done | bytes 786464 | tf_op jit(solution)/shard_map/ppermute | solution.py:340
  47.5 0.0 copy-start.1
  47.5 0.9 %copy-done.1 = bf16[256,1536]{1,0:T(8,128)(2,1)} copy-done((bf16[256,1536]{1,0:T(8,128)(2,1)}, bf16[256,1536]{1,0:T(8,128)(2,1)S(1)}, u32[]{:S(2)}) %copy-start.1) | copy-done | bytes 786456
  48.4 6.1 %all-to-all-done.rows_ref = bf16[16,128,128]{2,1,0:T(8,128)(2,1)S(1)} async-done(((bf16[16,128,128]{2,1,0:T(8,128)(2,1)}), bf16[16,128,128]{2,1,0:T(8,128)(2,1)S(1)}, u32[]{:S(2)}, u32[]{:S(2)}) %all-to-all-start) | async-done | bytes 524320 | tf_op jit(solution)/shard_map/all_to_all | solution.py:395
  54.4 0.0 copy-start.2
  54.4 1.1 %copy-done.2 = bf16[256,1536]{1,0:T(8,128)(2,1)S(1)} copy-done((bf16[256,1536]{1,0:T(8,128)(2,1)S(1)}, bf16[256,1536]{1,0:T(8,128)(2,1)}, u32[]{:S(2)}) %copy-start.2) | copy-done | bytes 786456
  55.6 1.3 %project.1 = bf16[128,1536]{1,0:T(8,128)(2,1)} custom-call(bf16[16,128,128]{2,1,0:T(8,128)(2,1)S(1)} %all-to-all-done.rows_ref, bf16[256,1536]{1,0:T(8,128)(2,1)S(1)} %copy-done, bf16[256,1536]{1,0:T(8,128)(2,1)S(1)} %collective-permute-done.10.refs_1_, bf16[256,1536]{1,0:T(8,128)(2,1)S(1)} %collective-permute-done.11.refs_2_, bf16[256,1536]{1,0:T(8,128)(2,1)S(1)} %copy-done.2), custom_call_target="tpu_custom_call" | custom-call | flops 805306368 | bytes 1048576 | tf_op jit(solution)/shard_map/project/pallas_call | solution.py:282
  (3 shorter events, 0.0 us)
Async XLA Ops:
  1.3 10.6 %collective-permute-start.5 = (bf16[512,256]{1,0:T(8,128)(2,1)S(1)}, bf16[512,256]{1,0:T(8,128)(2,1)S(1)}, u32[]{:S(2)}, u32[]{:S(2)}) collective-permute-start(bf16[512,256]{1,0:T(8,128)(2,1)S(1)} %get-tuple-element.23), channel_id=1, source_target_pairs={{0,4},{4,0},{8,12},{12,8},{16,20},{20,16},{24,28},{28,24},{1,5},{5... | collective-permute-start | bytes 786440 | tf_op jit(solution)/shard_map/ppermute | solution.py:332
  4.3 14.7 %collective-permute-start = (bf16[512,128]{1,0:T(8,128)(2,1)S(1)}, bf16[512,128]{1,0:T(8,128)(2,1)S(1)}, u32[]{:S(2)}, u32[]{:S(2)}) collective-permute-start(bf16[512,128]{1,0:T(8,128)(2,1)S(1)} %get-tuple-element.21), channel_id=1, source_target_pairs={{0,4},{4,0},{8,12},{12,8},{16,20},{20,16},{24,28},{28,24},{1,5},{5... | collective-permute-start | bytes 393224 | tf_op jit(solution)/shard_map/ppermute | solution.py:333
  4.4 16.2 %collective-permute-start.8 = (bf16[512,256]{1,0:T(8,128)(2,1)S(1)}, bf16[512,256]{1,0:T(8,128)(2,1)S(1)}, u32[]{:S(2)}, u32[]{:S(2)}) collective-permute-start(bf16[512,256]{1,0:T(8,128)(2,1)S(1)} %get-tuple-element.22.refs_4_.refs_6_), channel_id=1, source_target_pairs={{8,16},{12,20},{16,8},{20,12},{9,17},{13,21},{17,9},{21,13},{10,18... | collective-permute-start | bytes 786440 | tf_op jit(solution)/shard_map/ppermute | solution.py:324
  5.1 16.8 %collective-permute-start.3 = (bf16[512,256]{1,0:T(8,128)(2,1)S(1)}, bf16[512,256]{1,0:T(8,128)(2,1)S(1)}, u32[]{:S(2)}, u32[]{:S(2)}) collective-permute-start(bf16[512,256]{1,0:T(8,128)(2,1)S(1)} %get-tuple-element.22.refs_4_.refs_6_), channel_id=1, source_target_pairs={{0,8},{4,12},{24,16},{28,20},{1,9},{5,13},{25,17},{29,21},{2,10},{... | collective-permute-start | bytes 786440 | tf_op jit(solution)/shard_map/ppermute | solution.py:324
  11.9 11.4 %collective-permute-start.9 = (bf16[512,256]{1,0:T(8,128)(2,1)S(1)}, bf16[512,256]{1,0:T(8,128)(2,1)S(1)}, u32[]{:S(2)}, u32[]{:S(2)}) collective-permute-start(bf16[512,256]{1,0:T(8,128)(2,1)S(1)} %collective-permute-done.5.refs_5_.refs_7_), channel_id=1, source_target_pairs={{8,16},{12,20},{16,8},{20,12},{9,17},{13,21},{17,9},{21,13},{10,18... | collective-permute-start | bytes 786440 | tf_op jit(solution)/shard_map/ppermute | solution.py:324
  12.5 12.5 %collective-permute-start.6 = (bf16[512,256]{1,0:T(8,128)(2,1)S(1)}, bf16[512,256]{1,0:T(8,128)(2,1)S(1)}, u32[]{:S(2)}, u32[]{:S(2)}) collective-permute-start(bf16[512,256]{1,0:T(8,128)(2,1)S(1)} %collective-permute-done.5.refs_5_.refs_7_), channel_id=1, source_target_pairs={{0,8},{4,12},{24,16},{28,20},{1,9},{5,13},{25,17},{29,21},{2,10},{... | collective-permute-start | bytes 786440 | tf_op jit(solution)/shard_map/ppermute | solution.py:324
  19.0 25.4 %collective-permute-start.11 = (bf16[256,1536]{1,0:T(8,128)(2,1)}, bf16[256,1536]{1,0:T(8,128)(2,1)S(1)}, u32[]{:S(2)}, u32[]{:S(2)}) collective-permute-start(bf16[256,1536]{1,0:T(8,128)(2,1)} %refs_0_.1), channel_id=1, source_target_pairs={{0,2},{1,3},{2,0},{3,1},{4,6},{5,7},{6,4},{7,5},{8,10},{9,11},{10,... | collective-permute-start | bytes 2359304 | tf_op jit(solution)/shard_map/ppermute | solution.py:340
  20.6 5.9 %collective-permute-start.1 = (bf16[512,128]{1,0:T(8,128)(2,1)S(1)}, bf16[512,128]{1,0:T(8,128)(2,1)S(1)}, u32[]{:S(2)}, u32[]{:S(2)}) collective-permute-start(bf16[512,128]{1,0:T(8,128)(2,1)S(1)} %get-tuple-element.20.refs_0_.refs_2_), channel_id=1, source_target_pairs={{0,8},{4,12},{24,16},{28,20},{1,9},{5,13},{25,17},{29,21},{2,10},{... | collective-permute-start | bytes 393224 | tf_op jit(solution)/shard_map/ppermute | solution.py:324
  21.9 6.0 %collective-permute-start.2 = (bf16[512,128]{1,0:T(8,128)(2,1)S(1)}, bf16[512,128]{1,0:T(8,128)(2,1)S(1)}, u32[]{:S(2)}, u32[]{:S(2)}) collective-permute-start(bf16[512,128]{1,0:T(8,128)(2,1)S(1)} %collective-permute-done.refs_1_.refs_3_), channel_id=1, source_target_pairs={{0,8},{4,12},{24,16},{28,20},{1,9},{5,13},{25,17},{29,21},{2,10},{... | collective-permute-start | bytes 393224 | tf_op jit(solution)/shard_map/ppermute | solution.py:324
  23.2 4.7 %collective-permute-start.4 = (bf16[512,256]{1,0:T(8,128)(2,1)S(1)}, bf16[512,256]{1,0:T(8,128)(2,1)S(1)}, u32[]{:S(2)}, u32[]{:S(2)}) collective-permute-start(bf16[512,256]{1,0:T(8,128)(2,1)S(1)} %collective-permute-done.3.refs_4_), channel_id=1, source_target_pairs={{8,16},{12,20},{16,8},{20,12},{9,17},{13,21},{17,9},{21,13},{10,18... | collective-permute-start | bytes 786440 | tf_op jit(solution)/shard_map/ppermute | solution.py:324
  25.1 2.8 %collective-permute-start.7 = (bf16[512,256]{1,0:T(8,128)(2,1)S(1)}, bf16[512,256]{1,0:T(8,128)(2,1)S(1)}, u32[]{:S(2)}, u32[]{:S(2)}) collective-permute-start(bf16[512,256]{1,0:T(8,128)(2,1)S(1)} %collective-permute-done.6.refs_5_), channel_id=1, source_target_pairs={{8,16},{12,20},{16,8},{20,12},{9,17},{13,21},{17,9},{21,13},{10,18... | collective-permute-start | bytes 786440 | tf_op jit(solution)/shard_map/ppermute | solution.py:324
  27.9 16.0 %copy-start = (bf16[256,1536]{1,0:T(8,128)(2,1)S(1)}, bf16[256,1536]{1,0:T(8,128)(2,1)}, u32[]{:S(2)}) copy-start(bf16[256,1536]{1,0:T(8,128)(2,1)} %refs_0_.1) | copy-start | bytes 2359300
  28.7 25.7 %all-to-all-start = ((bf16[16,128,128]{2,1,0:T(8,128)(2,1)}), bf16[16,128,128]{2,1,0:T(8,128)(2,1)S(1)}, u32[]{:S(2)}, u32[]{:S(2)}) async-start(bf16[16,128,128]{2,1,0:T(8,128)(2,1)} %bitcast.1), calls=%async_computation | async-start | bytes 1048576 | tf_op jit(solution)/shard_map/all_to_all | solution.py:395
  43.9 2.4 %collective-permute-start.10 = (bf16[256,1536]{1,0:T(8,128)(2,1)S(1)}, bf16[256,1536]{1,0:T(8,128)(2,1)S(1)}, u32[]{:S(2)}, u32[]{:S(2)}) collective-permute-start(bf16[256,1536]{1,0:T(8,128)(2,1)S(1)} %copy-done), channel_id=1, source_target_pairs={{0,1},{1,0},{2,3},{3,2},{4,5},{5,4},{6,7},{7,6},{8,9},{9,8},{10,11... | collective-permute-start | bytes 2359304 | tf_op jit(solution)/shard_map/ppermute | solution.py:340
  44.4 3.1 %collective-permute-start.12 = (bf16[256,1536]{1,0:T(8,128)(2,1)S(1)}, bf16[256,1536]{1,0:T(8,128)(2,1)S(1)}, u32[]{:S(2)}, u32[]{:S(2)}) collective-permute-start(bf16[256,1536]{1,0:T(8,128)(2,1)S(1)} %collective-permute-done.11.refs_2_), channel_id=1, source_target_pairs={{0,1},{1,0},{2,3},{3,2},{4,5},{5,4},{6,7},{7,6},{8,9},{9,8},{10,11... | collective-permute-start | bytes 2359304 | tf_op jit(solution)/shard_map/ppermute | solution.py:340
  47.5 0.9 %copy-start.1 = (bf16[256,1536]{1,0:T(8,128)(2,1)}, bf16[256,1536]{1,0:T(8,128)(2,1)S(1)}, u32[]{:S(2)}) copy-start(bf16[256,1536]{1,0:T(8,128)(2,1)S(1)} %collective-permute-done.12.refs_3_) | copy-start | bytes 2359300
  54.4 1.1 %copy-start.2 = (bf16[256,1536]{1,0:T(8,128)(2,1)S(1)}, bf16[256,1536]{1,0:T(8,128)(2,1)}, u32[]{:S(2)}) copy-start(bf16[256,1536]{1,0:T(8,128)(2,1)} %copy-done.1) | copy-start | bytes 2359300

commit v3 on v2

--- a/solution.py
+++ b/solution.py
@@ -261,14 +261,20 @@
 
 
 def project_kernel(group, ranks, slabs, rows_ref, *refs):
-    weights, out_ref = refs[:-1], refs[-1]
+    weights, (out_ref, kept, sem) = refs[: ranks], refs[ranks:]
+    copy = pltpu.make_async_copy(weights[0], kept, sem)
+    copy.start()
     me = lax.axis_index("head")
     base = 0
     if slabs > 1:
         pair = lax.axis_index("frame") // (slabs * group)
         base = (1 - pair) * group * ranks
     total = None
-    for offset, weight in enumerate(weights):
+    for offset in [*range(1, ranks), 0]:
+        weight = weights[offset]
+        if offset == 0:
+            copy.wait()
+            weight = kept
         owner = me ^ offset
         left = jnp.concatenate([rows_ref[base + i * ranks + owner] for i in range(group)], axis=1)
         term = jnp.dot(left, weight[...], preferred_element_type=jnp.float32)
@@ -282,14 +288,15 @@
     return pl.pallas_call(
         functools.partial(project_kernel, group, ranks, slabs),
         out_shape=jax.ShapeDtypeStruct((tokens, columns), rows.dtype),
-        in_specs=[VMEM] * (1 + ranks),
+        in_specs=[VMEM, HBM] + [VMEM] * (ranks - 1),
         out_specs=VMEM,
+        scratch_shapes=[pltpu.VMEM(weights[0].shape, rows.dtype), pltpu.SemaphoreType.DMA],
         compiler_params=params(),
         cost_estimate=pl.CostEstimate(
             flops=2 * rows.size * columns, bytes_accessed=1 << 20, transcendentals=0
         ),
         name="project",
-    )(in_vmem(rows), *[in_vmem(w) for w in weights])
+    )(in_vmem(rows), in_hbm(weights[0]), *[in_vmem(w) for w in weights[1:]])
 
 
 def plan(shape, columns):

time: 57.3 us -> 57.3 us (level)
  local copies, waits for them, and re-layouts: 2.03 us -> 0 us
  Pallas kernels: 3.49 us -> 4.55 us
  waiting for transfers between devices: 12.3 us -> 13.2 us
    unnamed x6 -> x0, local copies, waits for them, and re-layouts: 2.03 us -> none
    pallas_call x1, Pallas kernels: 1.32 us -> 2.42 us  [project(): pl.pallas_call(functools.partial(project_kernel, group, ranks, slabs), ou...]
    all_to_all x1, waiting for transfers between devices: 6.06 us -> 6.83 us  [on_device(): lax.all_to_all(blocks, ('frame', 'head'), split_axis=0, concat_axis=0, ti...]
  transfers between devices with their start and end apart: 14 -> 14, of which waited for: 6 -> 6; matrix products, arithmetic and copies ran while one was open for 0% -> 0% of each run, Pallas kernels for 2% -> 1%
where the time goes in v3:
time: 57.3 us; the launch traced here: 56.8 us
  starting transfers between devices  39 us (68%)
  waiting for transfers between devices  13.2 us (23%)
  Pallas kernels  4.55 us (8%)
    ppermute x8, starting transfers between devices, along(): return lax.ppermute(value, 'frame', pairs)  18.5 us
    all_to_all x1, starting transfers between devices, on_device(): lax.all_to_all(blocks, ('frame', 'head'), split_axis=0, concat_axis=0, ti...  15.2 us
    all_to_all x1, waiting for transfers between devices, on_device(): lax.all_to_all(blocks, ('frame', 'head'), split_axis=0, concat_axis=0, ti...  6.83 us
    ppermute x8, waiting for transfers between devices, along(): return lax.ppermute(value, 'frame', pairs)  3.25 us
    ppermute x3, waiting for transfers between devices, on_device(): weights[offset ^ bit] = lax.ppermute(weights[offset], 'head', pairs)  3.11 us
    ppermute x1, starting transfers between devices, on_device(): chunks.append(lax.ppermute(pieces[2], 'frame', swap))  3.03 us
    pallas_call x1, Pallas kernels, project(): pl.pallas_call(functools.partial(project_kernel, group, ranks, slabs), ou...  2.42 us
    ppermute x3, starting transfers between devices, on_device(): weights[offset ^ bit] = lax.ppermute(weights[offset], 'head', pairs)  2.16 us
  transfers between devices with their start and end apart: 14, of which 6 were waited for; matrix products, arithmetic and copies ran while one was open for 0% of the time, Pallas kernels for 1%

profile of v3, /device:TPU:0, one launch (start us, length us, event | category | flops | bytes accessed | tf_op | source)
XLA Modules:
  0.0 56.8 jit_solution(1492128312880230756)
XLA Ops:
  0.0 1.3 %split.1 = (bf16[512,256]{1,0:T(8,128)(2,1)S(1)}, bf16[512,128]{1,0:T(8,128)(2,1)S(1)}, bf16[512,256]{1,0:T(8,128)(2,1)S(1)}, bf16[512,128]{1,0:T(8,128)(2,1)S(1...) custom-call(bf16[512,256]{1,0:T(8,128)(2,1)} %q_ref.1, bf16[512,256]{1,0:T(8,128)(2,1)} %k_ref.1, bf16[512,256]{1,0:T(8,128)(2,1)} %v_ref.1, ...), custom_call_target="tpu_custom_call" | custom-call | tf_op jit(solution)/shard_map/split/pallas_call | solution.py:66
  1.3 3.0 %collective-permute-start.5 = (bf16[512,256]{1,0:T(8,128)(2,1)S(1)}, bf16[512,256]{1,0:T(8,128)(2,1)S(1)}, u32[]{:S(2)}, u32[]{:S(2)}) collective-permute-start(bf16[512,256]{1,0:T(8,128)(2,1)S(1)} %get-tuple-element.23), channel_id=1, source_target_pairs={{0,4},{4,0},{8,12},{12,8},{16,20},{20,16},{24,28},{28,24},{1,5},{5... | collective-permute-start | bytes 786440 | tf_op jit(solution)/shard_map/ppermute | solution.py:339
  4.3 0.1 collective-permute-start
  4.4 0.7 %collective-permute-start.8 = (bf16[512,256]{1,0:T(8,128)(2,1)S(1)}, bf16[512,256]{1,0:T(8,128)(2,1)S(1)}, u32[]{:S(2)}, u32[]{:S(2)}) collective-permute-start(bf16[512,256]{1,0:T(8,128)(2,1)S(1)} %get-tuple-element.22.refs_4_.refs_6_), channel_id=1, source_target_pairs={{8,16},{12,20},{16,8},{20,12},{9,17},{13,21},{17,9},{21,13},{10,18... | collective-permute-start | bytes 786440 | tf_op jit(solution)/shard_map/ppermute | solution.py:331
  5.1 6.8 %collective-permute-start.3 = (bf16[512,256]{1,0:T(8,128)(2,1)S(1)}, bf16[512,256]{1,0:T(8,128)(2,1)S(1)}, u32[]{:S(2)}, u32[]{:S(2)}) collective-permute-start(bf16[512,256]{1,0:T(8,128)(2,1)S(1)} %get-tuple-element.22.refs_4_.refs_6_), channel_id=1, source_target_pairs={{0,8},{4,12},{24,16},{28,20},{1,9},{5,13},{25,17},{29,21},{2,10},{... | collective-permute-start | bytes 786440 | tf_op jit(solution)/shard_map/ppermute | solution.py:331
  11.8 0.0 collective-permute-done.5.refs_5_.refs_7_
  11.9 0.7 %collective-permute-start.9 = (bf16[512,256]{1,0:T(8,128)(2,1)S(1)}, bf16[512,256]{1,0:T(8,128)(2,1)S(1)}, u32[]{:S(2)}, u32[]{:S(2)}) collective-permute-start(bf16[512,256]{1,0:T(8,128)(2,1)S(1)} %collective-permute-done.5.refs_5_.refs_7_), channel_id=1, source_target_pairs={{8,16},{12,20},{16,8},{20,12},{9,17},{13,21},{17,9},{21,13},{10,18... | collective-permute-start | bytes 786440 | tf_op jit(solution)/shard_map/ppermute | solution.py:331
  12.5 6.4 %collective-permute-start.6 = (bf16[512,256]{1,0:T(8,128)(2,1)S(1)}, bf16[512,256]{1,0:T(8,128)(2,1)S(1)}, u32[]{:S(2)}, u32[]{:S(2)}) collective-permute-start(bf16[512,256]{1,0:T(8,128)(2,1)S(1)} %collective-permute-done.5.refs_5_.refs_7_), channel_id=1, source_target_pairs={{0,8},{4,12},{24,16},{28,20},{1,9},{5,13},{25,17},{29,21},{2,10},{... | collective-permute-start | bytes 786440 | tf_op jit(solution)/shard_map/ppermute | solution.py:331
  19.0 0.0 collective-permute-done.refs_1_.refs_3_
  19.0 1.6 %collective-permute-start.11 = (bf16[256,1536]{1,0:T(8,128)(2,1)}, bf16[256,1536]{1,0:T(8,128)(2,1)S(1)}, u32[]{:S(2)}, u32[]{:S(2)}) collective-permute-start(bf16[256,1536]{1,0:T(8,128)(2,1)} %refs_0_.1), channel_id=1, source_target_pairs={{0,2},{1,3},{2,0},{3,1},{4,6},{5,7},{6,4},{7,5},{8,10},{9,11},{10,... | collective-permute-start | bytes 2359304 | tf_op jit(solution)/shard_map/ppermute | solution.py:347
  20.6 0.0 collective-permute-done.8.refs_4_.refs_8_
  20.6 1.3 %collective-permute-start.1 = (bf16[512,128]{1,0:T(8,128)(2,1)S(1)}, bf16[512,128]{1,0:T(8,128)(2,1)S(1)}, u32[]{:S(2)}, u32[]{:S(2)}) collective-permute-start(bf16[512,128]{1,0:T(8,128)(2,1)S(1)} %get-tuple-element.20.refs_0_.refs_2_), channel_id=1, source_target_pairs={{0,8},{4,12},{24,16},{28,20},{1,9},{5,13},{25,17},{29,21},{2,10},{... | collective-permute-start | bytes 393224 | tf_op jit(solution)/shard_map/ppermute | solution.py:331
  21.9 0.0 collective-permute-done.3.refs_4_
  21.9 1.3 %collective-permute-start.2 = (bf16[512,128]{1,0:T(8,128)(2,1)S(1)}, bf16[512,128]{1,0:T(8,128)(2,1)S(1)}, u32[]{:S(2)}, u32[]{:S(2)}) collective-permute-start(bf16[512,128]{1,0:T(8,128)(2,1)S(1)} %collective-permute-done.refs_1_.refs_3_), channel_id=1, source_target_pairs={{0,8},{4,12},{24,16},{28,20},{1,9},{5,13},{25,17},{29,21},{2,10},{... | collective-permute-start | bytes 393224 | tf_op jit(solution)/shard_map/ppermute | solution.py:331
  23.2 0.0 collective-permute-done.9.refs_5_.refs_9_
  23.2 0.7 %collective-permute-start.4 = (bf16[512,256]{1,0:T(8,128)(2,1)S(1)}, bf16[512,256]{1,0:T(8,128)(2,1)S(1)}, u32[]{:S(2)}, u32[]{:S(2)}) collective-permute-start(bf16[512,256]{1,0:T(8,128)(2,1)S(1)} %collective-permute-done.3.refs_4_), channel_id=1, source_target_pairs={{8,16},{12,20},{16,8},{20,12},{9,17},{13,21},{17,9},{21,13},{10,18... | collective-permute-start | bytes 786440 | tf_op jit(solution)/shard_map/ppermute | solution.py:331
  23.9 1.2 %collective-permute-done.6.refs_5_ = bf16[512,256]{1,0:T(8,128)(2,1)S(1)} collective-permute-done((bf16[512,256]{1,0:T(8,128)(2,1)S(1)}, bf16[512,256]{1,0:T(8,128)(2,1)S(1)}, u32[]{:S(2)}, u32[]{:S(2)}) %collective-permute-start.6) | collective-permute-done | bytes 262176 | tf_op jit(solution)/shard_map/ppermute | solution.py:331
  25.1 0.7 %collective-permute-start.7 = (bf16[512,256]{1,0:T(8,128)(2,1)S(1)}, bf16[512,256]{1,0:T(8,128)(2,1)S(1)}, u32[]{:S(2)}, u32[]{:S(2)}) collective-permute-start(bf16[512,256]{1,0:T(8,128)(2,1)S(1)} %collective-permute-done.6.refs_5_), channel_id=1, source_target_pairs={{8,16},{12,20},{16,8},{20,12},{9,17},{13,21},{17,9},{21,13},{10,18... | collective-permute-start | bytes 786440 | tf_op jit(solution)/shard_map/ppermute | solution.py:331
  25.8 0.7 %collective-permute-done.1.refs_2_ = bf16[512,128]{1,0:T(8,128)(2,1)S(1)} collective-permute-done((bf16[512,128]{1,0:T(8,128)(2,1)S(1)}, bf16[512,128]{1,0:T(8,128)(2,1)S(1)}, u32[]{:S(2)}, u32[]{:S(2)}) %collective-permute-start.1) | collective-permute-done | bytes 131104 | tf_op jit(solution)/shard_map/ppermute | solution.py:331
  26.5 1.4 %collective-permute-done.2.refs_3_ = bf16[512,128]{1,0:T(8,128)(2,1)S(1)} collective-permute-done((bf16[512,128]{1,0:T(8,128)(2,1)S(1)}, bf16[512,128]{1,0:T(8,128)(2,1)S(1)}, u32[]{:S(2)}, u32[]{:S(2)}) %collective-permute-start.2) | collective-permute-done | bytes 131104 | tf_op jit(solution)/shard_map/ppermute | solution.py:331
  27.9 0.0 collective-permute-done.4.refs_4_
  27.9 0.0 collective-permute-done.7.refs_5_
  27.9 0.8 %attend.7 = (bf16[2048,128]{1,0:T(8,128)(2,1)}, f32[1,2048,128]{2,1,0:T(8,128)S(1)}, f32[1,2048,256]{2,1,0:T(8,128)S(1)}) custom-call(s32[8,8]{1,0:T(8,128)S(4)} %get-tuple-element.18.width_ref, s32[8,4,8]{2,1,0:T(4,128)S(4)} %get-tuple-element.19.offset_ref, ...), custom_call_target="tpu_custom_call", output_to_operand_aliasing={{1}: (8, {}), {2}: (9, {})} | custom-call | flops 1073741824 | bytes 1048576 | tf_op jit(solution)/shard_map/attend/pallas_call | solution.py:251
  28.7 15.2 %all-to-all-start = ((bf16[16,128,128]{2,1,0:T(8,128)(2,1)}), bf16[16,128,128]{2,1,0:T(8,128)(2,1)S(1)}, u32[]{:S(2)}, u32[]{:S(2)}) async-start(bf16[16,128,128]{2,1,0:T(8,128)(2,1)} %bitcast.1), calls=%async_computation | async-start | bytes 1048576 | tf_op jit(solution)/shard_map/all_to_all | solution.py:402
  43.9 0.4 collective-permute-start.10
  44.3 0.0 collective-permute-done.11.refs_2_
  44.3 0.2 collective-permute-start.12
  44.5 2.0 %collective-permute-done.10.refs_1_ = bf16[256,1536]{1,0:T(8,128)(2,1)S(1)} collective-permute-done((bf16[256,1536]{1,0:T(8,128)(2,1)}, bf16[256,1536]{1,0:T(8,128)(2,1)S(1)}, u32[]{:S(2)}, u32[]{:S(2)}) %collective-permute-start.10) | collective-permute-done | bytes 786464 | tf_op jit(solution)/shard_map/ppermute | solution.py:347
  46.5 1.1 %collective-permute-done.12.refs_3_ = bf16[256,1536]{1,0:T(8,128)(2,1)S(1)} collective-permute-done((bf16[256,1536]{1,0:T(8,128)(2,1)S(1)}, bf16[256,1536]{1,0:T(8,128)(2,1)S(1)}, u32[]{:S(2)}, u32[]{:S(2)}) %collective-permute-start.12) | collective-permute-done | bytes 786464 | tf_op jit(solution)/shard_map/ppermute | solution.py:347
  47.6 6.8 %all-to-all-done.rows_ref = bf16[16,128,128]{2,1,0:T(8,128)(2,1)S(1)} async-done(((bf16[16,128,128]{2,1,0:T(8,128)(2,1)}), bf16[16,128,128]{2,1,0:T(8,128)(2,1)S(1)}, u32[]{:S(2)}, u32[]{:S(2)}) %all-to-all-start) | async-done | bytes 524320 | tf_op jit(solution)/shard_map/all_to_all | solution.py:402
  54.4 2.4 %project.1 = bf16[128,1536]{1,0:T(8,128)(2,1)} custom-call(bf16[16,128,128]{2,1,0:T(8,128)(2,1)S(1)} %all-to-all-done.rows_ref, bf16[256,1536]{1,0:T(8,128)(2,1)} %refs_0_.1, bf16[256,1536]{1,0:T(8,128)(2,1)S(1)} %collective-permute-done.10.refs_1_, bf16[256,1536]{1,0:T(8,128)(2,1)S(1)} %collective-permute-done.11.refs_2_, ...), custom_call_target="tpu_custom_call" | custom-call | flops 805306368 | bytes 1048576 | tf_op jit(solution)/shard_map/project/pallas_call | solution.py:288
  (3 shorter events, 0.0 us)
Async XLA Ops:
  1.3 10.6 %collective-permute-start.5 = (bf16[512,256]{1,0:T(8,128)(2,1)S(1)}, bf16[512,256]{1,0:T(8,128)(2,1)S(1)}, u32[]{:S(2)}, u32[]{:S(2)}) collective-permute-start(bf16[512,256]{1,0:T(8,128)(2,1)S(1)} %get-tuple-element.23), channel_id=1, source_target_pairs={{0,4},{4,0},{8,12},{12,8},{16,20},{20,16},{24,28},{28,24},{1,5},{5... | collective-permute-start | bytes 786440 | tf_op jit(solution)/shard_map/ppermute | solution.py:339
  4.3 14.7 %collective-permute-start = (bf16[512,128]{1,0:T(8,128)(2,1)S(1)}, bf16[512,128]{1,0:T(8,128)(2,1)S(1)}, u32[]{:S(2)}, u32[]{:S(2)}) collective-permute-start(bf16[512,128]{1,0:T(8,128)(2,1)S(1)} %get-tuple-element.21), channel_id=1, source_target_pairs={{0,4},{4,0},{8,12},{12,8},{16,20},{20,16},{24,28},{28,24},{1,5},{5... | collective-permute-start | bytes 393224 | tf_op jit(solution)/shard_map/ppermute | solution.py:340
  4.4 16.2 %collective-permute-start.8 = (bf16[512,256]{1,0:T(8,128)(2,1)S(1)}, bf16[512,256]{1,0:T(8,128)(2,1)S(1)}, u32[]{:S(2)}, u32[]{:S(2)}) collective-permute-start(bf16[512,256]{1,0:T(8,128)(2,1)S(1)} %get-tuple-element.22.refs_4_.refs_6_), channel_id=1, source_target_pairs={{8,16},{12,20},{16,8},{20,12},{9,17},{13,21},{17,9},{21,13},{10,18... | collective-permute-start | bytes 786440 | tf_op jit(solution)/shard_map/ppermute | solution.py:331
  5.1 16.8 %collective-permute-start.3 = (bf16[512,256]{1,0:T(8,128)(2,1)S(1)}, bf16[512,256]{1,0:T(8,128)(2,1)S(1)}, u32[]{:S(2)}, u32[]{:S(2)}) collective-permute-start(bf16[512,256]{1,0:T(8,128)(2,1)S(1)} %get-tuple-element.22.refs_4_.refs_6_), channel_id=1, source_target_pairs={{0,8},{4,12},{24,16},{28,20},{1,9},{5,13},{25,17},{29,21},{2,10},{... | collective-permute-start | bytes 786440 | tf_op jit(solution)/shard_map/ppermute | solution.py:331
  11.9 11.4 %collective-permute-start.9 = (bf16[512,256]{1,0:T(8,128)(2,1)S(1)}, bf16[512,256]{1,0:T(8,128)(2,1)S(1)}, u32[]{:S(2)}, u32[]{:S(2)}) collective-permute-start(bf16[512,256]{1,0:T(8,128)(2,1)S(1)} %collective-permute-done.5.refs_5_.refs_7_), channel_id=1, source_target_pairs={{8,16},{12,20},{16,8},{20,12},{9,17},{13,21},{17,9},{21,13},{10,18... | collective-permute-start | bytes 786440 | tf_op jit(solution)/shard_map/ppermute | solution.py:331
  12.5 12.5 %collective-permute-start.6 = (bf16[512,256]{1,0:T(8,128)(2,1)S(1)}, bf16[512,256]{1,0:T(8,128)(2,1)S(1)}, u32[]{:S(2)}, u32[]{:S(2)}) collective-permute-start(bf16[512,256]{1,0:T(8,128)(2,1)S(1)} %collective-permute-done.5.refs_5_.refs_7_), channel_id=1, source_target_pairs={{0,8},{4,12},{24,16},{28,20},{1,9},{5,13},{25,17},{29,21},{2,10},{... | collective-permute-start | bytes 786440 | tf_op jit(solution)/shard_map/ppermute | solution.py:331
  19.0 25.3 %collective-permute-start.11 = (bf16[256,1536]{1,0:T(8,128)(2,1)}, bf16[256,1536]{1,0:T(8,128)(2,1)S(1)}, u32[]{:S(2)}, u32[]{:S(2)}) collective-permute-start(bf16[256,1536]{1,0:T(8,128)(2,1)} %refs_0_.1), channel_id=1, source_target_pairs={{0,2},{1,3},{2,0},{3,1},{4,6},{5,7},{6,4},{7,5},{8,10},{9,11},{10,... | collective-permute-start | bytes 2359304 | tf_op jit(solution)/shard_map/ppermute | solution.py:347
  20.6 5.9 %collective-permute-start.1 = (bf16[512,128]{1,0:T(8,128)(2,1)S(1)}, bf16[512,128]{1,0:T(8,128)(2,1)S(1)}, u32[]{:S(2)}, u32[]{:S(2)}) collective-permute-start(bf16[512,128]{1,0:T(8,128)(2,1)S(1)} %get-tuple-element.20.refs_0_.refs_2_), channel_id=1, source_target_pairs={{0,8},{4,12},{24,16},{28,20},{1,9},{5,13},{25,17},{29,21},{2,10},{... | collective-permute-start | bytes 393224 | tf_op jit(solution)/shard_map/ppermute | solution.py:331
  21.9 6.0 %collective-permute-start.2 = (bf16[512,128]{1,0:T(8,128)(2,1)S(1)}, bf16[512,128]{1,0:T(8,128)(2,1)S(1)}, u32[]{:S(2)}, u32[]{:S(2)}) collective-permute-start(bf16[512,128]{1,0:T(8,128)(2,1)S(1)} %collective-permute-done.refs_1_.refs_3_), channel_id=1, source_target_pairs={{0,8},{4,12},{24,16},{28,20},{1,9},{5,13},{25,17},{29,21},{2,10},{... | collective-permute-start | bytes 393224 | tf_op jit(solution)/shard_map/ppermute | solution.py:331
  23.2 4.7 %collective-permute-start.4 = (bf16[512,256]{1,0:T(8,128)(2,1)S(1)}, bf16[512,256]{1,0:T(8,128)(2,1)S(1)}, u32[]{:S(2)}, u32[]{:S(2)}) collective-permute-start(bf16[512,256]{1,0:T(8,128)(2,1)S(1)} %collective-permute-done.3.refs_4_), channel_id=1, source_target_pairs={{8,16},{12,20},{16,8},{20,12},{9,17},{13,21},{17,9},{21,13},{10,18... | collective-permute-start | bytes 786440 | tf_op jit(solution)/shard_map/ppermute | solution.py:331
  25.1 2.8 %collective-permute-start.7 = (bf16[512,256]{1,0:T(8,128)(2,1)S(1)}, bf16[512,256]{1,0:T(8,128)(2,1)S(1)}, u32[]{:S(2)}, u32[]{:S(2)}) collective-permute-start(bf16[512,256]{1,0:T(8,128)(2,1)S(1)} %collective-permute-done.6.refs_5_), channel_id=1, source_target_pairs={{8,16},{12,20},{16,8},{20,12},{9,17},{13,21},{17,9},{21,13},{10,18... | collective-permute-start | bytes 786440 | tf_op jit(solution)/shard_map/ppermute | solution.py:331
  28.7 25.7 %all-to-all-start = ((bf16[16,128,128]{2,1,0:T(8,128)(2,1)}), bf16[16,128,128]{2,1,0:T(8,128)(2,1)S(1)}, u32[]{:S(2)}, u32[]{:S(2)}) async-start(bf16[16,128,128]{2,1,0:T(8,128)(2,1)} %bitcast.1), calls=%async_computation | async-start | bytes 1048576 | tf_op jit(solution)/shard_map/all_to_all | solution.py:402
  43.9 2.6 %collective-permute-start.10 = (bf16[256,1536]{1,0:T(8,128)(2,1)}, bf16[256,1536]{1,0:T(8,128)(2,1)S(1)}, u32[]{:S(2)}, u32[]{:S(2)}) collective-permute-start(bf16[256,1536]{1,0:T(8,128)(2,1)} %refs_0_.1), channel_id=1, source_target_pairs={{0,1},{1,0},{2,3},{3,2},{4,5},{5,4},{6,7},{7,6},{8,9},{9,8},{10,11... | collective-permute-start | bytes 2359304 | tf_op jit(solution)/shard_map/ppermute | solution.py:347
  44.3 3.3 %collective-permute-start.12 = (bf16[256,1536]{1,0:T(8,128)(2,1)S(1)}, bf16[256,1536]{1,0:T(8,128)(2,1)S(1)}, u32[]{:S(2)}, u32[]{:S(2)}) collective-permute-start(bf16[256,1536]{1,0:T(8,128)(2,1)S(1)} %collective-permute-done.11.refs_2_), channel_id=1, source_target_pairs={{0,1},{1,0},{2,3},{3,2},{4,5},{5,4},{6,7},{7,6},{8,9},{9,8},{10,11... | collective-permute-start | bytes 2359304 | tf_op jit(solution)/shard_map/ppermute | solution.py:347

commit v4 on v1

--- a/solution.py
+++ b/solution.py
@@ -110,7 +110,7 @@
     if not begins:
         refs = refs[2:]
     if ends:
-        out_ref, m_ref, acc_ref = refs
+        keep_ref, give_ref, m_ref, acc_ref = refs
     else:
         m_ref, acc_ref = refs
     tokens = q_refs[0].shape[0]
@@ -193,16 +193,17 @@
                 steps(step, other, chunk, False)
 
     if ends:
-        for member in range(group):
-            start = (place if member == 0 else group - 1 - place) * tokens
-            for head in range(heads):
-                for b in range(blocks):
-                    rows = slice(member * tokens + b * BLK, member * tokens + (b + 1) * BLK)
-                    both = acc_ref[head, rows, :]
-                    at = pl.ds(pl.multiple_of(start + b * BLK, BLK), BLK)
-                    out_ref[at, head * HEAD : (head + 1) * HEAD] = (
-                        both[:, :HEAD] / both[:, HEAD:]
-                    ).astype(out_ref.dtype)
+        halves, rank_rows = keep_ref.shape[0] // group, keep_ref.shape[1]
+        rank = lax.axis_index("head")
+        for head in range(heads):
+            columns = slice(head * HEAD, (head + 1) * HEAD)
+            for r in range(keep_ref.shape[0]):
+                for ref, low in ((keep_ref, 0), (give_ref, 1)):
+                    block = rank ^ (2 * (r % halves) + low)
+                    start = (r // halves) * tokens + block * rank_rows
+                    at = pl.ds(pl.multiple_of(start, rank_rows), rank_rows)
+                    both = acc_ref[head, at, :]
+                    ref[r, :, columns] = (both[:, :HEAD] / both[:, HEAD:]).astype(ref.dtype)
 
 
 def attend(cfg, bands, queries, chunks, state):
@@ -218,8 +219,10 @@
     if not begins:
         aliases = {len(inputs) - 2: 0, len(inputs) - 1: 1}
     if ends:
-        outs = [jax.ShapeDtypeStruct((rows, heads * HEAD), queries[0].dtype), m_shape, acc_shape]
-        aliases = {index: out + 1 for index, out in aliases.items()}
+        sent = group * lax.axis_size("head") // 2
+        part = pltpu.VMEM((sent, rows // (2 * sent), heads * HEAD), queries[0].dtype)
+        outs = [part, part, m_shape, acc_shape]
+        aliases = {index: out + 2 for index, out in aliases.items()}
     work = 4 * len(flat) * tokens * rows * heads * HEAD
     return pl.pallas_call(
         functools.partial(attend_kernel, cfg),
@@ -232,13 +235,33 @@
     )(*inputs)
 
 
-def project_kernel(group, ranks, rows_ref, *refs):
-    weights, out_ref = refs[:-1], refs[-1]
-    me = lax.axis_index("head")
+def pack_kernel(keep_ref, got_ref, *outs):
+    for r, out in enumerate(outs):
+        out[0] = keep_ref[r]
+        out[1] = got_ref[r]
+
+
+def pack(keep, got):
+    count, *shape = keep.shape
+    return pl.pallas_call(
+        pack_kernel,
+        out_shape=[pltpu.VMEM((2, *shape), keep.dtype)] * count,
+        in_specs=[VMEM] * 2,
+        out_specs=[VMEM] * count,
+        compiler_params=params(),
+        name="pack",
+    )(in_vmem(keep), in_vmem(got))
+
+
+def project_kernel(group, ranks, *refs):
+    rows, weights, out_ref = refs[: group * ranks // 2], refs[group * ranks // 2 : -1], refs[-1]
+    place = lax.rem(lax.axis_index("frame"), group)
     total = None
     for offset, weight in enumerate(weights):
-        owner = me ^ offset
-        left = jnp.concatenate([rows_ref[i * ranks + owner] for i in range(group)], axis=1)
+        parts = [rows[i * ranks // 2 + offset // 2][offset % 2] for i in range(group)]
+        left = jnp.concatenate(parts, axis=1)
+        if group == 2:
+            left = jnp.where(place == 0, left, jnp.concatenate(parts[::-1], axis=1))
         term = jnp.dot(left, weight[...], preferred_element_type=jnp.float32)
         total = term if total is None else total + term
     out_ref[...] = total.astype(out_ref.dtype)
@@ -246,18 +269,18 @@
 
 def project(rows, weights, group):
     ranks = len(weights)
-    tokens, columns = rows.shape[1], weights[0].shape[1]
+    tokens, columns = rows[0].shape[1], weights[0].shape[1]
     return pl.pallas_call(
         functools.partial(project_kernel, group, ranks),
-        out_shape=jax.ShapeDtypeStruct((tokens, columns), rows.dtype),
-        in_specs=[VMEM] * (1 + ranks),
+        out_shape=jax.ShapeDtypeStruct((tokens, columns), rows[0].dtype),
+        in_specs=[VMEM] * (len(rows) + ranks),
         out_specs=VMEM,
         compiler_params=params(),
         cost_estimate=pl.CostEstimate(
-            flops=2 * rows.size * columns, bytes_accessed=1 << 20, transcendentals=0
+            flops=4 * rows[0].size * len(rows) * columns, bytes_accessed=1 << 20, transcendentals=0
         ),
         name="project",
-    )(in_vmem(rows), *[in_vmem(w) for w in weights])
+    )(*[in_vmem(r) for r in rows], *[in_vmem(w) for w in weights])
 
 
 def plan(shape, columns):
@@ -279,7 +302,6 @@
 
 def on_device(queries, keys, values, band_width, band_offset, out_weight):
     frames, ranks = lax.axis_size("frame"), lax.axis_size("head")
-    tokens = queries.shape[0]
     group, units, furthest = plan({"frame": frames}, queries.shape[1])
     heads = queries.shape[1] // HEAD // group
 
@@ -320,17 +342,18 @@
         shifts = tuple((k, parity) for parity in range(2) if edges(units, k, parity))
         cfg = (group, heads, shifts, units, False, k == furthest)
         state = attend(cfg, bands, query_rows, received, state)
-    attended = state[0]
-
-    members = [
-        [(u * group + i) * ranks + h for i in range(group) for h in range(ranks)]
-        for u in range(units)
-    ]
-    blocks = attended.reshape(group * ranks, tokens // ranks, heads * HEAD)
-    rows = lax.all_to_all(
-        blocks, ("frame", "head"), split_axis=0, concat_axis=0, tiled=True,
-        axis_index_groups=members,
-    )
+    keep, give = state[:2]
+    got = lax.ppermute(give, "head", [(h, h ^ 1) for h in range(ranks)])
+    packed = pack(keep, got)
+    rows = [packed[0]]
+    for r in range(1, len(packed)):
+        over, high = r // (ranks // 2), 2 * (r % (ranks // 2))
+        pairs = [
+            (f * ranks + h, (f ^ over) * ranks + (h ^ high))
+            for f in range(frames)
+            for h in range(ranks)
+        ]
+        rows.append(lax.ppermute(packed[r], ("frame", "head"), pairs))
     return project(rows, weights, group)
 
 

time: 60.3 us -> 60.5 us (level)
  starting transfers between devices: 19.9 us -> 21.9 us
  waiting for transfers between devices: 31.6 us -> 30.6 us
  local copies, waits for them, and re-layouts: 0.7 us -> 0.01 us
    all_to_all x1 -> x0, waiting for transfers between devices: 6.03 us -> none  [on_device(): lax.all_to_all(blocks, ('frame', 'head'), split_axis=0, concat_axis=0, ti...]
    ppermute x0 -> x4, waiting for transfers between devices: none -> 5.87 us  [the longest x3 4.54 us: on_device(): rows.append(lax.ppermute(packed[r], ('frame', 'head'), pairs))]
    ppermute x0 -> x4, starting transfers between devices: none -> 3.62 us  [the longest x3 3.55 us: on_device(): rows.append(lax.ppermute(packed[r], ('frame', 'head'), pairs))]
    all_to_all x1 -> x0, starting transfers between devices: 3.41 us -> none  [on_device(): lax.all_to_all(blocks, ('frame', 'head'), split_axis=0, concat_axis=0, ti...]
    ppermute x10, waiting for transfers between devices: 20.6 us -> 17.7 us  [along(): return lax.ppermute(value, 'frame', pairs)]
    ppermute x10, starting transfers between devices: 11 us -> 13.1 us  [along(): return lax.ppermute(value, 'frame', pairs)]
    ppermute x3, waiting for transfers between devices: 0.15 us -> 1.38 us  [on_device(): weights[offset ^ bit] = lax.ppermute(weights[offset], 'head', pairs)]
    ppermute x1, waiting for transfers between devices: 0.01 us -> 0.73 us  [on_device(): query_rows.append(lax.ppermute(pieces[3], 'frame', swap))]
  transfers between devices with their start and end apart: 16 -> 19, of which waited for: 8 -> 12; matrix products, arithmetic and copies ran while one was open for 0% -> 0% of each run, Pallas kernels for 10% -> 10%
where the time goes in v4:
time: 60.5 us; the launch traced here: 60.2 us
  waiting for transfers between devices  30.6 us (51%)
  starting transfers between devices  21.9 us (36%)
  Pallas kernels  7.56 us (12%)
    ppermute x10, waiting for transfers between devices, along(): return lax.ppermute(value, 'frame', pairs)  17.7 us
    ppermute x10, starting transfers between devices, along(): return lax.ppermute(value, 'frame', pairs)  13.1 us
    pallas_call x4, Pallas kernels, attend(): pl.pallas_call(functools.partial(attend_kernel, cfg), out_shape=outs, in_...  4.92 us
    ppermute x1, waiting for transfers between devices, on_device(): chunks.append(lax.ppermute(pieces[2], 'frame', swap))  4.89 us
    ppermute x3, waiting for transfers between devices, on_device(): rows.append(lax.ppermute(packed[r], ('frame', 'head'), pairs))  4.54 us
    ppermute x3, starting transfers between devices, on_device(): rows.append(lax.ppermute(packed[r], ('frame', 'head'), pairs))  3.55 us
    ppermute x3, starting transfers between devices, on_device(): weights[offset ^ bit] = lax.ppermute(weights[offset], 'head', pairs)  3.07 us
    ppermute x1, starting transfers between devices, on_device(): chunks.append(lax.ppermute(pieces[2], 'frame', swap))  1.56 us
  transfers between devices with their start and end apart: 19, of which 12 were waited for; matrix products, arithmetic and copies ran while one was open for 0% of the time, Pallas kernels for 10%

profile of v4, /device:TPU:0, one launch (start us, length us, event | category | flops | bytes accessed | tf_op | source)
XLA Modules:
  0.0 60.2 jit_solution(6182773361274802202)
XLA Ops:
  0.0 0.0 copy-start
  0.0 3.0 %collective-permute-start.17 = (bf16[256,1536]{1,0:T(8,128)(2,1)}, bf16[256,1536]{1,0:T(8,128)(2,1)S(1)}, u32[]{:S(2)}, u32[]{:S(2)}) collective-permute-start(bf16[256,1536]{1,0:T(8,128)(2,1)} %refs_4_.1), channel_id=1, source_target_pairs={{0,2},{1,3},{2,0},{3,1},{4,6},{5,7},{6,4},{7,5},{8,10},{9,11},{10,... | collective-permute-start | bytes 2359304 | tf_op jit(solution)/shard_map/ppermute | solution.py:326
  3.0 1.3 %split.1 = (bf16[512,256]{1,0:T(8,128)(2,1)S(1)}, bf16[512,128]{1,0:T(8,128)(2,1)S(1)}, bf16[512,256]{1,0:T(8,128)(2,1)S(1)}, bf16[512,128]{1,0:T(8,128)(2,1)S(1...) custom-call(bf16[512,256]{1,0:T(8,128)(2,1)} %q_ref.1, bf16[512,256]{1,0:T(8,128)(2,1)} %k_ref.1, bf16[512,256]{1,0:T(8,128)(2,1)} %v_ref.1, ...), custom_call_target="tpu_custom_call" | custom-call | tf_op jit(solution)/shard_map/split/pallas_call | solution.py:66
  4.3 1.6 %collective-permute-start.4 = (bf16[512,256]{1,0:T(8,128)(2,1)S(1)}, bf16[512,256]{1,0:T(8,128)(2,1)S(1)}, u32[]{:S(2)}, u32[]{:S(2)}) collective-permute-start(bf16[512,256]{1,0:T(8,128)(2,1)S(1)} %get-tuple-element.28), channel_id=1, source_target_pairs={{0,4},{4,0},{8,12},{12,8},{16,20},{20,16},{24,28},{28,24},{1,5},{5... | collective-permute-start | bytes 786440 | tf_op jit(solution)/shard_map/ppermute | solution.py:318
  5.8 0.5 collective-permute-start
  6.4 1.6 %collective-permute-start.1 = (bf16[512,256]{1,0:T(8,128)(2,1)S(1)}, bf16[512,256]{1,0:T(8,128)(2,1)S(1)}, u32[]{:S(2)}, u32[]{:S(2)}) collective-permute-start(bf16[512,256]{1,0:T(8,128)(2,1)S(1)} %get-tuple-element.27.refs_2_), channel_id=1, source_target_pairs={{0,8},{4,12},{8,0},{12,4},{16,24},{20,28},{24,16},{28,20},{1,9},{5... | collective-permute-start | bytes 786440 | tf_op jit(solution)/shard_map/ppermute | solution.py:310
  8.0 0.7 %collective-permute-start.8 = (bf16[512,256]{1,0:T(8,128)(2,1)S(1)}, bf16[512,256]{1,0:T(8,128)(2,1)S(1)}, u32[]{:S(2)}, u32[]{:S(2)}) collective-permute-start(bf16[512,256]{1,0:T(8,128)(2,1)S(1)} %get-tuple-element.27.refs_2_), channel_id=1, source_target_pairs={{8,16},{12,20},{16,8},{20,12},{9,17},{13,21},{17,9},{21,13},{10,18... | collective-permute-start | bytes 786440 | tf_op jit(solution)/shard_map/ppermute | solution.py:310
  8.6 4.9 %collective-permute-done.4.refs_3_ = bf16[512,256]{1,0:T(8,128)(2,1)S(1)} collective-permute-done((bf16[512,256]{1,0:T(8,128)(2,1)S(1)}, bf16[512,256]{1,0:T(8,128)(2,1)S(1)}, u32[]{:S(2)}, u32[]{:S(2)}) %collective-permute-start.4) | collective-permute-done | bytes 262176 | tf_op jit(solution)/shard_map/ppermute | solution.py:318
  13.5 0.7 %collective-permute-start.10 = (bf16[512,256]{1,0:T(8,128)(2,1)S(1)}, bf16[512,256]{1,0:T(8,128)(2,1)S(1)}, u32[]{:S(2)}, u32[]{:S(2)}) collective-permute-start(bf16[512,256]{1,0:T(8,128)(2,1)S(1)} %collective-permute-done.4.refs_3_), channel_id=1, source_target_pairs={{8,16},{12,20},{16,8},{20,12},{9,17},{13,21},{17,9},{21,13},{10,18... | collective-permute-start | bytes 786440 | tf_op jit(solution)/shard_map/ppermute | solution.py:310
  14.2 0.7 %collective-permute-done.refs_1_ = bf16[512,128]{1,0:T(8,128)(2,1)S(1)} collective-permute-done((bf16[512,128]{1,0:T(8,128)(2,1)S(1)}, bf16[512,128]{1,0:T(8,128)(2,1)S(1)}, u32[]{:S(2)}, u32[]{:S(2)}) %collective-permute-start) | collective-permute-done | bytes 131104 | tf_op jit(solution)/shard_map/ppermute | solution.py:319
  14.9 3.7 %collective-permute-start.5 = (bf16[512,256]{1,0:T(8,128)(2,1)S(1)}, bf16[512,256]{1,0:T(8,128)(2,1)S(1)}, u32[]{:S(2)}, u32[]{:S(2)}) collective-permute-start(bf16[512,256]{1,0:T(8,128)(2,1)S(1)} %collective-permute-done.4.refs_3_), channel_id=1, source_target_pairs={{0,8},{4,12},{8,0},{12,4},{16,24},{20,28},{24,16},{28,20},{1,9},{5... | collective-permute-start | bytes 786440 | tf_op jit(solution)/shard_map/ppermute | solution.py:310
  18.7 0.0 collective-permute-done.1.refs_2_
  18.7 0.7 %collective-permute-start.2 = (bf16[512,256]{1,0:T(8,128)(2,1)S(1)}, bf16[512,256]{1,0:T(8,128)(2,1)S(1)}, u32[]{:S(2)}, u32[]{:S(2)}) collective-permute-start(bf16[512,256]{1,0:T(8,128)(2,1)S(1)} %collective-permute-done.1.refs_2_), channel_id=1, source_target_pairs={{8,16},{12,20},{16,8},{20,12},{9,17},{13,21},{17,9},{21,13},{10,18... | collective-permute-start | bytes 786440 | tf_op jit(solution)/shard_map/ppermute | solution.py:310
  19.3 0.0 collective-permute-done.8.refs_4_
  19.4 0.0 copy-done
  19.4 0.1 collective-permute-start.16
  19.4 1.4 %collective-permute-done.17.refs_6_ = bf16[256,1536]{1,0:T(8,128)(2,1)S(1)} collective-permute-done((bf16[256,1536]{1,0:T(8,128)(2,1)}, bf16[256,1536]{1,0:T(8,128)(2,1)S(1)}, u32[]{:S(2)}, u32[]{:S(2)}) %collective-permute-start.17) | collective-permute-done | bytes 786464 | tf_op jit(solution)/shard_map/ppermute | solution.py:326
  20.8 0.0 collective-permute-start.18
  20.8 0.0 collective-permute-done.10.refs_5_
  20.8 1.3 %collective-permute-start.9 = (bf16[512,256]{1,0:T(8,128)(2,1)S(1)}, bf16[512,256]{1,0:T(8,128)(2,1)S(1)}, u32[]{:S(2)}, u32[]{:S(2)}) collective-permute-start(bf16[512,256]{1,0:T(8,128)(2,1)S(1)} %collective-permute-done.8.refs_4_), channel_id=1, source_target_pairs={{8,0},{12,4},{16,24},{20,28},{9,1},{13,5},{17,25},{21,29},{10,2},{... | collective-permute-start | bytes 786440 | tf_op jit(solution)/shard_map/ppermute | solution.py:310
  22.1 0.9 %collective-permute-done.5.refs_3_ = bf16[512,256]{1,0:T(8,128)(2,1)S(1)} collective-permute-done((bf16[512,256]{1,0:T(8,128)(2,1)S(1)}, bf16[512,256]{1,0:T(8,128)(2,1)S(1)}, u32[]{:S(2)}, u32[]{:S(2)}) %collective-permute-start.5) | collective-permute-done | bytes 262176 | tf_op jit(solution)/shard_map/ppermute | solution.py:310
  23.0 0.7 %collective-permute-start.6 = (bf16[512,256]{1,0:T(8,128)(2,1)S(1)}, bf16[512,256]{1,0:T(8,128)(2,1)S(1)}, u32[]{:S(2)}, u32[]{:S(2)}) collective-permute-start(bf16[512,256]{1,0:T(8,128)(2,1)S(1)} %collective-permute-done.5.refs_3_), channel_id=1, source_target_pairs={{8,16},{12,20},{16,8},{20,12},{9,17},{13,21},{17,9},{21,13},{10,18... | collective-permute-start | bytes 786440 | tf_op jit(solution)/shard_map/ppermute | solution.py:310
  23.7 0.0 collective-permute-done.2.refs_4_
  23.7 1.3 %collective-permute-start.11 = (bf16[512,256]{1,0:T(8,128)(2,1)S(1)}, bf16[512,256]{1,0:T(8,128)(2,1)S(1)}, u32[]{:S(2)}, u32[]{:S(2)}) collective-permute-start(bf16[512,256]{1,0:T(8,128)(2,1)S(1)} %collective-permute-done.10.refs_5_), channel_id=1, source_target_pairs={{8,0},{12,4},{16,24},{20,28},{9,1},{13,5},{17,25},{21,29},{10,2},{... | collective-permute-start | bytes 786440 | tf_op jit(solution)/shard_map/ppermute | solution.py:310
  25.0 6.9 %collective-permute-done.9.refs_2_ = bf16[512,256]{1,0:T(8,128)(2,1)S(1)} collective-permute-done((bf16[512,256]{1,0:T(8,128)(2,1)S(1)}, bf16[512,256]{1,0:T(8,128)(2,1)S(1)}, u32[]{:S(2)}, u32[]{:S(2)}) %collective-permute-start.9) | collective-permute-done | bytes 262176 | tf_op jit(solution)/shard_map/ppermute | solution.py:310
  31.9 1.3 %collective-permute-start.3 = (bf16[512,256]{1,0:T(8,128)(2,1)S(1)}, bf16[512,256]{1,0:T(8,128)(2,1)S(1)}, u32[]{:S(2)}, u32[]{:S(2)}) collective-permute-start(bf16[512,256]{1,0:T(8,128)(2,1)S(1)} %collective-permute-done.2.refs_4_), channel_id=1, source_target_pairs={{8,0},{12,4},{16,24},{20,28},{9,1},{13,5},{17,25},{21,29},{10,2},{... | collective-permute-start | bytes 786440 | tf_op jit(solution)/shard_map/ppermute | solution.py:310
  33.2 0.0 collective-permute-done.6.refs_5_
  33.2 1.3 %collective-permute-start.7 = (bf16[512,256]{1,0:T(8,128)(2,1)S(1)}, bf16[512,256]{1,0:T(8,128)(2,1)S(1)}, u32[]{:S(2)}, u32[]{:S(2)}) collective-permute-start(bf16[512,256]{1,0:T(8,128)(2,1)S(1)} %collective-permute-done.6.refs_5_), channel_id=1, source_target_pairs={{8,0},{12,4},{16,24},{20,28},{9,1},{13,5},{17,25},{21,29},{10,2},{... | collective-permute-start | bytes 786440 | tf_op jit(solution)/shard_map/ppermute | solution.py:310
  34.5 1.5 %shard_map.64 = (f32[1,1024,128]{2,1,0:T(8,128)S(1)}, f32[1,1024,256]{2,1,0:T(8,128)S(1)}) custom-call(s32[8,8]{1,0:T(8,128)S(4)} %get-tuple-element.23.width_ref, s32[8,4,8]{2,1,0:T(4,128)S(4)} %get-tuple-element.24.offset_ref, bf16[512,128]{1,0:T(8,128)(2,1)S(1)} %get-tuple-element.25.refs_0_, bf16[512,128]{1,0:T(8,128)(2,1)S(1)} %collective-permute-done.refs_1_, ...), custom_call_target="tpu_custom_call" | custom-call | flops 536870912 | bytes 1048576 | tf_op jit(solution)/shard_map/pallas_call | solution.py:227
  36.1 1.7 %shard_map.65 = (f32[1,1024,128]{2,1,0:T(8,128)S(1)}, f32[1,1024,256]{2,1,0:T(8,128)S(1)}) custom-call(s32[8,8]{1,0:T(8,128)S(4)} %get-tuple-element.23.width_ref, s32[8,4,8]{2,1,0:T(4,128)S(4)} %get-tuple-element.24.offset_ref, bf16[512,128]{1,0:T(8,128)(2,1)S(1)} %get-tuple-element.25.refs_0_, ...), custom_call_target="tpu_custom_call", output_to_operand_aliasing={{0}: (8, {}), {1}: (9, {})} | custom-call | flops 1073741824 | bytes 1048576 | tf_op jit(solution)/shard_map/pallas_call | solution.py:227
  37.8 1.7 %collective-permute-done.11.refs_3_ = bf16[512,256]{1,0:T(8,128)(2,1)S(1)} collective-permute-done((bf16[512,256]{1,0:T(8,128)(2,1)S(1)}, bf16[512,256]{1,0:T(8,128)(2,1)S(1)}, u32[]{:S(2)}, u32[]{:S(2)}) %collective-permute-start.11) | collective-permute-done | bytes 262176 | tf_op jit(solution)/shard_map/ppermute | solution.py:310
  39.4 1.0 %shard_map.66 = (f32[1,1024,128]{2,1,0:T(8,128)S(1)}, f32[1,1024,256]{2,1,0:T(8,128)S(1)}) custom-call(s32[8,8]{1,0:T(8,128)S(4)} %get-tuple-element.23.width_ref, s32[8,4,8]{2,1,0:T(4,128)S(4)} %get-tuple-element.24.offset_ref, bf16[512,128]{1,0:T(8,128)(2,1)S(1)} %get-tuple-element.25.refs_0_, ...), custom_call_target="tpu_custom_call", output_to_operand_aliasing={{0}: (8, {}), {1}: (9, {})} | custom-call | flops 1073741824 | bytes 1048576 | tf_op jit(solution)/shard_map/pallas_call | solution.py:227
  40.4 4.6 %collective-permute-done.3.refs_2_ = bf16[512,256]{1,0:T(8,128)(2,1)S(1)} collective-permute-done((bf16[512,256]{1,0:T(8,128)(2,1)S(1)}, bf16[512,256]{1,0:T(8,128)(2,1)S(1)}, u32[]{:S(2)}, u32[]{:S(2)}) %collective-permute-start.3) | collective-permute-done | bytes 262176 | tf_op jit(solution)/shard_map/ppermute | solution.py:310
  45.0 3.6 %collective-permute-done.7.refs_3_ = bf16[512,256]{1,0:T(8,128)(2,1)S(1)} collective-permute-done((bf16[512,256]{1,0:T(8,128)(2,1)S(1)}, bf16[512,256]{1,0:T(8,128)(2,1)S(1)}, u32[]{:S(2)}, u32[]{:S(2)}) %collective-permute-start.7) | collective-permute-done | bytes 262176 | tf_op jit(solution)/shard_map/ppermute | solution.py:310
  48.6 0.7 %shard_map.67 = (bf16[4,128,128]{2,1,0:T(8,128)(2,1)S(1)}, bf16[4,128,128]{2,1,0:T(8,128)(2,1)S(1)}, f32[1,1024,128]{2,1,0:T(8,128)S(1)}, f32[1,1024,256]{2,1,0:T(8,128)S(1)}) custom-call(s32[8,8]{1,0:T(8,128)S(4)} %get-tuple-element.23.width_ref, s32[8,4,8]{2,1,0:T(4,128)S(4)} %get-tuple-element.24.offset_ref, ...), custom_call_target="tpu_custom_call", output_to_operand_aliasing={{2}: (6, {}), {3}: (7, {})} | custom-call | flops 536870912 | bytes 1048576 | tf_op jit(solution)/shard_map/pallas_call | solution.py:227
  49.4 0.1 collective-permute-start.12
  49.4 1.3 %collective-permute-done.12.got_ref = bf16[4,128,128]{2,1,0:T(8,128)(2,1)S(1)} collective-permute-done((bf16[4,128,128]{2,1,0:T(8,128)(2,1)S(1)}, bf16[4,128,128]{2,1,0:T(8,128)(2,1)S(1)}, u32[]{:S(2)}, u32[]{:S(2)}) %collective-permute-start.12) | collective-permute-done | bytes 131104 | tf_op jit(solution)/shard_map/ppermute | solution.py:346
  50.8 1.4 %collective-permute-start.13 = (bf16[2,128,128]{2,1,0:T(8,128)(2,1)S(1)}, bf16[2,128,128]{2,1,0:T(8,128)(2,1)S(1)}, u32[]{:S(2)}, u32[]{:S(2)}) collective-permute-start(bf16[2,128,128]{2,1,0:T(8,128)(2,1)S(1)} %get-tuple-element.38), channel_id=1, source_target_pairs={{0,2},{1,3},{2,0},{3,1},{4,6},{5,7},{6,4},{7,5},{8,10},{9,11},{10,... | collective-permute-start | bytes 196616 | tf_op jit(solution)/shard_map/ppermute | solution.py:356
  52.2 1.5 %collective-permute-start.14 = (bf16[2,128,128]{2,1,0:T(8,128)(2,1)S(1)}, bf16[2,128,128]{2,1,0:T(8,128)(2,1)S(1)}, u32[]{:S(2)}, u32[]{:S(2)}) collective-permute-start(bf16[2,128,128]{2,1,0:T(8,128)(2,1)S(1)} %get-tuple-element.39), channel_id=1, source_target_pairs={{0,4},{1,5},{2,6},{3,7},{4,0},{5,1},{6,2},{7,3},{8,12},{9,13},{10,... | collective-permute-start | bytes 196616 | tf_op jit(solution)/shard_map/ppermute | solution.py:356
  53.7 0.6 %collective-permute-start.15 = (bf16[2,128,128]{2,1,0:T(8,128)(2,1)S(1)}, bf16[2,128,128]{2,1,0:T(8,128)(2,1)S(1)}, u32[]{:S(2)}, u32[]{:S(2)}) collective-permute-start(bf16[2,128,128]{2,1,0:T(8,128)(2,1)S(1)} %get-tuple-element.40), channel_id=1, source_target_pairs={{0,6},{1,7},{2,4},{3,5},{4,2},{5,3},{6,0},{7,1},{8,14},{9,15},{10,... | collective-permute-start | bytes 196616 | tf_op jit(solution)/shard_map/ppermute | solution.py:356
  54.3 0.0 collective-permute-done.16.refs_5_
  54.4 0.8 %collective-permute-done.13.refs_1_ = bf16[2,128,128]{2,1,0:T(8,128)(2,1)S(1)} collective-permute-done((bf16[2,128,128]{2,1,0:T(8,128)(2,1)S(1)}, bf16[2,128,128]{2,1,0:T(8,128)(2,1)S(1)}, u32[]{:S(2)}, u32[]{:S(2)}) %collective-permute-start.13) | collective-permute-done | bytes 65568 | tf_op jit(solution)/shard_map/ppermute | solution.py:356
  55.1 1.9 %collective-permute-done.14.refs_2_ = bf16[2,128,128]{2,1,0:T(8,128)(2,1)S(1)} collective-permute-done((bf16[2,128,128]{2,1,0:T(8,128)(2,1)S(1)}, bf16[2,128,128]{2,1,0:T(8,128)(2,1)S(1)}, u32[]{:S(2)}, u32[]{:S(2)}) %collective-permute-start.14) | collective-permute-done | bytes 65568 | tf_op jit(solution)/shard_map/ppermute | solution.py:356
  57.0 1.9 %collective-permute-done.15.refs_3_ = bf16[2,128,128]{2,1,0:T(8,128)(2,1)S(1)} collective-permute-done((bf16[2,128,128]{2,1,0:T(8,128)(2,1)S(1)}, bf16[2,128,128]{2,1,0:T(8,128)(2,1)S(1)}, u32[]{:S(2)}, u32[]{:S(2)}) %collective-permute-start.15) | collective-permute-done | bytes 65568 | tf_op jit(solution)/shard_map/ppermute | solution.py:356
  58.9 0.0 collective-permute-done.18.refs_7_
  58.9 1.3 %project.1 = bf16[128,1536]{1,0:T(8,128)(2,1)} custom-call(bf16[2,128,128]{2,1,0:T(8,128)(2,1)S(1)} %get-tuple-element.37.refs_0_, bf16[2,128,128]{2,1,0:T(8,128)(2,1)S(1)} %collective-permute-done.13.refs_1_, bf16[2,128,128]{2,1,0:T(8,128)(2,1)S(1)} %collective-permute-done.14.refs_2_, bf16[2,128,128]{2,1,0:T(8,128)(2,1)S(1)} %collective-permute-done.15.refs_3_, ...), custom_call_target="tpu_custom_call" | custom-call | flops 805306368 | bytes 1048576 | tf_op jit(solution)/shard_map/project/pallas_call | solution.py:273
  (1 shorter events, 0.0 us)
Async XLA Ops:
  0.0 19.4 %copy-start = (bf16[256,1536]{1,0:T(8,128)(2,1)S(1)}, bf16[256,1536]{1,0:T(8,128)(2,1)}, u32[]{:S(2)}) copy-start(bf16[256,1536]{1,0:T(8,128)(2,1)} %refs_4_.1) | copy-start | bytes 2359300
  0.0 20.8 %collective-permute-start.17 = (bf16[256,1536]{1,0:T(8,128)(2,1)}, bf16[256,1536]{1,0:T(8,128)(2,1)S(1)}, u32[]{:S(2)}, u32[]{:S(2)}) collective-permute-start(bf16[256,1536]{1,0:T(8,128)(2,1)} %refs_4_.1), channel_id=1, source_target_pairs={{0,2},{1,3},{2,0},{3,1},{4,6},{5,7},{6,4},{7,5},{8,10},{9,11},{10,... | collective-permute-start | bytes 2359304 | tf_op jit(solution)/shard_map/ppermute | solution.py:326
  4.3 9.2 %collective-permute-start.4 = (bf16[512,256]{1,0:T(8,128)(2,1)S(1)}, bf16[512,256]{1,0:T(8,128)(2,1)S(1)}, u32[]{:S(2)}, u32[]{:S(2)}) collective-permute-start(bf16[512,256]{1,0:T(8,128)(2,1)S(1)} %get-tuple-element.28), channel_id=1, source_target_pairs={{0,4},{4,0},{8,12},{12,8},{16,20},{20,16},{24,28},{28,24},{1,5},{5... | collective-permute-start | bytes 786440 | tf_op jit(solution)/shard_map/ppermute | solution.py:318
  5.8 9.1 %collective-permute-start = (bf16[512,128]{1,0:T(8,128)(2,1)S(1)}, bf16[512,128]{1,0:T(8,128)(2,1)S(1)}, u32[]{:S(2)}, u32[]{:S(2)}) collective-permute-start(bf16[512,128]{1,0:T(8,128)(2,1)S(1)} %get-tuple-element.26), channel_id=1, source_target_pairs={{0,4},{4,0},{8,12},{12,8},{16,20},{20,16},{24,28},{28,24},{1,5},{5... | collective-permute-start | bytes 393224 | tf_op jit(solution)/shard_map/ppermute | solution.py:319
  6.4 12.3 %collective-permute-start.1 = (bf16[512,256]{1,0:T(8,128)(2,1)S(1)}, bf16[512,256]{1,0:T(8,128)(2,1)S(1)}, u32[]{:S(2)}, u32[]{:S(2)}) collective-permute-start(bf16[512,256]{1,0:T(8,128)(2,1)S(1)} %get-tuple-element.27.refs_2_), channel_id=1, source_target_pairs={{0,8},{4,12},{8,0},{12,4},{16,24},{20,28},{24,16},{28,20},{1,9},{5... | collective-permute-start | bytes 786440 | tf_op jit(solution)/shard_map/ppermute | solution.py:310
  8.0 11.4 %collective-permute-start.8 = (bf16[512,256]{1,0:T(8,128)(2,1)S(1)}, bf16[512,256]{1,0:T(8,128)(2,1)S(1)}, u32[]{:S(2)}, u32[]{:S(2)}) collective-permute-start(bf16[512,256]{1,0:T(8,128)(2,1)S(1)} %get-tuple-element.27.refs_2_), channel_id=1, source_target_pairs={{8,16},{12,20},{16,8},{20,12},{9,17},{13,21},{17,9},{21,13},{10,18... | collective-permute-start | bytes 786440 | tf_op jit(solution)/shard_map/ppermute | solution.py:310
  13.5 7.3 %collective-permute-start.10 = (bf16[512,256]{1,0:T(8,128)(2,1)S(1)}, bf16[512,256]{1,0:T(8,128)(2,1)S(1)}, u32[]{:S(2)}, u32[]{:S(2)}) collective-permute-start(bf16[512,256]{1,0:T(8,128)(2,1)S(1)} %collective-permute-done.4.refs_3_), channel_id=1, source_target_pairs={{8,16},{12,20},{16,8},{20,12},{9,17},{13,21},{17,9},{21,13},{10,18... | collective-permute-start | bytes 786440 | tf_op jit(solution)/shard_map/ppermute | solution.py:310
  14.9 8.1 %collective-permute-start.5 = (bf16[512,256]{1,0:T(8,128)(2,1)S(1)}, bf16[512,256]{1,0:T(8,128)(2,1)S(1)}, u32[]{:S(2)}, u32[]{:S(2)}) collective-permute-start(bf16[512,256]{1,0:T(8,128)(2,1)S(1)} %collective-permute-done.4.refs_3_), channel_id=1, source_target_pairs={{0,8},{4,12},{8,0},{12,4},{16,24},{20,28},{24,16},{28,20},{1,9},{5... | collective-permute-start | bytes 786440 | tf_op jit(solution)/shard_map/ppermute | solution.py:310
  18.7 5.0 %collective-permute-start.2 = (bf16[512,256]{1,0:T(8,128)(2,1)S(1)}, bf16[512,256]{1,0:T(8,128)(2,1)S(1)}, u32[]{:S(2)}, u32[]{:S(2)}) collective-permute-start(bf16[512,256]{1,0:T(8,128)(2,1)S(1)} %collective-permute-done.1.refs_2_), channel_id=1, source_target_pairs={{8,16},{12,20},{16,8},{20,12},{9,17},{13,21},{17,9},{21,13},{10,18... | collective-permute-start | bytes 786440 | tf_op jit(solution)/shard_map/ppermute | solution.py:310
  19.4 35.0 %collective-permute-start.16 = (bf16[256,1536]{1,0:T(8,128)(2,1)S(1)}, bf16[256,1536]{1,0:T(8,128)(2,1)S(1)}, u32[]{:S(2)}, u32[]{:S(2)}) collective-permute-start(bf16[256,1536]{1,0:T(8,128)(2,1)S(1)} %copy-done), channel_id=1, source_target_pairs={{0,1},{1,0},{2,3},{3,2},{4,5},{5,4},{6,7},{7,6},{8,9},{9,8},{10,11... | collective-permute-start | bytes 2359304 | tf_op jit(solution)/shard_map/ppermute | solution.py:326
  20.8 38.1 %collective-permute-start.18 = (bf16[256,1536]{1,0:T(8,128)(2,1)S(1)}, bf16[256,1536]{1,0:T(8,128)(2,1)S(1)}, u32[]{:S(2)}, u32[]{:S(2)}) collective-permute-start(bf16[256,1536]{1,0:T(8,128)(2,1)S(1)} %collective-permute-done.17.refs_6_), channel_id=1, source_target_pairs={{0,1},{1,0},{2,3},{3,2},{4,5},{5,4},{6,7},{7,6},{8,9},{9,8},{10,11... | collective-permute-start | bytes 2359304 | tf_op jit(solution)/shard_map/ppermute | solution.py:326
  20.8 11.1 %collective-permute-start.9 = (bf16[512,256]{1,0:T(8,128)(2,1)S(1)}, bf16[512,256]{1,0:T(8,128)(2,1)S(1)}, u32[]{:S(2)}, u32[]{:S(2)}) collective-permute-start(bf16[512,256]{1,0:T(8,128)(2,1)S(1)} %collective-permute-done.8.refs_4_), channel_id=1, source_target_pairs={{8,0},{12,4},{16,24},{20,28},{9,1},{13,5},{17,25},{21,29},{10,2},{... | collective-permute-start | bytes 786440 | tf_op jit(solution)/shard_map/ppermute | solution.py:310
  23.0 10.2 %collective-permute-start.6 = (bf16[512,256]{1,0:T(8,128)(2,1)S(1)}, bf16[512,256]{1,0:T(8,128)(2,1)S(1)}, u32[]{:S(2)}, u32[]{:S(2)}) collective-permute-start(bf16[512,256]{1,0:T(8,128)(2,1)S(1)} %collective-permute-done.5.refs_3_), channel_id=1, source_target_pairs={{8,16},{12,20},{16,8},{20,12},{9,17},{13,21},{17,9},{21,13},{10,18... | collective-permute-start | bytes 786440 | tf_op jit(solution)/shard_map/ppermute | solution.py:310
  23.7 15.7 %collective-permute-start.11 = (bf16[512,256]{1,0:T(8,128)(2,1)S(1)}, bf16[512,256]{1,0:T(8,128)(2,1)S(1)}, u32[]{:S(2)}, u32[]{:S(2)}) collective-permute-start(bf16[512,256]{1,0:T(8,128)(2,1)S(1)} %collective-permute-done.10.refs_5_), channel_id=1, source_target_pairs={{8,0},{12,4},{16,24},{20,28},{9,1},{13,5},{17,25},{21,29},{10,2},{... | collective-permute-start | bytes 786440 | tf_op jit(solution)/shard_map/ppermute | solution.py:310
  31.9 13.1 %collective-permute-start.3 = (bf16[512,256]{1,0:T(8,128)(2,1)S(1)}, bf16[512,256]{1,0:T(8,128)(2,1)S(1)}, u32[]{:S(2)}, u32[]{:S(2)}) collective-permute-start(bf16[512,256]{1,0:T(8,128)(2,1)S(1)} %collective-permute-done.2.refs_4_), channel_id=1, source_target_pairs={{8,0},{12,4},{16,24},{20,28},{9,1},{13,5},{17,25},{21,29},{10,2},{... | collective-permute-start | bytes 786440 | tf_op jit(solution)/shard_map/ppermute | solution.py:310
  33.2 15.4 %collective-permute-start.7 = (bf16[512,256]{1,0:T(8,128)(2,1)S(1)}, bf16[512,256]{1,0:T(8,128)(2,1)S(1)}, u32[]{:S(2)}, u32[]{:S(2)}) collective-permute-start(bf16[512,256]{1,0:T(8,128)(2,1)S(1)} %collective-permute-done.6.refs_5_), channel_id=1, source_target_pairs={{8,0},{12,4},{16,24},{20,28},{9,1},{13,5},{17,25},{21,29},{10,2},{... | collective-permute-start | bytes 786440 | tf_op jit(solution)/shard_map/ppermute | solution.py:310
  49.4 1.4 %collective-permute-start.12 = (bf16[4,128,128]{2,1,0:T(8,128)(2,1)S(1)}, bf16[4,128,128]{2,1,0:T(8,128)(2,1)S(1)}, u32[]{:S(2)}, u32[]{:S(2)}) collective-permute-start(bf16[4,128,128]{2,1,0:T(8,128)(2,1)S(1)} %get-tuple-element.36), channel_id=1, source_target_pairs={{0,1},{1,0},{2,3},{3,2},{4,5},{5,4},{6,7},{7,6},{8,9},{9,8},{10,11... | collective-permute-start | bytes 393224 | tf_op jit(solution)/shard_map/ppermute | solution.py:346
  50.8 4.3 %collective-permute-start.13 = (bf16[2,128,128]{2,1,0:T(8,128)(2,1)S(1)}, bf16[2,128,128]{2,1,0:T(8,128)(2,1)S(1)}, u32[]{:S(2)}, u32[]{:S(2)}) collective-permute-start(bf16[2,128,128]{2,1,0:T(8,128)(2,1)S(1)} %get-tuple-element.38), channel_id=1, source_target_pairs={{0,2},{1,3},{2,0},{3,1},{4,6},{5,7},{6,4},{7,5},{8,10},{9,11},{10,... | collective-permute-start | bytes 196616 | tf_op jit(solution)/shard_map/ppermute | solution.py:356
  52.2 4.8 %collective-permute-start.14 = (bf16[2,128,128]{2,1,0:T(8,128)(2,1)S(1)}, bf16[2,128,128]{2,1,0:T(8,128)(2,1)S(1)}, u32[]{:S(2)}, u32[]{:S(2)}) collective-permute-start(bf16[2,128,128]{2,1,0:T(8,128)(2,1)S(1)} %get-tuple-element.39), channel_id=1, source_target_pairs={{0,4},{1,5},{2,6},{3,7},{4,0},{5,1},{6,2},{7,3},{8,12},{9,13},{10,... | collective-permute-start | bytes 196616 | tf_op jit(solution)/shard_map/ppermute | solution.py:356
  53.7 5.2 %collective-permute-start.15 = (bf16[2,128,128]{2,1,0:T(8,128)(2,1)S(1)}, bf16[2,128,128]{2,1,0:T(8,128)(2,1)S(1)}, u32[]{:S(2)}, u32[]{:S(2)}) collective-permute-start(bf16[2,128,128]{2,1,0:T(8,128)(2,1)S(1)} %get-tuple-element.40), channel_id=1, source_target_pairs={{0,6},{1,7},{2,4},{3,5},{4,2},{5,3},{6,0},{7,1},{8,14},{9,15},{10,... | collective-permute-start | bytes 196616 | tf_op jit(solution)/shard_map/ppermute | solution.py:356

commit v5 on v4

--- a/solution.py
+++ b/solution.py
@@ -14,6 +14,7 @@
 RADIUS = 7
 MAX_WIDTH = (4, 4, 2, 2, 1, 1, 1, 1)
 MASKED = -1e30
+PARTS = 3
 EXPONENT = math.log2(math.e) / math.sqrt(HEAD)
 
 VMEM = pl.BlockSpec(memory_space=pltpu.VMEM)
@@ -103,10 +104,11 @@
 
 
 def attend_kernel(cfg, width_ref, offset_ref, *refs):
-    group, heads, shifts, units, begins, ends = cfg
+    group, heads, shifts, units, members, begins, ends = cfg
     q_refs, refs = refs[:group], refs[group:]
-    chunks = [refs[group * i : group * (i + 1)] for i in range(len(shifts))]
-    refs = refs[group * len(shifts) :]
+    held = len(members)
+    chunks = [dict(zip(members, refs[held * i : held * (i + 1)])) for i in range(len(shifts))]
+    refs = refs[held * len(shifts) :]
     if not begins:
         refs = refs[2:]
     if ends:
@@ -154,7 +156,8 @@
         most = min(MAX_WIDTH[min(far, RADIUS)], blocks)
         for member in range(group):
             qf = frame_of(unit, place, group, member)
-            order = [member] + [i for i in range(group) if i != member]
+            order = [i for i in (member, *range(group)) if i in members]
+            order = list(dict.fromkeys(order))
             batches = [[i] for i in order] if most == blocks else [order]
             for index, batch in enumerate(batches):
                 for head in range(heads):
@@ -207,7 +210,7 @@
 
 
 def attend(cfg, bands, queries, chunks, state):
-    group, heads, _, _, begins, ends = cfg
+    group, heads, _, _, _, begins, ends = cfg
     tokens = queries[0].shape[0]
     rows = group * tokens
     m_shape = pltpu.VMEM((heads, rows, BLK), jnp.float32)
@@ -254,17 +257,30 @@
 
 
 def project_kernel(group, ranks, *refs):
-    rows, weights, out_ref = refs[: group * ranks // 2], refs[group * ranks // 2 : -1], refs[-1]
+    rows, weights = refs[: group * ranks // 2], refs[group * ranks // 2 : -3]
+    out_ref, kept, sem = refs[-3:]
     place = lax.rem(lax.axis_index("frame"), group)
-    total = None
-    for offset, weight in enumerate(weights):
+    lefts = []
+    for offset in range(ranks):
         parts = [rows[i * ranks // 2 + offset // 2][offset % 2] for i in range(group)]
         left = jnp.concatenate(parts, axis=1)
         if group == 2:
             left = jnp.where(place == 0, left, jnp.concatenate(parts[::-1], axis=1))
-        term = jnp.dot(left, weight[...], preferred_element_type=jnp.float32)
-        total = term if total is None else total + term
-    out_ref[...] = total.astype(out_ref.dtype)
+        lefts.append(left)
+    copies = []
+    for part in range(PARTS):
+        width = kept.shape[1] // PARTS
+        columns = slice(part * width, (part + 1) * width)
+        total = None
+        for left, weight in zip(lefts, weights):
+            term = jnp.dot(left, weight[:, columns], preferred_element_type=jnp.float32)
+            total = term if total is None else total + term
+        kept[:, columns] = total.astype(kept.dtype)
+        copy = pltpu.make_async_copy(kept.at[:, columns], out_ref.at[:, columns], sem.at[part])
+        copy.start()
+        copies.append(copy)
+    for copy in copies:
+        copy.wait()
 
 
 def project(rows, weights, group):
@@ -274,7 +290,11 @@
         functools.partial(project_kernel, group, ranks),
         out_shape=jax.ShapeDtypeStruct((tokens, columns), rows[0].dtype),
         in_specs=[VMEM] * (len(rows) + ranks),
-        out_specs=VMEM,
+        out_specs=HBM,
+        scratch_shapes=[
+            pltpu.VMEM((tokens, columns), rows[0].dtype),
+            pltpu.SemaphoreType.DMA((PARTS,)),
+        ],
         compiler_params=params(),
         cost_estimate=pl.CostEstimate(
             flops=4 * rows[0].size * len(rows) * columns, bytes_accessed=1 << 20, transcendentals=0
@@ -336,12 +356,17 @@
         ]
         arrived.append(held)
 
-    cfg = (group, heads, ((0, 0),), units, True, False)
+    everyone = tuple(range(group))
+    cfg = (group, heads, ((0, 0),), units, everyone, True, False)
     state = attend(cfg, bands, query_rows, [chunks], [])
     for k, received in enumerate(arrived, 1):
         shifts = tuple((k, parity) for parity in range(2) if edges(units, k, parity))
-        cfg = (group, heads, shifts, units, False, k == furthest)
-        state = attend(cfg, bands, query_rows, received, state)
+        last = k == furthest
+        for members in [(i,) for i in everyone] if last else [everyone]:
+            ends = last and members[-1] == group - 1
+            cfg = (group, heads, shifts, units, members, False, ends)
+            some = [[chunk[i] for i in members] for chunk in received]
+            state = attend(cfg, bands, query_rows, some, state)
     keep, give = state[:2]
     got = lax.ppermute(give, "head", [(h, h ^ 1) for h in range(ranks)])
     packed = pack(keep, got)

time: 60.5 us -> 61.8 us (1.021)
  Pallas kernels: 7.56 us -> 10.9 us
  waiting for transfers between devices: 30.6 us -> 28.6 us
    pallas_call x4 -> x5, Pallas kernels: 4.92 us -> 8.35 us  [attend(): pl.pallas_call(functools.partial(attend_kernel, cfg), out_shape=outs, in_...]
    ppermute x10, waiting for transfers between devices: 17.7 us -> 15.7 us  [along(): return lax.ppermute(value, 'frame', pairs)]
  transfers between devices with their start and end apart: 19 -> 19, of which waited for: 12 -> 12; matrix products, arithmetic and copies ran while one was open for 0% -> 0% of each run, Pallas kernels for 10% -> 16%
where the time goes in v5:
time: 61.8 us; the launch traced here: 61.6 us
  waiting for transfers between devices  28.6 us (46%)
  starting transfers between devices  21.9 us (35%)
  Pallas kernels  10.9 us (18%)
    ppermute x10, waiting for transfers between devices, along(): return lax.ppermute(value, 'frame', pairs)  15.7 us
    ppermute x10, starting transfers between devices, along(): return lax.ppermute(value, 'frame', pairs)  13.1 us
    pallas_call x5, Pallas kernels, attend(): pl.pallas_call(functools.partial(attend_kernel, cfg), out_shape=outs, in_...  8.35 us
    ppermute x1, waiting for transfers between devices, on_device(): chunks.append(lax.ppermute(pieces[2], 'frame', swap))  4.89 us
    ppermute x3, waiting for transfers between devices, on_device(): rows.append(lax.ppermute(packed[r], ('frame', 'head'), pairs))  4.54 us
    ppermute x3, starting transfers between devices, on_device(): rows.append(lax.ppermute(packed[r], ('frame', 'head'), pairs))  3.55 us
    ppermute x3, starting transfers between devices, on_device(): weights[offset ^ bit] = lax.ppermute(weights[offset], 'head', pairs)  3.07 us
    ppermute x1, starting transfers between devices, on_device(): chunks.append(lax.ppermute(pieces[2], 'frame', swap))  1.56 us
  transfers between devices with their start and end apart: 19, of which 12 were waited for; matrix products, arithmetic and copies ran while one was open for 0% of the time, Pallas kernels for 16%

profile of v5, /device:TPU:0, one launch (start us, length us, event | category | flops | bytes accessed | tf_op | source)
XLA Modules:
  0.0 61.6 jit_solution(11775192466639874819)
XLA Ops:
  0.0 0.0 copy-start
  0.0 3.0 %collective-permute-start.17 = (bf16[256,1536]{1,0:T(8,128)(2,1)}, bf16[256,1536]{1,0:T(8,128)(2,1)S(1)}, u32[]{:S(2)}, u32[]{:S(2)}) collective-permute-start(bf16[256,1536]{1,0:T(8,128)(2,1)} %refs_4_.1), channel_id=1, source_target_pairs={{0,2},{1,3},{2,0},{3,1},{4,6},{5,7},{6,4},{7,5},{8,10},{9,11},{10,... | collective-permute-start | bytes 2359304 | tf_op jit(solution)/shard_map/ppermute | solution.py:346
  3.0 1.3 %split.1 = (bf16[512,256]{1,0:T(8,128)(2,1)S(1)}, bf16[512,128]{1,0:T(8,128)(2,1)S(1)}, bf16[512,256]{1,0:T(8,128)(2,1)S(1)}, bf16[512,128]{1,0:T(8,128)(2,1)S(1...) custom-call(bf16[512,256]{1,0:T(8,128)(2,1)} %q_ref.1, bf16[512,256]{1,0:T(8,128)(2,1)} %k_ref.1, bf16[512,256]{1,0:T(8,128)(2,1)} %v_ref.1, ...), custom_call_target="tpu_custom_call" | custom-call | tf_op jit(solution)/shard_map/split/pallas_call | solution.py:67
  4.3 1.6 %collective-permute-start.1 = (bf16[512,256]{1,0:T(8,128)(2,1)S(1)}, bf16[512,256]{1,0:T(8,128)(2,1)S(1)}, u32[]{:S(2)}, u32[]{:S(2)}) collective-permute-start(bf16[512,256]{1,0:T(8,128)(2,1)S(1)} %get-tuple-element.29), channel_id=1, source_target_pairs={{0,4},{4,0},{8,12},{12,8},{16,20},{20,16},{24,28},{28,24},{1,5},{5... | collective-permute-start | bytes 786440 | tf_op jit(solution)/shard_map/ppermute | solution.py:338
  5.8 0.5 collective-permute-start
  6.4 1.6 %collective-permute-start.5 = (bf16[512,256]{1,0:T(8,128)(2,1)S(1)}, bf16[512,256]{1,0:T(8,128)(2,1)S(1)}, u32[]{:S(2)}, u32[]{:S(2)}) collective-permute-start(bf16[512,256]{1,0:T(8,128)(2,1)S(1)} %get-tuple-element.30.refs_2_), channel_id=1, source_target_pairs={{0,8},{4,12},{8,0},{12,4},{16,24},{20,28},{24,16},{28,20},{1,9},{5... | collective-permute-start | bytes 786440 | tf_op jit(solution)/shard_map/ppermute | solution.py:330
  8.0 0.7 %collective-permute-start.8 = (bf16[512,256]{1,0:T(8,128)(2,1)S(1)}, bf16[512,256]{1,0:T(8,128)(2,1)S(1)}, u32[]{:S(2)}, u32[]{:S(2)}) collective-permute-start(bf16[512,256]{1,0:T(8,128)(2,1)S(1)} %get-tuple-element.30.refs_2_), channel_id=1, source_target_pairs={{8,16},{12,20},{16,8},{20,12},{9,17},{13,21},{17,9},{21,13},{10,18... | collective-permute-start | bytes 786440 | tf_op jit(solution)/shard_map/ppermute | solution.py:330
  8.6 4.9 %collective-permute-done.1.refs_3_ = bf16[512,256]{1,0:T(8,128)(2,1)S(1)} collective-permute-done((bf16[512,256]{1,0:T(8,128)(2,1)S(1)}, bf16[512,256]{1,0:T(8,128)(2,1)S(1)}, u32[]{:S(2)}, u32[]{:S(2)}) %collective-permute-start.1) | collective-permute-done | bytes 262176 | tf_op jit(solution)/shard_map/ppermute | solution.py:338
  13.5 0.7 %collective-permute-start.10 = (bf16[512,256]{1,0:T(8,128)(2,1)S(1)}, bf16[512,256]{1,0:T(8,128)(2,1)S(1)}, u32[]{:S(2)}, u32[]{:S(2)}) collective-permute-start(bf16[512,256]{1,0:T(8,128)(2,1)S(1)} %collective-permute-done.1.refs_3_), channel_id=1, source_target_pairs={{8,16},{12,20},{16,8},{20,12},{9,17},{13,21},{17,9},{21,13},{10,18... | collective-permute-start | bytes 786440 | tf_op jit(solution)/shard_map/ppermute | solution.py:330
  14.2 0.7 %collective-permute-done.refs_1_ = bf16[512,128]{1,0:T(8,128)(2,1)S(1)} collective-permute-done((bf16[512,128]{1,0:T(8,128)(2,1)S(1)}, bf16[512,128]{1,0:T(8,128)(2,1)S(1)}, u32[]{:S(2)}, u32[]{:S(2)}) %collective-permute-start) | collective-permute-done | bytes 131104 | tf_op jit(solution)/shard_map/ppermute | solution.py:339
  14.9 3.7 %collective-permute-start.2 = (bf16[512,256]{1,0:T(8,128)(2,1)S(1)}, bf16[512,256]{1,0:T(8,128)(2,1)S(1)}, u32[]{:S(2)}, u32[]{:S(2)}) collective-permute-start(bf16[512,256]{1,0:T(8,128)(2,1)S(1)} %collective-permute-done.1.refs_3_), channel_id=1, source_target_pairs={{0,8},{4,12},{8,0},{12,4},{16,24},{20,28},{24,16},{28,20},{1,9},{5... | collective-permute-start | bytes 786440 | tf_op jit(solution)/shard_map/ppermute | solution.py:330
  18.7 0.0 collective-permute-done.5.refs_2_
  18.7 0.7 %collective-permute-start.6 = (bf16[512,256]{1,0:T(8,128)(2,1)S(1)}, bf16[512,256]{1,0:T(8,128)(2,1)S(1)}, u32[]{:S(2)}, u32[]{:S(2)}) collective-permute-start(bf16[512,256]{1,0:T(8,128)(2,1)S(1)} %collective-permute-done.5.refs_2_), channel_id=1, source_target_pairs={{8,16},{12,20},{16,8},{20,12},{9,17},{13,21},{17,9},{21,13},{10,18... | collective-permute-start | bytes 786440 | tf_op jit(solution)/shard_map/ppermute | solution.py:330
  19.3 0.0 collective-permute-done.8.refs_4_
  19.4 0.0 copy-done
  19.4 0.1 collective-permute-start.16
  19.4 1.4 %collective-permute-done.17.refs_6_ = bf16[256,1536]{1,0:T(8,128)(2,1)S(1)} collective-permute-done((bf16[256,1536]{1,0:T(8,128)(2,1)}, bf16[256,1536]{1,0:T(8,128)(2,1)S(1)}, u32[]{:S(2)}, u32[]{:S(2)}) %collective-permute-start.17) | collective-permute-done | bytes 786464 | tf_op jit(solution)/shard_map/ppermute | solution.py:346
  20.8 0.0 collective-permute-start.18
  20.8 0.0 collective-permute-done.10.refs_5_
  20.8 1.3 %collective-permute-start.9 = (bf16[512,256]{1,0:T(8,128)(2,1)S(1)}, bf16[512,256]{1,0:T(8,128)(2,1)S(1)}, u32[]{:S(2)}, u32[]{:S(2)}) collective-permute-start(bf16[512,256]{1,0:T(8,128)(2,1)S(1)} %collective-permute-done.8.refs_4_), channel_id=1, source_target_pairs={{8,0},{12,4},{16,24},{20,28},{9,1},{13,5},{17,25},{21,29},{10,2},{... | collective-permute-start | bytes 786440 | tf_op jit(solution)/shard_map/ppermute | solution.py:330
  22.1 0.9 %collective-permute-done.2.refs_3_ = bf16[512,256]{1,0:T(8,128)(2,1)S(1)} collective-permute-done((bf16[512,256]{1,0:T(8,128)(2,1)S(1)}, bf16[512,256]{1,0:T(8,128)(2,1)S(1)}, u32[]{:S(2)}, u32[]{:S(2)}) %collective-permute-start.2) | collective-permute-done | bytes 262176 | tf_op jit(solution)/shard_map/ppermute | solution.py:330
  23.0 0.7 %collective-permute-start.3 = (bf16[512,256]{1,0:T(8,128)(2,1)S(1)}, bf16[512,256]{1,0:T(8,128)(2,1)S(1)}, u32[]{:S(2)}, u32[]{:S(2)}) collective-permute-start(bf16[512,256]{1,0:T(8,128)(2,1)S(1)} %collective-permute-done.2.refs_3_), channel_id=1, source_target_pairs={{8,16},{12,20},{16,8},{20,12},{9,17},{13,21},{17,9},{21,13},{10,18... | collective-permute-start | bytes 786440 | tf_op jit(solution)/shard_map/ppermute | solution.py:330
  23.7 0.0 collective-permute-done.6.refs_4_
  23.7 1.3 %collective-permute-start.11 = (bf16[512,256]{1,0:T(8,128)(2,1)S(1)}, bf16[512,256]{1,0:T(8,128)(2,1)S(1)}, u32[]{:S(2)}, u32[]{:S(2)}) collective-permute-start(bf16[512,256]{1,0:T(8,128)(2,1)S(1)} %collective-permute-done.10.refs_5_), channel_id=1, source_target_pairs={{8,0},{12,4},{16,24},{20,28},{9,1},{13,5},{17,25},{21,29},{10,2},{... | collective-permute-start | bytes 786440 | tf_op jit(solution)/shard_map/ppermute | solution.py:330
  25.0 6.9 %collective-permute-done.9.refs_2_ = bf16[512,256]{1,0:T(8,128)(2,1)S(1)} collective-permute-done((bf16[512,256]{1,0:T(8,128)(2,1)S(1)}, bf16[512,256]{1,0:T(8,128)(2,1)S(1)}, u32[]{:S(2)}, u32[]{:S(2)}) %collective-permute-start.9) | collective-permute-done | bytes 262176 | tf_op jit(solution)/shard_map/ppermute | solution.py:330
  31.9 1.3 %collective-permute-start.7 = (bf16[512,256]{1,0:T(8,128)(2,1)S(1)}, bf16[512,256]{1,0:T(8,128)(2,1)S(1)}, u32[]{:S(2)}, u32[]{:S(2)}) collective-permute-start(bf16[512,256]{1,0:T(8,128)(2,1)S(1)} %collective-permute-done.6.refs_4_), channel_id=1, source_target_pairs={{8,0},{12,4},{16,24},{20,28},{9,1},{13,5},{17,25},{21,29},{10,2},{... | collective-permute-start | bytes 786440 | tf_op jit(solution)/shard_map/ppermute | solution.py:330
  33.2 0.0 collective-permute-done.3.refs_5_
  33.2 1.3 %collective-permute-start.4 = (bf16[512,256]{1,0:T(8,128)(2,1)S(1)}, bf16[512,256]{1,0:T(8,128)(2,1)S(1)}, u32[]{:S(2)}, u32[]{:S(2)}) collective-permute-start(bf16[512,256]{1,0:T(8,128)(2,1)S(1)} %collective-permute-done.3.refs_5_), channel_id=1, source_target_pairs={{8,0},{12,4},{16,24},{20,28},{9,1},{13,5},{17,25},{21,29},{10,2},{... | collective-permute-start | bytes 786440 | tf_op jit(solution)/shard_map/ppermute | solution.py:330
  34.5 1.5 %shard_map.64 = (f32[1,1024,128]{2,1,0:T(8,128)S(1)}, f32[1,1024,256]{2,1,0:T(8,128)S(1)}) custom-call(s32[8,8]{1,0:T(8,128)S(4)} %get-tuple-element.25.width_ref, s32[8,4,8]{2,1,0:T(4,128)S(4)} %get-tuple-element.26.offset_ref, bf16[512,128]{1,0:T(8,128)(2,1)S(1)} %get-tuple-element.27.refs_0_, bf16[512,128]{1,0:T(8,128)(2,1)S(1)} %collective-permute-done.refs_1_, ...), custom_call_target="tpu_custom_call" | custom-call | flops 536870912 | bytes 1048576 | tf_op jit(solution)/shard_map/pallas_call | solution.py:230
  36.1 1.7 %shard_map.65 = (f32[1,1024,128]{2,1,0:T(8,128)S(1)}, f32[1,1024,256]{2,1,0:T(8,128)S(1)}) custom-call(s32[8,8]{1,0:T(8,128)S(4)} %get-tuple-element.25.width_ref, s32[8,4,8]{2,1,0:T(4,128)S(4)} %get-tuple-element.26.offset_ref, bf16[512,128]{1,0:T(8,128)(2,1)S(1)} %get-tuple-element.27.refs_0_, ...), custom_call_target="tpu_custom_call", output_to_operand_aliasing={{0}: (8, {}), {1}: (9, {})} | custom-call | flops 1073741824 | bytes 1048576 | tf_op jit(solution)/shard_map/pallas_call | solution.py:230
  37.8 1.7 %collective-permute-done.11.refs_3_ = bf16[512,256]{1,0:T(8,128)(2,1)S(1)} collective-permute-done((bf16[512,256]{1,0:T(8,128)(2,1)S(1)}, bf16[512,256]{1,0:T(8,128)(2,1)S(1)}, u32[]{:S(2)}, u32[]{:S(2)}) %collective-permute-start.11) | collective-permute-done | bytes 262176 | tf_op jit(solution)/shard_map/ppermute | solution.py:330
  39.4 1.0 %shard_map.66 = (f32[1,1024,128]{2,1,0:T(8,128)S(1)}, f32[1,1024,256]{2,1,0:T(8,128)S(1)}) custom-call(s32[8,8]{1,0:T(8,128)S(4)} %get-tuple-element.25.width_ref, s32[8,4,8]{2,1,0:T(4,128)S(4)} %get-tuple-element.26.offset_ref, bf16[512,128]{1,0:T(8,128)(2,1)S(1)} %get-tuple-element.27.refs_0_, ...), custom_call_target="tpu_custom_call", output_to_operand_aliasing={{0}: (8, {}), {1}: (9, {})} | custom-call | flops 1073741824 | bytes 1048576 | tf_op jit(solution)/shard_map/pallas_call | solution.py:230
  40.4 4.6 %collective-permute-done.7.refs_2_ = bf16[512,256]{1,0:T(8,128)(2,1)S(1)} collective-permute-done((bf16[512,256]{1,0:T(8,128)(2,1)S(1)}, bf16[512,256]{1,0:T(8,128)(2,1)S(1)}, u32[]{:S(2)}, u32[]{:S(2)}) %collective-permute-start.7) | collective-permute-done | bytes 262176 | tf_op jit(solution)/shard_map/ppermute | solution.py:330
  45.0 2.0 %shard_map.67 = (f32[1,1024,128]{2,1,0:T(8,128)S(1)}, f32[1,1024,256]{2,1,0:T(8,128)S(1)}) custom-call(s32[8,8]{1,0:T(8,128)S(4)} %get-tuple-element.25.width_ref, s32[8,4,8]{2,1,0:T(4,128)S(4)} %get-tuple-element.26.offset_ref, bf16[512,128]{1,0:T(8,128)(2,1)S(1)} %get-tuple-element.27.refs_0_, ...), custom_call_target="tpu_custom_call", output_to_operand_aliasing={{0}: (5, {}), {1}: (6, {})} | custom-call | flops 268435456 | bytes 1048576 | tf_op jit(solution)/shard_map/pallas_call | solution.py:230
  47.1 1.6 %collective-permute-done.4.refs_2_ = bf16[512,256]{1,0:T(8,128)(2,1)S(1)} collective-permute-done((bf16[512,256]{1,0:T(8,128)(2,1)S(1)}, bf16[512,256]{1,0:T(8,128)(2,1)S(1)}, u32[]{:S(2)}, u32[]{:S(2)}) %collective-permute-start.4) | collective-permute-done | bytes 262176 | tf_op jit(solution)/shard_map/ppermute | solution.py:330
  48.6 2.1 %shard_map.68 = (bf16[4,128,128]{2,1,0:T(8,128)(2,1)S(1)}, bf16[4,128,128]{2,1,0:T(8,128)(2,1)S(1)}, f32[1,1024,128]{2,1,0:T(8,128)S(1)}, f32[1,1024,256]{2,1,0:T(8,128)S(1)}) custom-call(s32[8,8]{1,0:T(8,128)S(4)} %get-tuple-element.25.width_ref, s32[8,4,8]{2,1,0:T(4,128)S(4)} %get-tuple-element.26.offset_ref, ...), custom_call_target="tpu_custom_call", output_to_operand_aliasing={{2}: (5, {}), {3}: (6, {})} | custom-call | flops 268435456 | bytes 1048576 | tf_op jit(solution)/shard_map/pallas_call | solution.py:230
  50.8 0.1 collective-permute-start.12
  50.8 1.3 %collective-permute-done.12.got_ref = bf16[4,128,128]{2,1,0:T(8,128)(2,1)S(1)} collective-permute-done((bf16[4,128,128]{2,1,0:T(8,128)(2,1)S(1)}, bf16[4,128,128]{2,1,0:T(8,128)(2,1)S(1)}, u32[]{:S(2)}, u32[]{:S(2)}) %collective-permute-start.12) | collective-permute-done | bytes 131104 | tf_op jit(solution)/shard_map/ppermute | solution.py:371
  52.2 1.4 %collective-permute-start.13 = (bf16[2,128,128]{2,1,0:T(8,128)(2,1)S(1)}, bf16[2,128,128]{2,1,0:T(8,128)(2,1)S(1)}, u32[]{:S(2)}, u32[]{:S(2)}) collective-permute-start(bf16[2,128,128]{2,1,0:T(8,128)(2,1)S(1)} %get-tuple-element.42), channel_id=1, source_target_pairs={{0,2},{1,3},{2,0},{3,1},{4,6},{5,7},{6,4},{7,5},{8,10},{9,11},{10,... | collective-permute-start | bytes 196616 | tf_op jit(solution)/shard_map/ppermute | solution.py:381
  53.6 1.5 %collective-permute-start.14 = (bf16[2,128,128]{2,1,0:T(8,128)(2,1)S(1)}, bf16[2,128,128]{2,1,0:T(8,128)(2,1)S(1)}, u32[]{:S(2)}, u32[]{:S(2)}) collective-permute-start(bf16[2,128,128]{2,1,0:T(8,128)(2,1)S(1)} %get-tuple-element.43), channel_id=1, source_target_pairs={{0,4},{1,5},{2,6},{3,7},{4,0},{5,1},{6,2},{7,3},{8,12},{9,13},{10,... | collective-permute-start | bytes 196616 | tf_op jit(solution)/shard_map/ppermute | solution.py:381
  55.1 0.6 %collective-permute-start.15 = (bf16[2,128,128]{2,1,0:T(8,128)(2,1)S(1)}, bf16[2,128,128]{2,1,0:T(8,128)(2,1)S(1)}, u32[]{:S(2)}, u32[]{:S(2)}) collective-permute-start(bf16[2,128,128]{2,1,0:T(8,128)(2,1)S(1)} %get-tuple-element.44), channel_id=1, source_target_pairs={{0,6},{1,7},{2,4},{3,5},{4,2},{5,3},{6,0},{7,1},{8,14},{9,15},{10,... | collective-permute-start | bytes 196616 | tf_op jit(solution)/shard_map/ppermute | solution.py:381
  55.7 0.0 collective-permute-done.16.refs_5_
  55.7 0.8 %collective-permute-done.13.refs_1_ = bf16[2,128,128]{2,1,0:T(8,128)(2,1)S(1)} collective-permute-done((bf16[2,128,128]{2,1,0:T(8,128)(2,1)S(1)}, bf16[2,128,128]{2,1,0:T(8,128)(2,1)S(1)}, u32[]{:S(2)}, u32[]{:S(2)}) %collective-permute-start.13) | collective-permute-done | bytes 65568 | tf_op jit(solution)/shard_map/ppermute | solution.py:381
  56.5 1.9 %collective-permute-done.14.refs_2_ = bf16[2,128,128]{2,1,0:T(8,128)(2,1)S(1)} collective-permute-done((bf16[2,128,128]{2,1,0:T(8,128)(2,1)S(1)}, bf16[2,128,128]{2,1,0:T(8,128)(2,1)S(1)}, u32[]{:S(2)}, u32[]{:S(2)}) %collective-permute-start.14) | collective-permute-done | bytes 65568 | tf_op jit(solution)/shard_map/ppermute | solution.py:381
  58.4 1.9 %collective-permute-done.15.refs_3_ = bf16[2,128,128]{2,1,0:T(8,128)(2,1)S(1)} collective-permute-done((bf16[2,128,128]{2,1,0:T(8,128)(2,1)S(1)}, bf16[2,128,128]{2,1,0:T(8,128)(2,1)S(1)}, u32[]{:S(2)}, u32[]{:S(2)}) %collective-permute-start.15) | collective-permute-done | bytes 65568 | tf_op jit(solution)/shard_map/ppermute | solution.py:381
  60.3 0.0 collective-permute-done.18.refs_7_
  60.3 1.3 %project.1 = bf16[128,1536]{1,0:T(8,128)(2,1)} custom-call(bf16[2,128,128]{2,1,0:T(8,128)(2,1)S(1)} %get-tuple-element.41.refs_0_, bf16[2,128,128]{2,1,0:T(8,128)(2,1)S(1)} %collective-permute-done.13.refs_1_, bf16[2,128,128]{2,1,0:T(8,128)(2,1)S(1)} %collective-permute-done.14.refs_2_, bf16[2,128,128]{2,1,0:T(8,128)(2,1)S(1)} %collective-permute-done.15.refs_3_, ...), custom_call_target="tpu_custom_call" | custom-call | flops 805306368 | bytes 1048576 | tf_op jit(solution)/shard_map/project/pallas_call | solution.py:289
  (1 shorter events, 0.0 us)
Async XLA Ops:
  0.0 19.4 %copy-start = (bf16[256,1536]{1,0:T(8,128)(2,1)S(1)}, bf16[256,1536]{1,0:T(8,128)(2,1)}, u32[]{:S(2)}) copy-start(bf16[256,1536]{1,0:T(8,128)(2,1)} %refs_4_.1) | copy-start | bytes 2359300
  0.0 20.8 %collective-permute-start.17 = (bf16[256,1536]{1,0:T(8,128)(2,1)}, bf16[256,1536]{1,0:T(8,128)(2,1)S(1)}, u32[]{:S(2)}, u32[]{:S(2)}) collective-permute-start(bf16[256,1536]{1,0:T(8,128)(2,1)} %refs_4_.1), channel_id=1, source_target_pairs={{0,2},{1,3},{2,0},{3,1},{4,6},{5,7},{6,4},{7,5},{8,10},{9,11},{10,... | collective-permute-start | bytes 2359304 | tf_op jit(solution)/shard_map/ppermute | solution.py:346
  4.3 9.2 %collective-permute-start.1 = (bf16[512,256]{1,0:T(8,128)(2,1)S(1)}, bf16[512,256]{1,0:T(8,128)(2,1)S(1)}, u32[]{:S(2)}, u32[]{:S(2)}) collective-permute-start(bf16[512,256]{1,0:T(8,128)(2,1)S(1)} %get-tuple-element.29), channel_id=1, source_target_pairs={{0,4},{4,0},{8,12},{12,8},{16,20},{20,16},{24,28},{28,24},{1,5},{5... | collective-permute-start | bytes 786440 | tf_op jit(solution)/shard_map/ppermute | solution.py:338
  5.8 9.1 %collective-permute-start = (bf16[512,128]{1,0:T(8,128)(2,1)S(1)}, bf16[512,128]{1,0:T(8,128)(2,1)S(1)}, u32[]{:S(2)}, u32[]{:S(2)}) collective-permute-start(bf16[512,128]{1,0:T(8,128)(2,1)S(1)} %get-tuple-element.28), channel_id=1, source_target_pairs={{0,4},{4,0},{8,12},{12,8},{16,20},{20,16},{24,28},{28,24},{1,5},{5... | collective-permute-start | bytes 393224 | tf_op jit(solution)/shard_map/ppermute | solution.py:339
  6.4 12.3 %collective-permute-start.5 = (bf16[512,256]{1,0:T(8,128)(2,1)S(1)}, bf16[512,256]{1,0:T(8,128)(2,1)S(1)}, u32[]{:S(2)}, u32[]{:S(2)}) collective-permute-start(bf16[512,256]{1,0:T(8,128)(2,1)S(1)} %get-tuple-element.30.refs_2_), channel_id=1, source_target_pairs={{0,8},{4,12},{8,0},{12,4},{16,24},{20,28},{24,16},{28,20},{1,9},{5... | collective-permute-start | bytes 786440 | tf_op jit(solution)/shard_map/ppermute | solution.py:330
  8.0 11.4 %collective-permute-start.8 = (bf16[512,256]{1,0:T(8,128)(2,1)S(1)}, bf16[512,256]{1,0:T(8,128)(2,1)S(1)}, u32[]{:S(2)}, u32[]{:S(2)}) collective-permute-start(bf16[512,256]{1,0:T(8,128)(2,1)S(1)} %get-tuple-element.30.refs_2_), channel_id=1, source_target_pairs={{8,16},{12,20},{16,8},{20,12},{9,17},{13,21},{17,9},{21,13},{10,18... | collective-permute-start | bytes 786440 | tf_op jit(solution)/shard_map/ppermute | solution.py:330
  13.5 7.3 %collective-permute-start.10 = (bf16[512,256]{1,0:T(8,128)(2,1)S(1)}, bf16[512,256]{1,0:T(8,128)(2,1)S(1)}, u32[]{:S(2)}, u32[]{:S(2)}) collective-permute-start(bf16[512,256]{1,0:T(8,128)(2,1)S(1)} %collective-permute-done.1.refs_3_), channel_id=1, source_target_pairs={{8,16},{12,20},{16,8},{20,12},{9,17},{13,21},{17,9},{21,13},{10,18... | collective-permute-start | bytes 786440 | tf_op jit(solution)/shard_map/ppermute | solution.py:330
  14.9 8.1 %collective-permute-start.2 = (bf16[512,256]{1,0:T(8,128)(2,1)S(1)}, bf16[512,256]{1,0:T(8,128)(2,1)S(1)}, u32[]{:S(2)}, u32[]{:S(2)}) collective-permute-start(bf16[512,256]{1,0:T(8,128)(2,1)S(1)} %collective-permute-done.1.refs_3_), channel_id=1, source_target_pairs={{0,8},{4,12},{8,0},{12,4},{16,24},{20,28},{24,16},{28,20},{1,9},{5... | collective-permute-start | bytes 786440 | tf_op jit(solution)/shard_map/ppermute | solution.py:330
  18.7 5.0 %collective-permute-start.6 = (bf16[512,256]{1,0:T(8,128)(2,1)S(1)}, bf16[512,256]{1,0:T(8,128)(2,1)S(1)}, u32[]{:S(2)}, u32[]{:S(2)}) collective-permute-start(bf16[512,256]{1,0:T(8,128)(2,1)S(1)} %collective-permute-done.5.refs_2_), channel_id=1, source_target_pairs={{8,16},{12,20},{16,8},{20,12},{9,17},{13,21},{17,9},{21,13},{10,18... | collective-permute-start | bytes 786440 | tf_op jit(solution)/shard_map/ppermute | solution.py:330
  19.4 36.4 %collective-permute-start.16 = (bf16[256,1536]{1,0:T(8,128)(2,1)S(1)}, bf16[256,1536]{1,0:T(8,128)(2,1)S(1)}, u32[]{:S(2)}, u32[]{:S(2)}) collective-permute-start(bf16[256,1536]{1,0:T(8,128)(2,1)S(1)} %copy-done), channel_id=1, source_target_pairs={{0,1},{1,0},{2,3},{3,2},{4,5},{5,4},{6,7},{7,6},{8,9},{9,8},{10,11... | collective-permute-start | bytes 2359304 | tf_op jit(solution)/shard_map/ppermute | solution.py:346
  20.8 39.5 %collective-permute-start.18 = (bf16[256,1536]{1,0:T(8,128)(2,1)S(1)}, bf16[256,1536]{1,0:T(8,128)(2,1)S(1)}, u32[]{:S(2)}, u32[]{:S(2)}) collective-permute-start(bf16[256,1536]{1,0:T(8,128)(2,1)S(1)} %collective-permute-done.17.refs_6_), channel_id=1, source_target_pairs={{0,1},{1,0},{2,3},{3,2},{4,5},{5,4},{6,7},{7,6},{8,9},{9,8},{10,11... | collective-permute-start | bytes 2359304 | tf_op jit(solution)/shard_map/ppermute | solution.py:346
  20.8 11.1 %collective-permute-start.9 = (bf16[512,256]{1,0:T(8,128)(2,1)S(1)}, bf16[512,256]{1,0:T(8,128)(2,1)S(1)}, u32[]{:S(2)}, u32[]{:S(2)}) collective-permute-start(bf16[512,256]{1,0:T(8,128)(2,1)S(1)} %collective-permute-done.8.refs_4_), channel_id=1, source_target_pairs={{8,0},{12,4},{16,24},{20,28},{9,1},{13,5},{17,25},{21,29},{10,2},{... | collective-permute-start | bytes 786440 | tf_op jit(solution)/shard_map/ppermute | solution.py:330
  23.0 10.2 %collective-permute-start.3 = (bf16[512,256]{1,0:T(8,128)(2,1)S(1)}, bf16[512,256]{1,0:T(8,128)(2,1)S(1)}, u32[]{:S(2)}, u32[]{:S(2)}) collective-permute-start(bf16[512,256]{1,0:T(8,128)(2,1)S(1)} %collective-permute-done.2.refs_3_), channel_id=1, source_target_pairs={{8,16},{12,20},{16,8},{20,12},{9,17},{13,21},{17,9},{21,13},{10,18... | collective-permute-start | bytes 786440 | tf_op jit(solution)/shard_map/ppermute | solution.py:330
  23.7 15.7 %collective-permute-start.11 = (bf16[512,256]{1,0:T(8,128)(2,1)S(1)}, bf16[512,256]{1,0:T(8,128)(2,1)S(1)}, u32[]{:S(2)}, u32[]{:S(2)}) collective-permute-start(bf16[512,256]{1,0:T(8,128)(2,1)S(1)} %collective-permute-done.10.refs_5_), channel_id=1, source_target_pairs={{8,0},{12,4},{16,24},{20,28},{9,1},{13,5},{17,25},{21,29},{10,2},{... | collective-permute-start | bytes 786440 | tf_op jit(solution)/shard_map/ppermute | solution.py:330
  31.9 13.1 %collective-permute-start.7 = (bf16[512,256]{1,0:T(8,128)(2,1)S(1)}, bf16[512,256]{1,0:T(8,128)(2,1)S(1)}, u32[]{:S(2)}, u32[]{:S(2)}) collective-permute-start(bf16[512,256]{1,0:T(8,128)(2,1)S(1)} %collective-permute-done.6.refs_4_), channel_id=1, source_target_pairs={{8,0},{12,4},{16,24},{20,28},{9,1},{13,5},{17,25},{21,29},{10,2},{... | collective-permute-start | bytes 786440 | tf_op jit(solution)/shard_map/ppermute | solution.py:330
  33.2 15.4 %collective-permute-start.4 = (bf16[512,256]{1,0:T(8,128)(2,1)S(1)}, bf16[512,256]{1,0:T(8,128)(2,1)S(1)}, u32[]{:S(2)}, u32[]{:S(2)}) collective-permute-start(bf16[512,256]{1,0:T(8,128)(2,1)S(1)} %collective-permute-done.3.refs_5_), channel_id=1, source_target_pairs={{8,0},{12,4},{16,24},{20,28},{9,1},{13,5},{17,25},{21,29},{10,2},{... | collective-permute-start | bytes 786440 | tf_op jit(solution)/shard_map/ppermute | solution.py:330
  50.8 1.4 %collective-permute-start.12 = (bf16[4,128,128]{2,1,0:T(8,128)(2,1)S(1)}, bf16[4,128,128]{2,1,0:T(8,128)(2,1)S(1)}, u32[]{:S(2)}, u32[]{:S(2)}) collective-permute-start(bf16[4,128,128]{2,1,0:T(8,128)(2,1)S(1)} %get-tuple-element.40), channel_id=1, source_target_pairs={{0,1},{1,0},{2,3},{3,2},{4,5},{5,4},{6,7},{7,6},{8,9},{9,8},{10,11... | collective-permute-start | bytes 393224 | tf_op jit(solution)/shard_map/ppermute | solution.py:371
  52.2 4.3 %collective-permute-start.13 = (bf16[2,128,128]{2,1,0:T(8,128)(2,1)S(1)}, bf16[2,128,128]{2,1,0:T(8,128)(2,1)S(1)}, u32[]{:S(2)}, u32[]{:S(2)}) collective-permute-start(bf16[2,128,128]{2,1,0:T(8,128)(2,1)S(1)} %get-tuple-element.42), channel_id=1, source_target_pairs={{0,2},{1,3},{2,0},{3,1},{4,6},{5,7},{6,4},{7,5},{8,10},{9,11},{10,... | collective-permute-start | bytes 196616 | tf_op jit(solution)/shard_map/ppermute | solution.py:381
  53.6 4.8 %collective-permute-start.14 = (bf16[2,128,128]{2,1,0:T(8,128)(2,1)S(1)}, bf16[2,128,128]{2,1,0:T(8,128)(2,1)S(1)}, u32[]{:S(2)}, u32[]{:S(2)}) collective-permute-start(bf16[2,128,128]{2,1,0:T(8,128)(2,1)S(1)} %get-tuple-element.43), channel_id=1, source_target_pairs={{0,4},{1,5},{2,6},{3,7},{4,0},{5,1},{6,2},{7,3},{8,12},{9,13},{10,... | collective-permute-start | bytes 196616 | tf_op jit(solution)/shard_map/ppermute | solution.py:381
  55.1 5.2 %collective-permute-start.15 = (bf16[2,128,128]{2,1,0:T(8,128)(2,1)S(1)}, bf16[2,128,128]{2,1,0:T(8,128)(2,1)S(1)}, u32[]{:S(2)}, u32[]{:S(2)}) collective-permute-start(bf16[2,128,128]{2,1,0:T(8,128)(2,1)S(1)} %get-tuple-element.44), channel_id=1, source_target_pairs={{0,6},{1,7},{2,4},{3,5},{4,2},{5,3},{6,0},{7,1},{8,14},{9,15},{10,... | collective-permute-start | bytes 196616 | tf_op jit(solution)/shard_map/ppermute | solution.py:381

commit v6 on v4

--- a/solution.py
+++ b/solution.py
@@ -110,7 +110,7 @@
     if not begins:
         refs = refs[2:]
     if ends:
-        keep_ref, give_ref, m_ref, acc_ref = refs
+        keep_ref, first_ref, give_ref, m_ref, acc_ref = refs
     else:
         m_ref, acc_ref = refs
     tokens = q_refs[0].shape[0]
@@ -193,17 +193,21 @@
                 steps(step, other, chunk, False)
 
     if ends:
-        halves, rank_rows = keep_ref.shape[0] // group, keep_ref.shape[1]
+        sent, rank_rows = give_ref.shape[0], give_ref.shape[1]
+        halves = sent // group
         rank = lax.axis_index("head")
         for head in range(heads):
             columns = slice(head * HEAD, (head + 1) * HEAD)
-            for r in range(keep_ref.shape[0]):
-                for ref, low in ((keep_ref, 0), (give_ref, 1)):
+            for r in range(sent):
+                for low in range(2):
+                    ref, slot = (give_ref, r) if low else (keep_ref, r)
+                    if low == 0 and r == sent - 1:
+                        ref, slot = first_ref, 0
                     block = rank ^ (2 * (r % halves) + low)
                     start = (r // halves) * tokens + block * rank_rows
                     at = pl.ds(pl.multiple_of(start, rank_rows), rank_rows)
                     both = acc_ref[head, at, :]
-                    ref[r, :, columns] = (both[:, :HEAD] / both[:, HEAD:]).astype(ref.dtype)
+                    ref[slot, :, columns] = (both[:, :HEAD] / both[:, HEAD:]).astype(ref.dtype)
 
 
 def attend(cfg, bands, queries, chunks, state):
@@ -220,9 +224,12 @@
         aliases = {len(inputs) - 2: 0, len(inputs) - 1: 1}
     if ends:
         sent = group * lax.axis_size("head") // 2
-        part = pltpu.VMEM((sent, rows // (2 * sent), heads * HEAD), queries[0].dtype)
-        outs = [part, part, m_shape, acc_shape]
-        aliases = {index: out + 2 for index, out in aliases.items()}
+        parts = [
+            pltpu.VMEM((count, rows // (2 * sent), heads * HEAD), queries[0].dtype)
+            for count in (sent - 1, 1, sent)
+        ]
+        outs = [*parts, m_shape, acc_shape]
+        aliases = {index: out + 3 for index, out in aliases.items()}
     work = 4 * len(flat) * tokens * rows * heads * HEAD
     return pl.pallas_call(
         functools.partial(attend_kernel, cfg),
@@ -236,29 +243,37 @@
 
 
 def pack_kernel(keep_ref, got_ref, *outs):
-    for r, out in enumerate(outs):
+    *pairs, alone = outs
+    for r, out in enumerate(pairs):
         out[0] = keep_ref[r]
         out[1] = got_ref[r]
+    alone[0] = got_ref[len(pairs)]
 
 
 def pack(keep, got):
     count, *shape = keep.shape
     return pl.pallas_call(
         pack_kernel,
-        out_shape=[pltpu.VMEM((2, *shape), keep.dtype)] * count,
+        out_shape=[pltpu.VMEM((2, *shape), keep.dtype)] * count
+        + [pltpu.VMEM((1, *shape), keep.dtype)],
         in_specs=[VMEM] * 2,
-        out_specs=[VMEM] * count,
+        out_specs=[VMEM] * (count + 1),
         compiler_params=params(),
         name="pack",
     )(in_vmem(keep), in_vmem(got))
 
 
 def project_kernel(group, ranks, *refs):
-    rows, weights, out_ref = refs[: group * ranks // 2], refs[group * ranks // 2 : -1], refs[-1]
+    sent = group * ranks // 2
+    rows, weights, out_ref = refs[: sent + 1], refs[sent + 1 : -1], refs[-1]
     place = lax.rem(lax.axis_index("frame"), group)
     total = None
     for offset, weight in enumerate(weights):
-        parts = [rows[i * ranks // 2 + offset // 2][offset % 2] for i in range(group)]
+        parts = []
+        for i in range(group):
+            r = i * ranks // 2 + offset // 2
+            apart = r == sent - 1
+            parts.append(rows[r + offset % 2][0] if apart else rows[r][offset % 2])
         left = jnp.concatenate(parts, axis=1)
         if group == 2:
             left = jnp.where(place == 0, left, jnp.concatenate(parts[::-1], axis=1))
@@ -277,7 +292,7 @@
         out_specs=VMEM,
         compiler_params=params(),
         cost_estimate=pl.CostEstimate(
-            flops=4 * rows[0].size * len(rows) * columns, bytes_accessed=1 << 20, transcendentals=0
+            flops=4 * rows[0].size * (len(rows) - 1) * columns, bytes_accessed=1 << 20, transcendentals=0
         ),
         name="project",
     )(*[in_vmem(r) for r in rows], *[in_vmem(w) for w in weights])
@@ -342,18 +357,23 @@
         shifts = tuple((k, parity) for parity in range(2) if edges(units, k, parity))
         cfg = (group, heads, shifts, units, False, k == furthest)
         state = attend(cfg, bands, query_rows, received, state)
-    keep, give = state[:2]
-    got = lax.ppermute(give, "head", [(h, h ^ 1) for h in range(ranks)])
-    packed = pack(keep, got)
-    rows = [packed[0]]
-    for r in range(1, len(packed)):
+
+    def across(value, r):
         over, high = r // (ranks // 2), 2 * (r % (ranks // 2))
         pairs = [
             (f * ranks + h, (f ^ over) * ranks + (h ^ high))
             for f in range(frames)
             for h in range(ranks)
         ]
-        rows.append(lax.ppermute(packed[r], ("frame", "head"), pairs))
+        return lax.ppermute(value, ("frame", "head"), pairs)
+
+    keep, first, give = state[:3]
+    got = lax.ppermute(give, "head", [(h, h ^ 1) for h in range(ranks)])
+    count = keep.shape[0]
+    first = across(first, count)
+    packed = pack(keep, got)
+    rows = [packed[0], *[across(packed[r], r) for r in range(1, count)]]
+    rows += [first, across(packed[count], count)]
     return project(rows, weights, group)
 
 

time: 60.5 us -> 60.8 us (level)
  starting transfers between devices: 21.9 us -> 24.2 us
  waiting for transfers between devices: 30.6 us -> 28.6 us
    ppermute x3 -> x4, starting transfers between devices: 3.55 us -> 5.86 us  [across(): return lax.ppermute(value, ('frame', 'head'), pairs)]
    ppermute x3 -> x4, waiting for transfers between devices: 4.54 us -> 2.52 us  [across(): return lax.ppermute(value, ('frame', 'head'), pairs)]
  transfers between devices with their start and end apart: 19 -> 20, of which waited for: 12 -> 11; matrix products, arithmetic and copies ran while one was open for 0% -> 0% of each run, Pallas kernels for 10% -> 10%
where the time goes in v6:
time: 60.8 us; the launch traced here: 60.5 us
  waiting for transfers between devices  28.6 us (47%)
  starting transfers between devices  24.2 us (40%)
  Pallas kernels  7.54 us (12%)
    ppermute x10, waiting for transfers between devices, along(): return lax.ppermute(value, 'frame', pairs)  17.7 us
    ppermute x10, starting transfers between devices, along(): return lax.ppermute(value, 'frame', pairs)  13.1 us
    ppermute x4, starting transfers between devices, across(): return lax.ppermute(value, ('frame', 'head'), pairs)  5.86 us
    pallas_call x4, Pallas kernels, attend(): pl.pallas_call(functools.partial(attend_kernel, cfg), out_shape=outs, in_...  4.92 us
    ppermute x1, waiting for transfers between devices, on_device(): chunks.append(lax.ppermute(pieces[2], 'frame', swap))  4.89 us
    ppermute x3, starting transfers between devices, on_device(): weights[offset ^ bit] = lax.ppermute(weights[offset], 'head', pairs)  3.07 us
    ppermute x4, waiting for transfers between devices, across(): return lax.ppermute(value, ('frame', 'head'), pairs)  2.52 us
    ppermute x1, starting transfers between devices, on_device(): chunks.append(lax.ppermute(pieces[2], 'frame', swap))  1.56 us
  transfers between devices with their start and end apart: 20, of which 11 were waited for; matrix products, arithmetic and copies ran while one was open for 0% of the time, Pallas kernels for 10%

profile of v6, /device:TPU:0, one launch (start us, length us, event | category | flops | bytes accessed | tf_op | source)
XLA Modules:
  0.0 60.5 jit_solution(2458031156593761978)
XLA Ops:
  0.0 0.0 copy-start
  0.0 3.0 %collective-permute-start.18 = (bf16[256,1536]{1,0:T(8,128)(2,1)}, bf16[256,1536]{1,0:T(8,128)(2,1)S(1)}, u32[]{:S(2)}, u32[]{:S(2)}) collective-permute-start(bf16[256,1536]{1,0:T(8,128)(2,1)} %refs_5_.1), channel_id=1, source_target_pairs={{0,2},{1,3},{2,0},{3,1},{4,6},{5,7},{6,4},{7,5},{8,10},{9,11},{10,... | collective-permute-start | bytes 2359304 | tf_op jit(solution)/shard_map/ppermute | solution.py:341
  3.0 1.3 %split.1 = (bf16[512,256]{1,0:T(8,128)(2,1)S(1)}, bf16[512,128]{1,0:T(8,128)(2,1)S(1)}, bf16[512,256]{1,0:T(8,128)(2,1)S(1)}, bf16[512,128]{1,0:T(8,128)(2,1)S(1...) custom-call(bf16[512,256]{1,0:T(8,128)(2,1)} %q_ref.1, bf16[512,256]{1,0:T(8,128)(2,1)} %k_ref.1, bf16[512,256]{1,0:T(8,128)(2,1)} %v_ref.1, ...), custom_call_target="tpu_custom_call" | custom-call | tf_op jit(solution)/shard_map/split/pallas_call | solution.py:66
  4.3 1.6 %collective-permute-start.4 = (bf16[512,256]{1,0:T(8,128)(2,1)S(1)}, bf16[512,256]{1,0:T(8,128)(2,1)S(1)}, u32[]{:S(2)}, u32[]{:S(2)}) collective-permute-start(bf16[512,256]{1,0:T(8,128)(2,1)S(1)} %get-tuple-element.29), channel_id=1, source_target_pairs={{0,4},{4,0},{8,12},{12,8},{16,20},{20,16},{24,28},{28,24},{1,5},{5... | collective-permute-start | bytes 786440 | tf_op jit(solution)/shard_map/ppermute | solution.py:333
  5.8 0.5 collective-permute-start
  6.4 1.6 %collective-permute-start.1 = (bf16[512,256]{1,0:T(8,128)(2,1)S(1)}, bf16[512,256]{1,0:T(8,128)(2,1)S(1)}, u32[]{:S(2)}, u32[]{:S(2)}) collective-permute-start(bf16[512,256]{1,0:T(8,128)(2,1)S(1)} %get-tuple-element.28.refs_2_), channel_id=1, source_target_pairs={{0,8},{4,12},{8,0},{12,4},{16,24},{20,28},{24,16},{28,20},{1,9},{5... | collective-permute-start | bytes 786440 | tf_op jit(solution)/shard_map/ppermute | solution.py:325
  8.0 0.7 %collective-permute-start.8 = (bf16[512,256]{1,0:T(8,128)(2,1)S(1)}, bf16[512,256]{1,0:T(8,128)(2,1)S(1)}, u32[]{:S(2)}, u32[]{:S(2)}) collective-permute-start(bf16[512,256]{1,0:T(8,128)(2,1)S(1)} %get-tuple-element.28.refs_2_), channel_id=1, source_target_pairs={{8,16},{12,20},{16,8},{20,12},{9,17},{13,21},{17,9},{21,13},{10,18... | collective-permute-start | bytes 786440 | tf_op jit(solution)/shard_map/ppermute | solution.py:325
  8.6 4.9 %collective-permute-done.4.refs_3_ = bf16[512,256]{1,0:T(8,128)(2,1)S(1)} collective-permute-done((bf16[512,256]{1,0:T(8,128)(2,1)S(1)}, bf16[512,256]{1,0:T(8,128)(2,1)S(1)}, u32[]{:S(2)}, u32[]{:S(2)}) %collective-permute-start.4) | collective-permute-done | bytes 262176 | tf_op jit(solution)/shard_map/ppermute | solution.py:333
  13.5 0.7 %collective-permute-start.10 = (bf16[512,256]{1,0:T(8,128)(2,1)S(1)}, bf16[512,256]{1,0:T(8,128)(2,1)S(1)}, u32[]{:S(2)}, u32[]{:S(2)}) collective-permute-start(bf16[512,256]{1,0:T(8,128)(2,1)S(1)} %collective-permute-done.4.refs_3_), channel_id=1, source_target_pairs={{8,16},{12,20},{16,8},{20,12},{9,17},{13,21},{17,9},{21,13},{10,18... | collective-permute-start | bytes 786440 | tf_op jit(solution)/shard_map/ppermute | solution.py:325
  14.2 0.7 %collective-permute-done.refs_1_ = bf16[512,128]{1,0:T(8,128)(2,1)S(1)} collective-permute-done((bf16[512,128]{1,0:T(8,128)(2,1)S(1)}, bf16[512,128]{1,0:T(8,128)(2,1)S(1)}, u32[]{:S(2)}, u32[]{:S(2)}) %collective-permute-start) | collective-permute-done | bytes 131104 | tf_op jit(solution)/shard_map/ppermute | solution.py:334
  14.9 3.7 %collective-permute-start.5 = (bf16[512,256]{1,0:T(8,128)(2,1)S(1)}, bf16[512,256]{1,0:T(8,128)(2,1)S(1)}, u32[]{:S(2)}, u32[]{:S(2)}) collective-permute-start(bf16[512,256]{1,0:T(8,128)(2,1)S(1)} %collective-permute-done.4.refs_3_), channel_id=1, source_target_pairs={{0,8},{4,12},{8,0},{12,4},{16,24},{20,28},{24,16},{28,20},{1,9},{5... | collective-permute-start | bytes 786440 | tf_op jit(solution)/shard_map/ppermute | solution.py:325
  18.7 0.0 collective-permute-done.1.refs_2_
  18.7 0.7 %collective-permute-start.2 = (bf16[512,256]{1,0:T(8,128)(2,1)S(1)}, bf16[512,256]{1,0:T(8,128)(2,1)S(1)}, u32[]{:S(2)}, u32[]{:S(2)}) collective-permute-start(bf16[512,256]{1,0:T(8,128)(2,1)S(1)} %collective-permute-done.1.refs_2_), channel_id=1, source_target_pairs={{8,16},{12,20},{16,8},{20,12},{9,17},{13,21},{17,9},{21,13},{10,18... | collective-permute-start | bytes 786440 | tf_op jit(solution)/shard_map/ppermute | solution.py:325
  19.3 0.0 collective-permute-done.8.refs_4_
  19.4 0.0 copy-done
  19.4 0.1 collective-permute-start.17
  19.4 1.4 %collective-permute-done.18.refs_7_ = bf16[256,1536]{1,0:T(8,128)(2,1)S(1)} collective-permute-done((bf16[256,1536]{1,0:T(8,128)(2,1)}, bf16[256,1536]{1,0:T(8,128)(2,1)S(1)}, u32[]{:S(2)}, u32[]{:S(2)}) %collective-permute-start.18) | collective-permute-done | bytes 786464 | tf_op jit(solution)/shard_map/ppermute | solution.py:341
  20.8 0.0 collective-permute-start.19
  20.8 0.0 collective-permute-done.10.refs_5_
  20.8 1.3 %collective-permute-start.9 = (bf16[512,256]{1,0:T(8,128)(2,1)S(1)}, bf16[512,256]{1,0:T(8,128)(2,1)S(1)}, u32[]{:S(2)}, u32[]{:S(2)}) collective-permute-start(bf16[512,256]{1,0:T(8,128)(2,1)S(1)} %collective-permute-done.8.refs_4_), channel_id=1, source_target_pairs={{8,0},{12,4},{16,24},{20,28},{9,1},{13,5},{17,25},{21,29},{10,2},{... | collective-permute-start | bytes 786440 | tf_op jit(solution)/shard_map/ppermute | solution.py:325
  22.1 0.9 %collective-permute-done.5.refs_3_ = bf16[512,256]{1,0:T(8,128)(2,1)S(1)} collective-permute-done((bf16[512,256]{1,0:T(8,128)(2,1)S(1)}, bf16[512,256]{1,0:T(8,128)(2,1)S(1)}, u32[]{:S(2)}, u32[]{:S(2)}) %collective-permute-start.5) | collective-permute-done | bytes 262176 | tf_op jit(solution)/shard_map/ppermute | solution.py:325
  23.0 0.7 %collective-permute-start.6 = (bf16[512,256]{1,0:T(8,128)(2,1)S(1)}, bf16[512,256]{1,0:T(8,128)(2,1)S(1)}, u32[]{:S(2)}, u32[]{:S(2)}) collective-permute-start(bf16[512,256]{1,0:T(8,128)(2,1)S(1)} %collective-permute-done.5.refs_3_), channel_id=1, source_target_pairs={{8,16},{12,20},{16,8},{20,12},{9,17},{13,21},{17,9},{21,13},{10,18... | collective-permute-start | bytes 786440 | tf_op jit(solution)/shard_map/ppermute | solution.py:325
  23.7 0.0 collective-permute-done.2.refs_4_
  23.7 1.3 %collective-permute-start.11 = (bf16[512,256]{1,0:T(8,128)(2,1)S(1)}, bf16[512,256]{1,0:T(8,128)(2,1)S(1)}, u32[]{:S(2)}, u32[]{:S(2)}) collective-permute-start(bf16[512,256]{1,0:T(8,128)(2,1)S(1)} %collective-permute-done.10.refs_5_), channel_id=1, source_target_pairs={{8,0},{12,4},{16,24},{20,28},{9,1},{13,5},{17,25},{21,29},{10,2},{... | collective-permute-start | bytes 786440 | tf_op jit(solution)/shard_map/ppermute | solution.py:325
  25.0 6.9 %collective-permute-done.9.refs_2_ = bf16[512,256]{1,0:T(8,128)(2,1)S(1)} collective-permute-done((bf16[512,256]{1,0:T(8,128)(2,1)S(1)}, bf16[512,256]{1,0:T(8,128)(2,1)S(1)}, u32[]{:S(2)}, u32[]{:S(2)}) %collective-permute-start.9) | collective-permute-done | bytes 262176 | tf_op jit(solution)/shard_map/ppermute | solution.py:325
  31.9 1.3 %collective-permute-start.3 = (bf16[512,256]{1,0:T(8,128)(2,1)S(1)}, bf16[512,256]{1,0:T(8,128)(2,1)S(1)}, u32[]{:S(2)}, u32[]{:S(2)}) collective-permute-start(bf16[512,256]{1,0:T(8,128)(2,1)S(1)} %collective-permute-done.2.refs_4_), channel_id=1, source_target_pairs={{8,0},{12,4},{16,24},{20,28},{9,1},{13,5},{17,25},{21,29},{10,2},{... | collective-permute-start | bytes 786440 | tf_op jit(solution)/shard_map/ppermute | solution.py:325
  33.2 0.0 collective-permute-done.6.refs_5_
  33.2 1.3 %collective-permute-start.7 = (bf16[512,256]{1,0:T(8,128)(2,1)S(1)}, bf16[512,256]{1,0:T(8,128)(2,1)S(1)}, u32[]{:S(2)}, u32[]{:S(2)}) collective-permute-start(bf16[512,256]{1,0:T(8,128)(2,1)S(1)} %collective-permute-done.6.refs_5_), channel_id=1, source_target_pairs={{8,0},{12,4},{16,24},{20,28},{9,1},{13,5},{17,25},{21,29},{10,2},{... | collective-permute-start | bytes 786440 | tf_op jit(solution)/shard_map/ppermute | solution.py:325
  34.5 1.5 %shard_map.64 = (f32[1,1024,128]{2,1,0:T(8,128)S(1)}, f32[1,1024,256]{2,1,0:T(8,128)S(1)}) custom-call(s32[8,8]{1,0:T(8,128)S(4)} %get-tuple-element.24.width_ref, s32[8,4,8]{2,1,0:T(4,128)S(4)} %get-tuple-element.25.offset_ref, bf16[512,128]{1,0:T(8,128)(2,1)S(1)} %get-tuple-element.26.refs_0_, bf16[512,128]{1,0:T(8,128)(2,1)S(1)} %collective-permute-done.refs_1_, ...), custom_call_target="tpu_custom_call" | custom-call | flops 536870912 | bytes 1048576 | tf_op jit(solution)/shard_map/pallas_call | solution.py:234
  36.1 1.7 %shard_map.65 = (f32[1,1024,128]{2,1,0:T(8,128)S(1)}, f32[1,1024,256]{2,1,0:T(8,128)S(1)}) custom-call(s32[8,8]{1,0:T(8,128)S(4)} %get-tuple-element.24.width_ref, s32[8,4,8]{2,1,0:T(4,128)S(4)} %get-tuple-element.25.offset_ref, bf16[512,128]{1,0:T(8,128)(2,1)S(1)} %get-tuple-element.26.refs_0_, ...), custom_call_target="tpu_custom_call", output_to_operand_aliasing={{0}: (8, {}), {1}: (9, {})} | custom-call | flops 1073741824 | bytes 1048576 | tf_op jit(solution)/shard_map/pallas_call | solution.py:234
  37.8 1.7 %collective-permute-done.11.refs_3_ = bf16[512,256]{1,0:T(8,128)(2,1)S(1)} collective-permute-done((bf16[512,256]{1,0:T(8,128)(2,1)S(1)}, bf16[512,256]{1,0:T(8,128)(2,1)S(1)}, u32[]{:S(2)}, u32[]{:S(2)}) %collective-permute-start.11) | collective-permute-done | bytes 262176 | tf_op jit(solution)/shard_map/ppermute | solution.py:325
  39.4 1.0 %shard_map.66 = (f32[1,1024,128]{2,1,0:T(8,128)S(1)}, f32[1,1024,256]{2,1,0:T(8,128)S(1)}) custom-call(s32[8,8]{1,0:T(8,128)S(4)} %get-tuple-element.24.width_ref, s32[8,4,8]{2,1,0:T(4,128)S(4)} %get-tuple-element.25.offset_ref, bf16[512,128]{1,0:T(8,128)(2,1)S(1)} %get-tuple-element.26.refs_0_, ...), custom_call_target="tpu_custom_call", output_to_operand_aliasing={{0}: (8, {}), {1}: (9, {})} | custom-call | flops 1073741824 | bytes 1048576 | tf_op jit(solution)/shard_map/pallas_call | solution.py:234
  40.4 4.6 %collective-permute-done.3.refs_2_ = bf16[512,256]{1,0:T(8,128)(2,1)S(1)} collective-permute-done((bf16[512,256]{1,0:T(8,128)(2,1)S(1)}, bf16[512,256]{1,0:T(8,128)(2,1)S(1)}, u32[]{:S(2)}, u32[]{:S(2)}) %collective-permute-start.3) | collective-permute-done | bytes 262176 | tf_op jit(solution)/shard_map/ppermute | solution.py:325
  45.0 3.6 %collective-permute-done.7.refs_3_ = bf16[512,256]{1,0:T(8,128)(2,1)S(1)} collective-permute-done((bf16[512,256]{1,0:T(8,128)(2,1)S(1)}, bf16[512,256]{1,0:T(8,128)(2,1)S(1)}, u32[]{:S(2)}, u32[]{:S(2)}) %collective-permute-start.7) | collective-permute-done | bytes 262176 | tf_op jit(solution)/shard_map/ppermute | solution.py:325
  48.6 0.7 %shard_map.67 = (bf16[3,128,128]{2,1,0:T(8,128)(2,1)S(1)}, bf16[1,128,128]{2,1,0:T(8,128)(2,1)S(1)}, bf16[4,128,128]{2,1,0:T(8,128)(2,1)S(1)}, f32[1,1024,128]{2,1,0:T(8,128)S(1)}, f32[1,1024,256]{2,1,0:T(8,128)S(1)}) custom-call(s32[8,8]{1,0:T(8,128)S(4)} %get-tuple-element.24.width_ref, ...), custom_call_target="tpu_custom_call", output_to_operand_aliasing={{3}: (6, {}), {4}: (7, {})} | custom-call | flops 536870912 | bytes 1048576 | tf_op jit(solution)/shard_map/pallas_call | solution.py:234
  49.4 0.1 collective-permute-start.12
  49.4 1.3 %collective-permute-done.12.got_ref = bf16[4,128,128]{2,1,0:T(8,128)(2,1)S(1)} collective-permute-done((bf16[4,128,128]{2,1,0:T(8,128)(2,1)S(1)}, bf16[4,128,128]{2,1,0:T(8,128)(2,1)S(1)}, u32[]{:S(2)}, u32[]{:S(2)}) %collective-permute-start.12) | collective-permute-done | bytes 131104 | tf_op jit(solution)/shard_map/ppermute | solution.py:371
  50.8 1.4 %collective-permute-start.13 = (bf16[2,128,128]{2,1,0:T(8,128)(2,1)S(1)}, bf16[2,128,128]{2,1,0:T(8,128)(2,1)S(1)}, u32[]{:S(2)}, u32[]{:S(2)}) collective-permute-start(bf16[2,128,128]{2,1,0:T(8,128)(2,1)S(1)} %get-tuple-element.39), channel_id=1, source_target_pairs={{0,2},{1,3},{2,0},{3,1},{4,6},{5,7},{6,4},{7,5},{8,10},{9,11},{10,... | collective-permute-start | bytes 196616 | tf_op jit(solution)/shard_map/ppermute | solution.py:368
  52.2 1.5 %collective-permute-start.14 = (bf16[2,128,128]{2,1,0:T(8,128)(2,1)S(1)}, bf16[2,128,128]{2,1,0:T(8,128)(2,1)S(1)}, u32[]{:S(2)}, u32[]{:S(2)}) collective-permute-start(bf16[2,128,128]{2,1,0:T(8,128)(2,1)S(1)} %get-tuple-element.40), channel_id=1, source_target_pairs={{0,4},{1,5},{2,6},{3,7},{4,0},{5,1},{6,2},{7,3},{8,12},{9,13},{10,... | collective-permute-start | bytes 196616 | tf_op jit(solution)/shard_map/ppermute | solution.py:368
  53.7 0.6 %collective-permute-start.15 = (bf16[1,128,128]{2,1,0:T(8,128)(2,1)S(1)}, bf16[1,128,128]{2,1,0:T(8,128)(2,1)S(1)}, u32[]{:S(2)}, u32[]{:S(2)}) collective-permute-start(bf16[1,128,128]{2,1,0:T(8,128)(2,1)S(1)} %get-tuple-element.41), channel_id=1, source_target_pairs={{0,6},{1,7},{2,4},{3,5},{4,2},{5,3},{6,0},{7,1},{8,14},{9,15},{10,... | collective-permute-start | bytes 98312 | tf_op jit(solution)/shard_map/ppermute | solution.py:368
  54.3 0.0 collective-permute-done.17.refs_6_
  54.3 2.3 %collective-permute-start.16 = (bf16[1,128,128]{2,1,0:T(8,128)(2,1)S(1)}, bf16[1,128,128]{2,1,0:T(8,128)(2,1)S(1)}, u32[]{:S(2)}, u32[]{:S(2)}) collective-permute-start(bf16[1,128,128]{2,1,0:T(8,128)(2,1)S(1)} %get-tuple-element.42), channel_id=1, source_target_pairs={{0,6},{1,7},{2,4},{3,5},{4,2},{5,3},{6,0},{7,1},{8,14},{9,15},{10,... | collective-permute-start | bytes 98312 | tf_op jit(solution)/shard_map/ppermute | solution.py:368
  56.7 1.9 %collective-permute-done.15.refs_3_ = bf16[1,128,128]{2,1,0:T(8,128)(2,1)S(1)} collective-permute-done((bf16[1,128,128]{2,1,0:T(8,128)(2,1)S(1)}, bf16[1,128,128]{2,1,0:T(8,128)(2,1)S(1)}, u32[]{:S(2)}, u32[]{:S(2)}) %collective-permute-start.15) | collective-permute-done | bytes 32800 | tf_op jit(solution)/shard_map/ppermute | solution.py:368
  58.5 0.6 %collective-permute-done.16.refs_4_ = bf16[1,128,128]{2,1,0:T(8,128)(2,1)S(1)} collective-permute-done((bf16[1,128,128]{2,1,0:T(8,128)(2,1)S(1)}, bf16[1,128,128]{2,1,0:T(8,128)(2,1)S(1)}, u32[]{:S(2)}, u32[]{:S(2)}) %collective-permute-start.16) | collective-permute-done | bytes 32800 | tf_op jit(solution)/shard_map/ppermute | solution.py:368
  59.2 0.0 collective-permute-done.13.refs_1_
  59.2 0.0 collective-permute-done.14.refs_2_
  59.2 0.0 collective-permute-done.19.refs_8_
  59.2 1.3 %project.1 = bf16[128,1536]{1,0:T(8,128)(2,1)} custom-call(bf16[2,128,128]{2,1,0:T(8,128)(2,1)S(1)} %get-tuple-element.38.refs_0_, bf16[2,128,128]{2,1,0:T(8,128)(2,1)S(1)} %collective-permute-done.13.refs_1_, bf16[2,128,128]{2,1,0:T(8,128)(2,1)S(1)} %collective-permute-done.14.refs_2_, bf16[1,128,128]{2,1,0:T(8,128)(2,1)S(1)} %collective-permute-done.15.refs_3_, ...), custom_call_target="tpu_custom_call" | custom-call | flops 805306368 | bytes 1048576 | tf_op jit(solution)/shard_map/project/pallas_call | solution.py:288
  (1 shorter events, 0.0 us)
Async XLA Ops:
  0.0 19.4 %copy-start = (bf16[256,1536]{1,0:T(8,128)(2,1)S(1)}, bf16[256,1536]{1,0:T(8,128)(2,1)}, u32[]{:S(2)}) copy-start(bf16[256,1536]{1,0:T(8,128)(2,1)} %refs_5_.1) | copy-start | bytes 2359300
  0.0 20.8 %collective-permute-start.18 = (bf16[256,1536]{1,0:T(8,128)(2,1)}, bf16[256,1536]{1,0:T(8,128)(2,1)S(1)}, u32[]{:S(2)}, u32[]{:S(2)}) collective-permute-start(bf16[256,1536]{1,0:T(8,128)(2,1)} %refs_5_.1), channel_id=1, source_target_pairs={{0,2},{1,3},{2,0},{3,1},{4,6},{5,7},{6,4},{7,5},{8,10},{9,11},{10,... | collective-permute-start | bytes 2359304 | tf_op jit(solution)/shard_map/ppermute | solution.py:341
  4.3 9.2 %collective-permute-start.4 = (bf16[512,256]{1,0:T(8,128)(2,1)S(1)}, bf16[512,256]{1,0:T(8,128)(2,1)S(1)}, u32[]{:S(2)}, u32[]{:S(2)}) collective-permute-start(bf16[512,256]{1,0:T(8,128)(2,1)S(1)} %get-tuple-element.29), channel_id=1, source_target_pairs={{0,4},{4,0},{8,12},{12,8},{16,20},{20,16},{24,28},{28,24},{1,5},{5... | collective-permute-start | bytes 786440 | tf_op jit(solution)/shard_map/ppermute | solution.py:333
  5.8 9.1 %collective-permute-start = (bf16[512,128]{1,0:T(8,128)(2,1)S(1)}, bf16[512,128]{1,0:T(8,128)(2,1)S(1)}, u32[]{:S(2)}, u32[]{:S(2)}) collective-permute-start(bf16[512,128]{1,0:T(8,128)(2,1)S(1)} %get-tuple-element.27), channel_id=1, source_target_pairs={{0,4},{4,0},{8,12},{12,8},{16,20},{20,16},{24,28},{28,24},{1,5},{5... | collective-permute-start | bytes 393224 | tf_op jit(solution)/shard_map/ppermute | solution.py:334
  6.4 12.3 %collective-permute-start.1 = (bf16[512,256]{1,0:T(8,128)(2,1)S(1)}, bf16[512,256]{1,0:T(8,128)(2,1)S(1)}, u32[]{:S(2)}, u32[]{:S(2)}) collective-permute-start(bf16[512,256]{1,0:T(8,128)(2,1)S(1)} %get-tuple-element.28.refs_2_), channel_id=1, source_target_pairs={{0,8},{4,12},{8,0},{12,4},{16,24},{20,28},{24,16},{28,20},{1,9},{5... | collective-permute-start | bytes 786440 | tf_op jit(solution)/shard_map/ppermute | solution.py:325
  8.0 11.4 %collective-permute-start.8 = (bf16[512,256]{1,0:T(8,128)(2,1)S(1)}, bf16[512,256]{1,0:T(8,128)(2,1)S(1)}, u32[]{:S(2)}, u32[]{:S(2)}) collective-permute-start(bf16[512,256]{1,0:T(8,128)(2,1)S(1)} %get-tuple-element.28.refs_2_), channel_id=1, source_target_pairs={{8,16},{12,20},{16,8},{20,12},{9,17},{13,21},{17,9},{21,13},{10,18... | collective-permute-start | bytes 786440 | tf_op jit(solution)/shard_map/ppermute | solution.py:325
  13.5 7.3 %collective-permute-start.10 = (bf16[512,256]{1,0:T(8,128)(2,1)S(1)}, bf16[512,256]{1,0:T(8,128)(2,1)S(1)}, u32[]{:S(2)}, u32[]{:S(2)}) collective-permute-start(bf16[512,256]{1,0:T(8,128)(2,1)S(1)} %collective-permute-done.4.refs_3_), channel_id=1, source_target_pairs={{8,16},{12,20},{16,8},{20,12},{9,17},{13,21},{17,9},{21,13},{10,18... | collective-permute-start | bytes 786440 | tf_op jit(solution)/shard_map/ppermute | solution.py:325
  14.9 8.1 %collective-permute-start.5 = (bf16[512,256]{1,0:T(8,128)(2,1)S(1)}, bf16[512,256]{1,0:T(8,128)(2,1)S(1)}, u32[]{:S(2)}, u32[]{:S(2)}) collective-permute-start(bf16[512,256]{1,0:T(8,128)(2,1)S(1)} %collective-permute-done.4.refs_3_), channel_id=1, source_target_pairs={{0,8},{4,12},{8,0},{12,4},{16,24},{20,28},{24,16},{28,20},{1,9},{5... | collective-permute-start | bytes 786440 | tf_op jit(solution)/shard_map/ppermute | solution.py:325
  18.7 5.0 %collective-permute-start.2 = (bf16[512,256]{1,0:T(8,128)(2,1)S(1)}, bf16[512,256]{1,0:T(8,128)(2,1)S(1)}, u32[]{:S(2)}, u32[]{:S(2)}) collective-permute-start(bf16[512,256]{1,0:T(8,128)(2,1)S(1)} %collective-permute-done.1.refs_2_), channel_id=1, source_target_pairs={{8,16},{12,20},{16,8},{20,12},{9,17},{13,21},{17,9},{21,13},{10,18... | collective-permute-start | bytes 786440 | tf_op jit(solution)/shard_map/ppermute | solution.py:325
  19.4 35.0 %collective-permute-start.17 = (bf16[256,1536]{1,0:T(8,128)(2,1)S(1)}, bf16[256,1536]{1,0:T(8,128)(2,1)S(1)}, u32[]{:S(2)}, u32[]{:S(2)}) collective-permute-start(bf16[256,1536]{1,0:T(8,128)(2,1)S(1)} %copy-done), channel_id=1, source_target_pairs={{0,1},{1,0},{2,3},{3,2},{4,5},{5,4},{6,7},{7,6},{8,9},{9,8},{10,11... | collective-permute-start | bytes 2359304 | tf_op jit(solution)/shard_map/ppermute | solution.py:341
  20.8 38.4 %collective-permute-start.19 = (bf16[256,1536]{1,0:T(8,128)(2,1)S(1)}, bf16[256,1536]{1,0:T(8,128)(2,1)S(1)}, u32[]{:S(2)}, u32[]{:S(2)}) collective-permute-start(bf16[256,1536]{1,0:T(8,128)(2,1)S(1)} %collective-permute-done.18.refs_7_), channel_id=1, source_target_pairs={{0,1},{1,0},{2,3},{3,2},{4,5},{5,4},{6,7},{7,6},{8,9},{9,8},{10,11... | collective-permute-start | bytes 2359304 | tf_op jit(solution)/shard_map/ppermute | solution.py:341
  20.8 11.1 %collective-permute-start.9 = (bf16[512,256]{1,0:T(8,128)(2,1)S(1)}, bf16[512,256]{1,0:T(8,128)(2,1)S(1)}, u32[]{:S(2)}, u32[]{:S(2)}) collective-permute-start(bf16[512,256]{1,0:T(8,128)(2,1)S(1)} %collective-permute-done.8.refs_4_), channel_id=1, source_target_pairs={{8,0},{12,4},{16,24},{20,28},{9,1},{13,5},{17,25},{21,29},{10,2},{... | collective-permute-start | bytes 786440 | tf_op jit(solution)/shard_map/ppermute | solution.py:325
  23.0 10.2 %collective-permute-start.6 = (bf16[512,256]{1,0:T(8,128)(2,1)S(1)}, bf16[512,256]{1,0:T(8,128)(2,1)S(1)}, u32[]{:S(2)}, u32[]{:S(2)}) collective-permute-start(bf16[512,256]{1,0:T(8,128)(2,1)S(1)} %collective-permute-done.5.refs_3_), channel_id=1, source_target_pairs={{8,16},{12,20},{16,8},{20,12},{9,17},{13,21},{17,9},{21,13},{10,18... | collective-permute-start | bytes 786440 | tf_op jit(solution)/shard_map/ppermute | solution.py:325
  23.7 15.7 %collective-permute-start.11 = (bf16[512,256]{1,0:T(8,128)(2,1)S(1)}, bf16[512,256]{1,0:T(8,128)(2,1)S(1)}, u32[]{:S(2)}, u32[]{:S(2)}) collective-permute-start(bf16[512,256]{1,0:T(8,128)(2,1)S(1)} %collective-permute-done.10.refs_5_), channel_id=1, source_target_pairs={{8,0},{12,4},{16,24},{20,28},{9,1},{13,5},{17,25},{21,29},{10,2},{... | collective-permute-start | bytes 786440 | tf_op jit(solution)/shard_map/ppermute | solution.py:325
  31.9 13.1 %collective-permute-start.3 = (bf16[512,256]{1,0:T(8,128)(2,1)S(1)}, bf16[512,256]{1,0:T(8,128)(2,1)S(1)}, u32[]{:S(2)}, u32[]{:S(2)}) collective-permute-start(bf16[512,256]{1,0:T(8,128)(2,1)S(1)} %collective-permute-done.2.refs_4_), channel_id=1, source_target_pairs={{8,0},{12,4},{16,24},{20,28},{9,1},{13,5},{17,25},{21,29},{10,2},{... | collective-permute-start | bytes 786440 | tf_op jit(solution)/shard_map/ppermute | solution.py:325
  33.2 15.4 %collective-permute-start.7 = (bf16[512,256]{1,0:T(8,128)(2,1)S(1)}, bf16[512,256]{1,0:T(8,128)(2,1)S(1)}, u32[]{:S(2)}, u32[]{:S(2)}) collective-permute-start(bf16[512,256]{1,0:T(8,128)(2,1)S(1)} %collective-permute-done.6.refs_5_), channel_id=1, source_target_pairs={{8,0},{12,4},{16,24},{20,28},{9,1},{13,5},{17,25},{21,29},{10,2},{... | collective-permute-start | bytes 786440 | tf_op jit(solution)/shard_map/ppermute | solution.py:325
  49.4 1.4 %collective-permute-start.12 = (bf16[4,128,128]{2,1,0:T(8,128)(2,1)S(1)}, bf16[4,128,128]{2,1,0:T(8,128)(2,1)S(1)}, u32[]{:S(2)}, u32[]{:S(2)}) collective-permute-start(bf16[4,128,128]{2,1,0:T(8,128)(2,1)S(1)} %get-tuple-element.37), channel_id=1, source_target_pairs={{0,1},{1,0},{2,3},{3,2},{4,5},{5,4},{6,7},{7,6},{8,9},{9,8},{10,11... | collective-permute-start | bytes 393224 | tf_op jit(solution)/shard_map/ppermute | solution.py:371
  50.8 8.4 %collective-permute-start.13 = (bf16[2,128,128]{2,1,0:T(8,128)(2,1)S(1)}, bf16[2,128,128]{2,1,0:T(8,128)(2,1)S(1)}, u32[]{:S(2)}, u32[]{:S(2)}) collective-permute-start(bf16[2,128,128]{2,1,0:T(8,128)(2,1)S(1)} %get-tuple-element.39), channel_id=1, source_target_pairs={{0,2},{1,3},{2,0},{3,1},{4,6},{5,7},{6,4},{7,5},{8,10},{9,11},{10,... | collective-permute-start | bytes 196616 | tf_op jit(solution)/shard_map/ppermute | solution.py:368
  52.2 6.9 %collective-permute-start.14 = (bf16[2,128,128]{2,1,0:T(8,128)(2,1)S(1)}, bf16[2,128,128]{2,1,0:T(8,128)(2,1)S(1)}, u32[]{:S(2)}, u32[]{:S(2)}) collective-permute-start(bf16[2,128,128]{2,1,0:T(8,128)(2,1)S(1)} %get-tuple-element.40), channel_id=1, source_target_pairs={{0,4},{1,5},{2,6},{3,7},{4,0},{5,1},{6,2},{7,3},{8,12},{9,13},{10,... | collective-permute-start | bytes 196616 | tf_op jit(solution)/shard_map/ppermute | solution.py:368
  53.7 4.8 %collective-permute-start.15 = (bf16[1,128,128]{2,1,0:T(8,128)(2,1)S(1)}, bf16[1,128,128]{2,1,0:T(8,128)(2,1)S(1)}, u32[]{:S(2)}, u32[]{:S(2)}) collective-permute-start(bf16[1,128,128]{2,1,0:T(8,128)(2,1)S(1)} %get-tuple-element.41), channel_id=1, source_target_pairs={{0,6},{1,7},{2,4},{3,5},{4,2},{5,3},{6,0},{7,1},{8,14},{9,15},{10,... | collective-permute-start | bytes 98312 | tf_op jit(solution)/shard_map/ppermute | solution.py:368
  54.3 4.8 %collective-permute-start.16 = (bf16[1,128,128]{2,1,0:T(8,128)(2,1)S(1)}, bf16[1,128,128]{2,1,0:T(8,128)(2,1)S(1)}, u32[]{:S(2)}, u32[]{:S(2)}) collective-permute-start(bf16[1,128,128]{2,1,0:T(8,128)(2,1)S(1)} %get-tuple-element.42), channel_id=1, source_target_pairs={{0,6},{1,7},{2,4},{3,5},{4,2},{5,3},{6,0},{7,1},{8,14},{9,15},{10,... | collective-permute-start | bytes 98312 | tf_op jit(solution)/shard_map/ppermute | solution.py:368
